TPU v7x, 256 devices: a whole 4x4x8 slice. The times are simulated.
256 devices in a mesh: row: 8 (over y, core), col: 32 (over x, z).
Axes of the slice: x: 4, y: 4, z: 8, core: 2. Of those that a mesh axis runs over, the one named last changes fastest.
Arguments:
- eigvecs: float32 [1024, 100352], P('col', 'row'), may hold values from -6 to 6
- span_vectors: float32 [2, 64, 4, 128], P(None, 'row'), may hold values from -6 to 6
- span_offsets: int32 [2, 64], P(None, 'row'), may hold values from 0 to 12543, as said below
- panels: bfloat16 [2, 256, 100352], P(None, 'col', 'row'), may hold values from -0.01894036 to 0.01894036
Outputs:
- back_vectors: float32 [1024, 100352], P('col', 'row')
Inputs may be any that keep to these rules, and one draw needn't show every extreme that they name: `span_offsets`: each block starts within the rows of its index of row and ends at most 128 rows after them, and inside the matrix; on every index of row but the last the last block of each sweep reaches into the next index's rows.
All inputs are finite; a program needn't handle non-finite values.
Results may differ from a plain program's by a relative error of at most 0.0075.
Values may be sent and summed in bfloat16 or wider, within the bound.
No kernel may reach another device: no remote copies, remote signals or barrier semaphores. Data moves between devices by JAX's collectives and lax.ppermute only.
A program may use at most 128 MiB of HBM per device.

v0:
```python
import jax
import jax.numpy as jnp
from jax import lax
from jax.sharding import Mesh
from jax.sharding import PartitionSpec as P

COL = ("col_0", "col_1")


CONTRACT_LAST = (((1,), (1,)), ((), ()))
CONTRACT_FIRST = (((0,), (0,)), ((), ()))


def from_behind(value, axis, steps):
    count = lax.axis_size(axis)
    first, last = (max(0, -steps), min(count, count - steps))
    return lax.ppermute(value, axis, [(source, source + steps) for source in range(first, last)])


def in_order(pieces, dim):
    pieces = jnp.moveaxis(pieces, 0, dim)
    shape = pieces.shape
    return pieces.reshape(*shape[:dim], shape[dim] * shape[dim + 1], *shape[dim + 2 :])


def all_blocks(x, axes, sequence):
    pieces = x[None]
    for k in sequence:
        pieces = lax.all_gather(pieces, axes[k], axis=0, tiled=True)
    current = [lax.axis_size(axes[k]) for k in reversed(sequence)]
    pieces = pieces.reshape(*current, *x.shape)
    turned = sorted(range(len(sequence)), key=lambda place: sequence[len(sequence) - 1 - place])
    return pieces.transpose(*turned, *range(len(sequence), pieces.ndim)).reshape(-1, *x.shape)


def gather_axes(x, axes, sequence, dim):
    return in_order(all_blocks(x, axes, sequence), dim)


def sent_to_all(x, axis):
    peers = lax.axis_size(axis)
    return lax.all_to_all(jnp.broadcast_to(x[None], (peers, *x.shape)), axis, 0, 0, tiled=True)


def over_copies(x, axis):
    everything = sent_to_all(x, axis)
    return jnp.sum(everything.astype(jnp.float32), axis=0)


def wy_matrix(gram_mat):
    return jnp.triu(gram_mat, 1) + 0.5 * jnp.diag(jnp.diag(gram_mat))


def upper_solve(matrix, right):
    order = matrix.shape[0]
    if order <= 8:
        solved = [None] * order
        for back_at in range(order - 1, -1, -1):
            value = right[back_at]
            for later in range(back_at + 1, order):
                value = value - matrix[back_at, later] * solved[later]
            solved[back_at] = value / matrix[back_at, back_at]
        return jnp.stack(solved, axis=0)

    def step(count, solution):
        place = (order - 1 - count).astype(jnp.int32)
        matrow = lax.dynamic_index_in_dim(matrix, place, 0, keepdims=False)
        rhsrow = lax.dynamic_index_in_dim(right, place, 0, keepdims=False)
        pivot = lax.dynamic_index_in_dim(matrow, place, 0, keepdims=False)
        partial_sum = jnp.dot(matrow, solution)
        value = (rhsrow - partial_sum) / pivot
        return lax.dynamic_update_index_in_dim(solution, value, place, 0)

    return lax.fori_loop(0, order, step, jnp.zeros(right.shape, jnp.float32))


def apply_span(window, vectors):
    gram_mat = jnp.dot(vectors, vectors.T)
    inner = jnp.dot(vectors, window.T)
    coeffs = upper_solve(wy_matrix(gram_mat), inner)
    return window - jnp.dot(coeffs.T, vectors)


def run_spans(block, vectors, offsets, band_len):

    def advance(span_at, state):
        begin_at = offsets[span_at]
        window = lax.dynamic_slice_in_dim(state, begin_at, band_len, 1)
        return lax.dynamic_update_slice_in_dim(
            state, apply_span(window, vectors[span_at]), begin_at, 1
        )

    return lax.fori_loop(0, vectors.shape[0], advance, block)


def sweep_chain(eigen, vectors, offsets, band_len):
    columns, rows_dev = eigen.shape
    row_count = lax.axis_size("row")
    row_index = lax.axis_index("row")
    below = from_behind(eigen[:, :band_len], "row", -1)
    extended = jnp.concatenate([eigen, below], axis=1)

    def section(moment, state):
        finished = lax.cond(
            row_index == moment,
            lambda inside: run_spans(inside, vectors, offsets, band_len),
            lambda inside: inside,
            state,
        )
        arrived = from_behind(finished[:, rows_dev:], "row", 1)
        replaced = lax.dynamic_update_slice_in_dim(finished, arrived, 0, 1)
        return jnp.where(row_index == moment + 1, replaced, finished)

    extended = lax.fori_loop(0, row_count, section, extended)
    return extended[:, :rows_dev]


def panel_update(eigen, reflect, gram_mat, inner):
    coeffs = upper_solve(wy_matrix(gram_mat), inner)
    return eigen - lax.dot_general(
        coeffs.astype(jnp.bfloat16), reflect, CONTRACT_FIRST, preferred_element_type=jnp.float32
    )


def local_sums(reflect, eigen):
    gram_mat = lax.dot_general(reflect, reflect, CONTRACT_LAST, preferred_element_type=jnp.float32)
    inner = lax.dot_general(
        reflect, eigen.astype(jnp.bfloat16), CONTRACT_LAST, preferred_element_type=jnp.float32
    )
    return (gram_mat, inner)


def local(eigvecs, span_vectors, span_offsets, panels):
    band_len = span_vectors.shape[3]
    eigen = eigvecs
    for sweep_at in range(span_vectors.shape[0]):
        eigen = sweep_chain(eigen, span_vectors[sweep_at], span_offsets[sweep_at], band_len)
    gathered = gather_axes(panels, COL, (0, 1), 1)
    for panel_at in range(gathered.shape[0]):
        reflect = gathered[panel_at]
        gram_mat, inner = local_sums(reflect, eigen)
        gram_mat, inner = (
            over_copies(gram_mat.astype(jnp.bfloat16), "row").astype(jnp.float32),
            over_copies(inner.astype(jnp.bfloat16), "row").astype(jnp.float32),
        )
        eigen = panel_update(eigen, reflect, gram_mat, inner)
    return eigen


def solution(mesh):
    finer = Mesh(mesh.devices.reshape(mesh.shape["row"], 4, 8), ("row", "col_0", "col_1"))
    placed = (P(COL, "row"), P(None, "row", None, None), P(None, "row"), P(None, COL, "row"))
    return jax.shard_map(
        local, mesh=finer, in_specs=placed, out_specs=P(COL, "row"), check_vma=False
    )
```

profile of v0, /device:TPU:1, one launch (start us, length us, event | category | flops | bytes accessed | tf_op | source)
XLA Modules:
  0.0 2024.3 jit_solution(10539556407410454324)
XLA Ops:
  7.3 34.7 %all-gather.6.cloned.1.call-done = bf16[8,8,12544]{2,1,0:T(8,128)(2,1)} async-done(((bf16[2,8,12544]{2,1,0:T(8,128)(2,1)}), bf16[8,8,12544]{2,1,0:T(8,128)(2,1)}) %all-gather.6.cloned.1.call-update) | async-done | bytes 1605648 | tf_op jit(solution)/shard_map/all_gather | solution.py:29
  47.5 447.9 %while.90 = (s32[]{:T(128)}, f32[32,12672]{1,0:T(8,128)S(1)}, s32[]{:T(128)}, s32[8]{0:T(128)S(1)}, bf16[8,4,128]{2,1,0:T(4,128)(2,1)S(1)}, /*index=5*/s32[]{:T(128)}) while((s32[]{:T(128)}, f32[32,12672]{1,0:T(8,128)S(1)}, s32[]{:T(128)}, s32[8]{0:T(128)S(1)}, bf16[8,4,128]{2,1,0:T(4,128)(2,1)S(1)}, /*index=5*/s32[]{:T(128)}) %tuple.233), condition=%wide.region_5.6_spmd, body=%wide.region_0.5_spmd.sunk | while | flops 79610 | bytes 228376 | solution.py:114
  49.5 82.8 %collective-permute-done.1 = f32[32,128]{1,0:T(8,128)S(1)} collective-permute-done((f32[32,128]{1,0:T(8,128)S(1)}, f32[32,128]{1,0:T(8,128)S(1)}, u32[]{:S(2)}, u32[]{:S(2)}) %collective-permute-start.1) | collective-permute-done | bytes 16416 | tf_op jit(solution)/shard_map/while/body/eval_jaxpr/ppermute | solution.py:17
  132.3 84.1 %conditional.4 = (f32[32,12672]{1,0:T(8,128)S(1)}) conditional(s32[]{:T(128)} %convert_element_type.92, f32[32,12672]{1,0:T(8,128)S(1)} %get-tuple-element.1018, (s32[8]{0:T(128)S(1)}, bf16[8,4,128]{2,1,0:T(4,128)(2,1)S(1)}, f32[32,12672]{1,0:T(8,128)S(1)}) %tuple.216), branch_computations={%region_1.0_spmd, %region_2.4_spmd} | conditional | flops 75509 | bytes 80763 | solution.py:104
  132.3 84.1 %while.88 = (s32[]{:T(128)}, f32[32,12672]{1,0:T(8,128)S(1)}, s32[8]{0:T(128)S(1)}, bf16[8,4,128]{2,1,0:T(4,128)(2,1)S(1)}, s32[]{:T(128)}, /*index=5*/s32[]{:T(128)}, s32[]{:T(128)}) while((s32[]{:T(128)}, f32[32,12672]{1,0:T(8,128)S(1)}, s32[8]{0:T(128)S(1)}, bf16[8,4,128]{2,1,0:T(4,128)(2,1)S(1)}, s32[]{:T(128)}, /*index=5*/s32[]{:T(128)}, ...), condition=%wide.region_4.3_spmd, body=%wide.region_3.2_spmd.sunk | while | flops 75509 | bytes 80691 | solution.py:93
  136.2 6.0 subtract_divide_fusion.13
  146.7 6.0 subtract_divide_fusion.13
  219.5 88.0 %collective-permute-start.1 = (f32[32,128]{1,0:T(8,128)S(1)}, f32[32,128]{1,0:T(8,128)S(1)}, u32[]{:S(2)}, u32[]{:S(2)}) collective-permute-start(f32[32,128]{1,0:T(8,128)S(1)} %slice.356), channel_id=1, source_target_pairs={{0,32},{32,64},{64,96},{96,128},{128,160},{160,192},{192,224},{1,3... | collective-permute-start | bytes 49160 | tf_op jit(solution)/shard_map/while/body/eval_jaxpr/ppermute | solution.py:17
  313.5 84.0 %collective-permute-start.1 = (f32[32,128]{1,0:T(8,128)S(1)}, f32[32,128]{1,0:T(8,128)S(1)}, u32[]{:S(2)}, u32[]{:S(2)}) collective-permute-start(f32[32,128]{1,0:T(8,128)S(1)} %slice.356), channel_id=1, source_target_pairs={{0,32},{32,64},{64,96},{96,128},{128,160},{160,192},{192,224},{1,3... | collective-permute-start | bytes 49160 | tf_op jit(solution)/shard_map/while/body/eval_jaxpr/ppermute | solution.py:17
  403.4 86.0 %collective-permute-start.1 = (f32[32,128]{1,0:T(8,128)S(1)}, f32[32,128]{1,0:T(8,128)S(1)}, u32[]{:S(2)}, u32[]{:S(2)}) collective-permute-start(f32[32,128]{1,0:T(8,128)S(1)} %slice.356), channel_id=1, source_target_pairs={{0,32},{32,64},{64,96},{96,128},{128,160},{160,192},{192,224},{1,3... | collective-permute-start | bytes 49160 | tf_op jit(solution)/shard_map/while/body/eval_jaxpr/ppermute | solution.py:17
  497.4 83.4 %collective-permute-done.3 = f32[32,128]{1,0:T(8,128)S(1)} collective-permute-done((f32[32,128]{1,0:T(8,128)S(1)}, f32[32,128]{1,0:T(8,128)S(1)}, u32[]{:S(2)}, u32[]{:S(2)}) %collective-permute-start.3) | collective-permute-done | bytes 16416 | tf_op jit(solution)/shard_map/ppermute | solution.py:17
  581.0 10.7 copy.16
  591.7 388.9 %while.91 = (s32[]{:T(128)}, f32[32,12672]{1,0:T(8,128)S(1)}, s32[]{:T(128)}, s32[8]{0:T(128)S(1)}, bf16[8,4,128]{2,1,0:T(4,128)(2,1)S(1)}, /*index=5*/s32[]{:T(128)}) while((s32[]{:T(128)}, f32[32,12672]{1,0:T(8,128)S(1)}, s32[]{:T(128)}, s32[8]{0:T(128)S(1)}, bf16[8,4,128]{2,1,0:T(4,128)(2,1)S(1)}, /*index=5*/s32[]{:T(128)}) %tuple.236), condition=%wide.region_11.12_spmd, body=%wide.region_6.11_spmd.sunk | while | flops 79610 | bytes 228376 | solution.py:114
  599.9 88.4 %conditional.5 = (f32[32,12672]{1,0:T(8,128)S(1)}) conditional(s32[]{:T(128)} %convert_element_type.93, f32[32,12672]{1,0:T(8,128)S(1)} %get-tuple-element.1036, (s32[8]{0:T(128)S(1)}, bf16[8,4,128]{2,1,0:T(4,128)(2,1)S(1)}, f32[32,12672]{1,0:T(8,128)S(1)}) %tuple.218), branch_computations={%region_7.7_spmd, %region_8.10_spmd} | conditional | flops 75509 | bytes 80763 | solution.py:104
  599.9 88.4 %while.89 = (s32[]{:T(128)}, f32[32,12672]{1,0:T(8,128)S(1)}, s32[8]{0:T(128)S(1)}, bf16[8,4,128]{2,1,0:T(4,128)(2,1)S(1)}, s32[]{:T(128)}, /*index=5*/s32[]{:T(128)}, s32[]{:T(128)}) while((s32[]{:T(128)}, f32[32,12672]{1,0:T(8,128)S(1)}, s32[8]{0:T(128)S(1)}, bf16[8,4,128]{2,1,0:T(4,128)(2,1)S(1)}, s32[]{:T(128)}, /*index=5*/s32[]{:T(128)}, ...), condition=%wide.region_10.9_spmd, body=%wide.region_9.8_spmd.sunk | while | flops 75509 | bytes 80691 | solution.py:93
  604.1 6.2 subtract_divide_fusion.12
  615.0 6.2 subtract_divide_fusion.12
  626.1 6.2 subtract_divide_fusion.12
  637.2 6.2 subtract_divide_fusion.12
  648.2 6.2 subtract_divide_fusion.12
  659.3 6.2 subtract_divide_fusion.12
  670.4 6.2 subtract_divide_fusion.12
  681.4 6.2 subtract_divide_fusion.12
  691.4 92.5 %collective-permute-start = (f32[32,128]{1,0:T(8,128)S(1)}, f32[32,128]{1,0:T(8,128)S(1)}, u32[]{:S(2)}, u32[]{:S(2)}) collective-permute-start(f32[32,128]{1,0:T(8,128)S(1)} %slice.357), channel_id=1, source_target_pairs={{0,32},{32,64},{64,96},{96,128},{128,160},{160,192},{192,224},{1,3... | collective-permute-start | bytes 49160 | tf_op jit(solution)/shard_map/while/body/eval_jaxpr/ppermute | solution.py:17
  789.8 88.5 %collective-permute-start = (f32[32,128]{1,0:T(8,128)S(1)}, f32[32,128]{1,0:T(8,128)S(1)}, u32[]{:S(2)}, u32[]{:S(2)}) collective-permute-start(f32[32,128]{1,0:T(8,128)S(1)} %slice.357), channel_id=1, source_target_pairs={{0,32},{32,64},{64,96},{96,128},{128,160},{160,192},{192,224},{1,3... | collective-permute-start | bytes 49160 | tf_op jit(solution)/shard_map/while/body/eval_jaxpr/ppermute | solution.py:17
  884.2 90.5 %collective-permute-start = (f32[32,128]{1,0:T(8,128)S(1)}, f32[32,128]{1,0:T(8,128)S(1)}, u32[]{:S(2)}, u32[]{:S(2)}) collective-permute-start(f32[32,128]{1,0:T(8,128)S(1)} %slice.357), channel_id=1, source_target_pairs={{0,32},{32,64},{64,96},{96,128},{128,160},{160,192},{192,224},{1,3... | collective-permute-start | bytes 49160 | tf_op jit(solution)/shard_map/while/body/eval_jaxpr/ppermute | solution.py:17
  986.1 266.3 %all-to-all-start = ((bf16[8,256,32]{1,2,0:T(8,128)(2,1)}), bf16[8,256,32]{1,2,0:T(8,128)(2,1)S(1)}, u32[]{:S(2)}, u32[]{:S(2)}) async-start(bf16[8,256,32]{1,2,0:T(8,128)(2,1)} %broadcast_in_dim.142), calls=%async_computation | async-start | bytes 262144 | tf_op jit(solution)/shard_map/all_to_all | solution.py:42
  1252.4 6.7 fusion.59
  1264.9 6.6 fusion.58
  1271.6 8.3 all-to-all-done.1
  1288.7 343.0 %while.92 = (s32[]{:T(128)}, bf16[256,32]{1,0:T(8,128)(2,1)S(1)}, f32[256,32]{1,0:T(8,128)S(1)}, f32[256,256]{1,0:T(8,128)S(1)}, s32[]{:T(128)}, /*index=5*/s32[]{:T(128)}, s32[]{:T(128)}, s32[]{:T(128)}) while((s32[]{:T(128)}, bf16[256,32]{1,0:T(8,128)(2,1)S(1)}, f32[256,32]{1,0:T(8,128)S(1)}, f32[256,256]{1,0:T(8,128)S(1)}, s32[]{:T(128)}, ...), condition=%wide.region_15.16_spmd, body=%wide.region_14.15_spmd.sunk | while | flops 16487 | bytes 68463 | solution.py:74
  1651.5 360.7 %while.93 = (s32[]{:T(128)}, bf16[256,32]{1,0:T(8,128)(2,1)S(1)}, f32[256,32]{1,0:T(8,128)S(1)}, f32[256,256]{1,0:T(8,128)S(1)}, s32[]{:T(128)}, /*index=5*/s32[]{:T(128)}, s32[]{:T(128)}, s32[]{:T(128)}) while((s32[]{:T(128)}, bf16[256,32]{1,0:T(8,128)(2,1)S(1)}, f32[256,32]{1,0:T(8,128)S(1)}, f32[256,256]{1,0:T(8,128)S(1)}, s32[]{:T(128)}, ...), condition=%wide.region_19.20_spmd, body=%wide.region_18.19_spmd.sunk | while | flops 16487 | bytes 68463 | solution.py:74
  (1805 shorter events, 881.8 us)
Async XLA Ops:
  6.5 35.5 %copy-start = (f32[32,12544]{1,0:T(8,128)S(1)}, f32[32,12544]{1,0:T(8,128)}, u32[]{:S(2)}) copy-start(f32[32,12544]{1,0:T(8,128)} %param.20) | copy-start | bytes 4816900
  6.5 38.3 %copy-start.1 = (f32[2,8,4,128]{3,2,1,0:T(4,128)S(1)}, f32[2,8,4,128]{3,2,1,0:T(4,128)}, u32[]{:S(2)}) copy-start(f32[2,8,4,128]{3,2,1,0:T(4,128)} %param.21) | copy-start | bytes 98308
  6.5 38.3 %copy-start.2 = (s32[2,8]{1,0:T(2,128)S(1)}, s32[2,8]{1,0:T(2,128)}, u32[]{:S(2)}) copy-start(s32[2,8]{1,0:T(2,128)} %param.22) | copy-start | bytes 196
  6.5 35.5 %all-gather.6.cloned.1.call-start = ((), (), s32[]{:S(2)}) async-start(), calls=%async_computation.5 | async-start | bytes 2007040 | tf_op jit(solution)/shard_map/all_gather | solution.py:29
  7.3 573.7 %all-gather.4.cloned.1.call-start = ((), (), s32[]{:S(2)}) async-start(), calls=%async_computation.4 | async-start | bytes 14450688 | tf_op jit(solution)/shard_map/all_gather | solution.py:29
  42.1 5.3 collective-permute-start.2
  47.5 84.8 %collective-permute-start.1 = (f32[32,128]{1,0:T(8,128)S(1)}, f32[32,128]{1,0:T(8,128)S(1)}, u32[]{:S(2)}, u32[]{:S(2)}) collective-permute-start(f32[32,128]{1,0:T(8,128)S(1)} %slice.356), channel_id=1, source_target_pairs={{0,32},{32,64},{64,96},{96,128},{128,160},{160,192},{192,224},{1,3... | collective-permute-start | bytes 49160 | tf_op jit(solution)/shard_map/while/body/eval_jaxpr/ppermute | solution.py:17
  216.4 3.1 collective-permute-start.1
  219.5 88.9 %collective-permute-start.1 = (f32[32,128]{1,0:T(8,128)S(1)}, f32[32,128]{1,0:T(8,128)S(1)}, u32[]{:S(2)}, u32[]{:S(2)}) collective-permute-start(f32[32,128]{1,0:T(8,128)S(1)} %slice.356), channel_id=1, source_target_pairs={{0,32},{32,64},{64,96},{96,128},{128,160},{160,192},{192,224},{1,3... | collective-permute-start | bytes 49160 | tf_op jit(solution)/shard_map/while/body/eval_jaxpr/ppermute | solution.py:17
  308.4 5.1 collective-permute-start.1
  313.5 84.9 %collective-permute-start.1 = (f32[32,128]{1,0:T(8,128)S(1)}, f32[32,128]{1,0:T(8,128)S(1)}, u32[]{:S(2)}, u32[]{:S(2)}) collective-permute-start(f32[32,128]{1,0:T(8,128)S(1)} %slice.356), channel_id=1, source_target_pairs={{0,32},{32,64},{64,96},{96,128},{128,160},{160,192},{192,224},{1,3... | collective-permute-start | bytes 49160 | tf_op jit(solution)/shard_map/while/body/eval_jaxpr/ppermute | solution.py:17
  398.4 5.1 collective-permute-start.1
  403.4 86.9 %collective-permute-start.1 = (f32[32,128]{1,0:T(8,128)S(1)}, f32[32,128]{1,0:T(8,128)S(1)}, u32[]{:S(2)}, u32[]{:S(2)}) collective-permute-start(f32[32,128]{1,0:T(8,128)S(1)} %slice.356), channel_id=1, source_target_pairs={{0,32},{32,64},{64,96},{96,128},{128,160},{160,192},{192,224},{1,3... | collective-permute-start | bytes 49160 | tf_op jit(solution)/shard_map/while/body/eval_jaxpr/ppermute | solution.py:17
  490.3 5.1 collective-permute-start.1
  495.4 85.4 %collective-permute-start.3 = (f32[32,128]{1,0:T(8,128)S(1)}, f32[32,128]{1,0:T(8,128)S(1)}, u32[]{:S(2)}, u32[]{:S(2)}) collective-permute-start(f32[32,128]{1,0:T(8,128)S(1)} %slice.253), channel_id=1, source_target_pairs={{32,0},{64,32},{96,64},{128,96},{160,128},{192,160},{224,192},{33,... | collective-permute-start | bytes 49160 | tf_op jit(solution)/shard_map/ppermute | solution.py:17
  591.7 8.2 collective-permute-start
  688.3 3.1 collective-permute-start
  691.4 93.3 %collective-permute-start = (f32[32,128]{1,0:T(8,128)S(1)}, f32[32,128]{1,0:T(8,128)S(1)}, u32[]{:S(2)}, u32[]{:S(2)}) collective-permute-start(f32[32,128]{1,0:T(8,128)S(1)} %slice.357), channel_id=1, source_target_pairs={{0,32},{32,64},{64,96},{96,128},{128,160},{160,192},{192,224},{1,3... | collective-permute-start | bytes 49160 | tf_op jit(solution)/shard_map/while/body/eval_jaxpr/ppermute | solution.py:17
  784.7 5.1 collective-permute-start
  789.8 89.3 %collective-permute-start = (f32[32,128]{1,0:T(8,128)S(1)}, f32[32,128]{1,0:T(8,128)S(1)}, u32[]{:S(2)}, u32[]{:S(2)}) collective-permute-start(f32[32,128]{1,0:T(8,128)S(1)} %slice.357), channel_id=1, source_target_pairs={{0,32},{32,64},{64,96},{96,128},{128,160},{160,192},{192,224},{1,3... | collective-permute-start | bytes 49160 | tf_op jit(solution)/shard_map/while/body/eval_jaxpr/ppermute | solution.py:17
  879.1 5.1 collective-permute-start
  884.2 91.3 %collective-permute-start = (f32[32,128]{1,0:T(8,128)S(1)}, f32[32,128]{1,0:T(8,128)S(1)}, u32[]{:S(2)}, u32[]{:S(2)}) collective-permute-start(f32[32,128]{1,0:T(8,128)S(1)} %slice.357), channel_id=1, source_target_pairs={{0,32},{32,64},{64,96},{96,128},{128,160},{160,192},{192,224},{1,3... | collective-permute-start | bytes 49160 | tf_op jit(solution)/shard_map/while/body/eval_jaxpr/ppermute | solution.py:17
  975.6 5.1 collective-permute-start
  986.1 273.0 %all-to-all-start = ((bf16[8,256,32]{1,2,0:T(8,128)(2,1)}), bf16[8,256,32]{1,2,0:T(8,128)(2,1)S(1)}, u32[]{:S(2)}, u32[]{:S(2)}) async-start(bf16[8,256,32]{1,2,0:T(8,128)(2,1)} %broadcast_in_dim.142), calls=%async_computation | async-start | bytes 262144 | tf_op jit(solution)/shard_map/all_to_all | solution.py:42
  1260.1 19.8 all-to-all-start.1
  1280.9 359.6 %all-to-all-start.3 = ((bf16[8,256,256]{2,1,0:T(8,128)(2,1)}), bf16[8,256,256]{2,1,0:T(8,128)(2,1)}, u32[]{:S(2)}, u32[]{:S(2)}) async-start(bf16[8,256,256]{2,1,0:T(8,128)(2,1)} %broadcast_in_dim.147), calls=%async_computation.3 | async-start | bytes 2097152 | tf_op jit(solution)/shard_map/all_to_all | solution.py:42
  1641.3 10.1 all-to-all-start.2
Sparse Core Ops, SparseCore 0:
  9.1 32.8 all-gather.5
  43.8 135.8 all-gather.3
where the time goes:
time: 2030 us; the launch traced here: 2020 us
  starting transfers between devices  850 us (42%)
  matrix products  416 us (20%)
  local copies, waits for them, and re-layouts  375 us (18%)
  waiting for transfers between devices  231 us (11%)
  other arithmetic  101 us (5%)
  loops' own time  38 us (2%)
    ppermute x18, starting transfers between devices, from_behind(): lax.ppermute(value, axis, [(source, source + steps) for source in range(f...  569 us
    dot_general x512, matrix products, step(): partial_sum = jnp.dot(matrow, solution)  377 us
    dynamic_slice x512, local copies, waits for them, and re-layouts, step(): pivot = lax.dynamic_index_in_dim(matrow, place, 0, keepdims=False)  303 us
    all_to_all x4, starting transfers between devices, sent_to_all(): lax.all_to_all(jnp.broadcast_to(x[None], (peers, *x.shape)), axis, 0, 0,...  281 us
    ppermute x18, waiting for transfers between devices, from_behind(): lax.ppermute(value, axis, [(source, source + steps) for source in range(f...  186 us
    div x16, other arithmetic, upper_solve(): solved[back_at] = value / matrix[back_at, back_at]  97.9 us
  transfers between devices with their start and end apart: 24, of which 21 were waited for; matrix products, arithmetic and copies ran while one was open for 22% of the time, Pallas kernels for 0%

commit v1 on v0

v1 whole, which is shorter than its diff:
```python
import functools

import jax
import jax.numpy as jnp
from jax import lax
from jax.experimental import pallas as pl
from jax.experimental.pallas import tpu as pltpu
from jax.sharding import Mesh
from jax.sharding import PartitionSpec as P

COL = ("x", "z")
LANE = 128
F32 = jnp.float32
BF16 = jnp.bfloat16
CONTRACT_LAST = (((1,), (1,)), ((), ()))
HIGH = lax.Precision.HIGHEST


def from_behind(value, axis, steps):
    count = lax.axis_size(axis)
    first, last = (max(0, -steps), min(count, count - steps))
    return lax.ppermute(value, axis, [(source, source + steps) for source in range(first, last)])


def span_factors(vectors):
    refl = len(vectors)
    solved = []
    for i in range(refl):
        value = vectors[i]
        for j in range(i):
            value = value - jnp.sum(vectors[j] * vectors[i], axis=1, keepdims=True) * solved[j]
        pivot = 0.5 * jnp.sum(vectors[i] * vectors[i], axis=1, keepdims=True)
        solved.append(value / pivot)
    return solved


def sweep_body(offsets_ref, vectors_ref, state_ref, pairs_ref):
    spans, refl, band = vectors_ref.shape
    vectors = [vectors_ref[:, i, :] for i in range(refl)]
    factors = span_factors(vectors)
    for i in range(refl):
        pairs_ref[:, i, 0:band] = vectors[i]
        pairs_ref[:, refl + i, 0:band] = factors[i]
        pairs_ref[:, i, band:] = jnp.zeros((spans, band), F32)
        pairs_ref[:, refl + i, band:] = jnp.zeros((spans, band), F32)
    for span_at in range(spans):
        begin = offsets_ref[span_at]
        base = pl.multiple_of(begin // LANE * LANE, LANE)
        moved = pltpu.roll(pairs_ref[span_at], begin - base, 1)
        window = state_ref[:, pl.ds(base, 2 * band)]
        update = window
        for i in range(refl):
            inner = jnp.sum(window * moved[i : i + 1, :], axis=1, keepdims=True)
            update = update - inner * moved[refl + i : refl + i + 1, :]
        state_ref[:, pl.ds(base, 2 * band)] = update


def overhang_kernel(offsets_ref, vectors_ref, own_ref, below_ref, out_ref, state_ref, pairs_ref):
    columns = own_ref.shape[1]
    state_ref[:, 0:columns] = own_ref[...]
    state_ref[:, columns:] = below_ref[...]
    sweep_body(offsets_ref, vectors_ref, state_ref, pairs_ref)
    out_ref[...] = state_ref[:, columns:]


def sweep_kernel(
    place_ref, offsets_ref, vectors_ref, own_ref, above_ref, below_ref, out_ref, *rest, cut
):
    state_ref, pairs_ref = rest[-2:]
    rows, columns = own_ref.shape
    band = below_ref.shape[1]
    state_ref[:, 0:columns] = own_ref[...]
    state_ref[:, columns:] = below_ref[...]

    @pl.when(place_ref[0] > 0)
    def _():
        state_ref[:, 0:band] = above_ref[...]

    sweep_body(offsets_ref, vectors_ref, state_ref, pairs_ref)
    out_ref[...] = state_ref[:, 0:columns]
    if cut:
        pieces_ref = rest[0]
        for at in range(pieces_ref.shape[0]):
            span = min(cut, columns - at * cut)
            pieces_ref[at, :, 0:span] = state_ref[:, at * cut : at * cut + span].astype(BF16)
            if span < cut:
                pieces_ref[at, :, span:] = jnp.zeros((rows, cut - span), BF16)


def sweep_scratch(own, vectors):
    rows, columns = own.shape
    spans, refl, band = vectors.shape
    return [pltpu.VMEM((rows, columns + band), F32), pltpu.VMEM((spans, 2 * refl, 2 * band), F32)]


VM = pl.BlockSpec(memory_space=pltpu.VMEM)
SM = pl.BlockSpec(memory_space=pltpu.SMEM)


def cost(flops, size):
    return pl.CostEstimate(flops=flops, bytes_accessed=size, transcendentals=0)


def overhang(own, below, vectors, offsets):
    return pl.pallas_call(
        overhang_kernel,
        out_shape=jax.ShapeDtypeStruct(below.shape, F32),
        in_specs=[SM, VM, VM, VM],
        out_specs=VM,
        scratch_shapes=sweep_scratch(own, vectors),
        cost_estimate=cost(8 * own.size, 8 * own.size),
    )(offsets, vectors, own, below)


def sweep(place, own, above, below, vectors, offsets, pieces, cut):
    shapes = [jax.ShapeDtypeStruct(own.shape, F32)]
    if cut:
        shapes.append(jax.ShapeDtypeStruct((pieces, own.shape[0], cut), BF16))
    return pl.pallas_call(
        functools.partial(sweep_kernel, cut=cut),
        out_shape=shapes,
        in_specs=[SM, SM, VM, VM, VM, VM],
        out_specs=[VM] * len(shapes),
        scratch_shapes=sweep_scratch(own, vectors),
        cost_estimate=cost(8 * own.size, 8 * own.size),
    )(place, offsets, vectors, own, above, below)


def sweeps(eigen, vectors, offsets, pieces, cut):
    band = vectors.shape[3]
    count, spans = offsets.shape
    assert eigen.shape[1] > (spans + 1) * band
    place = lax.axis_index("row").astype(jnp.int32)[None]
    for at in range(count):
        below = from_behind(eigen[:, :band], "row", -1)
        above = from_behind(overhang(eigen, below, vectors[at], offsets[at]), "row", 1)
        last = at == count - 1
        got = sweep(
            place, eigen, above, below, vectors[at], offsets[at], pieces, cut if last else 0
        )
        eigen = got[0]
    return got


def products_kernel(gathered_ref, eigen_ref, ordered_ref, sums_ref, total_ref, *, dims):
    z_size, x_size, panels, own = dims
    step = pl.program_id(0)
    for z in range(z_size):
        for x in range(x_size):
            for p in range(panels):
                to = ((p * x_size + x) * z_size + z) * own
                at = ((z * x_size + x) * panels + p) * own
                ordered_ref[to : to + own, :] = gathered_ref[at : at + own, :]

    @pl.when(step == 0)
    def _():
        total_ref[...] = jnp.zeros_like(total_ref)

    order = ordered_ref.shape[0]
    reflect = ordered_ref[...]
    total_ref[:, 0:order] += lax.dot_general(
        reflect, reflect, CONTRACT_LAST, preferred_element_type=F32
    )
    total_ref[:, order:] += lax.dot_general(
        reflect, eigen_ref[...], CONTRACT_LAST, preferred_element_type=F32
    )

    @pl.when(step == pl.num_programs(0) - 1)
    def _():
        sums_ref[...] = total_ref[...].astype(BF16)


def block_of(columns):
    tiles = columns // LANE
    return LANE * max(d for d in range(1, 9) if tiles % d == 0)


def products(gathered, eigen, dims):
    order, columns = gathered.shape
    count = eigen.shape[0]
    block = block_of(columns)
    return pl.pallas_call(
        functools.partial(products_kernel, dims=dims),
        grid=(columns // block,),
        in_specs=[
            pl.BlockSpec((order, block), lambda k: (0, k)),
            pl.BlockSpec((count, block), lambda k: (0, k)),
        ],
        out_specs=[
            pl.BlockSpec((order, block), lambda k: (0, k)),
            pl.BlockSpec((order, order + count), lambda k: (0, 0)),
        ],
        out_shape=[
            jax.ShapeDtypeStruct((order, columns), BF16),
            jax.ShapeDtypeStruct((order, order + count), BF16),
        ],
        scratch_shapes=[pltpu.VMEM((order, order + count), F32)],
        compiler_params=pltpu.CompilerParams(dimension_semantics=("arbitrary",)),
        cost_estimate=cost(2 * order * (order + count) * columns, 6 * order * columns),
    )(gathered, eigen)


def small_inverses(grams):
    order = grams[0].shape[0]
    row = lax.broadcasted_iota(jnp.int32, (order, order), 0)
    col = lax.broadcasted_iota(jnp.int32, (order, order), 1)
    eye = row == col
    found = [jnp.where(eye, 2.0 / jnp.where(eye, gram, 1.0), 0.0) for gram in grams]
    size = 1
    while size < order:
        pick = (row // (2 * size) == col // (2 * size)) & (row // size < col // size)
        for at, gram in enumerate(grams):
            part = jnp.where(pick, gram, 0.0)
            if size == 1:
                left = jnp.sum(found[at], axis=1, keepdims=True)
                right = jnp.sum(found[at], axis=0, keepdims=True)
                step = left * part * right
            else:
                step = jnp.dot(part, found[at], precision=HIGH, preferred_element_type=F32)
                step = jnp.dot(found[at], step, precision=HIGH, preferred_element_type=F32)
            found[at] = found[at] - step
        size *= 2
    return found


def correction_kernel(sums_ref, ordered_ref, out_ref, coeffs_ref, *, panels):
    order = ordered_ref.shape[0]
    pieces, count, _ = out_ref.shape

    @pl.when(pl.program_id(0) == 0)
    def _():
        width = order // panels
        parts = width // LANE
        gram = lambda i, j: sums_ref[i : i + LANE, j : j + LANE].astype(F32)
        starts = [k * LANE for k in range(order // LANE)]
        inverses = small_inverses([gram(i, i) for i in starts])
        solved = {}
        for panel in range(panels):
            for part in range(parts - 1, -1, -1):
                i = panel * width + part * LANE
                value = sums_ref[i : i + LANE, order:].astype(F32)
                for j in solved:
                    if j < panel * width:
                        value = value - jnp.dot(
                            sums_ref[i : i + LANE, j : j + LANE],
                            solved[j].astype(BF16),
                            preferred_element_type=F32,
                        )
                    else:
                        value = value - jnp.dot(
                            gram(i, j), solved[j], precision=HIGH, preferred_element_type=F32
                        )
                value = jnp.dot(
                    inverses[i // LANE], value, precision=HIGH, preferred_element_type=F32
                )
                solved[i] = value
        for i in solved:
            coeffs_ref[:, i : i + LANE] = solved[i].T.astype(BF16)

    product = jnp.dot(coeffs_ref[...], ordered_ref[...], preferred_element_type=F32).astype(BF16)
    for at in range(pieces):
        out_ref[at] = product[at * count : (at + 1) * count]


def correction(sums, ordered, pieces, panels):
    order, columns = ordered.shape
    count = sums.shape[1] - order
    block = block_of(columns)
    return pl.pallas_call(
        functools.partial(correction_kernel, panels=panels),
        grid=(columns // block,),
        in_specs=[
            pl.BlockSpec((order, order + count), lambda k: (0, 0)),
            pl.BlockSpec((order, block), lambda k: (0, k)),
        ],
        out_specs=pl.BlockSpec((pieces, count // pieces, block), lambda k: (0, 0, k)),
        out_shape=jax.ShapeDtypeStruct((pieces, count // pieces, columns), BF16),
        scratch_shapes=[pltpu.VMEM((count, order), BF16)],
        compiler_params=pltpu.CompilerParams(dimension_semantics=("arbitrary",)),
        cost_estimate=cost(2 * order * count * columns, 2 * order * columns),
    )(sums, ordered)


def subtract_kernel(eigen_ref, piece_ref, out_ref):
    out_ref[...] = eigen_ref[...] - piece_ref[0].astype(F32)


def subtract(eigen, pieces):
    count, rows, cut = pieces.shape
    return pl.pallas_call(
        subtract_kernel,
        grid=(count,),
        in_specs=[
            pl.BlockSpec((rows, cut), lambda k: (0, k)),
            pl.BlockSpec((1, rows, cut), lambda k: (k, 0, 0)),
        ],
        out_specs=pl.BlockSpec((rows, cut), lambda k: (0, k)),
        out_shape=jax.ShapeDtypeStruct(eigen.shape, F32),
        compiler_params=pltpu.CompilerParams(dimension_semantics=("arbitrary",)),
        cost_estimate=cost(eigen.size, 10 * eigen.size),
    )(eigen, pieces)


def exchange(pieces, axes):
    return lax.all_to_all(pieces, axes, 0, 0, tiled=True)


def local(eigvecs, span_vectors, span_offsets, panels):
    x_size, z_size = lax.axis_size("x"), lax.axis_size("z")
    peers = lax.axis_size("row") * x_size
    count, own, columns = panels.shape
    order = count * own * x_size * z_size
    cut = -(-columns // (LANE * x_size)) * LANE
    padded = jnp.pad(panels, ((0, 0), (0, 0), (0, x_size * cut - columns)))
    pieces = padded.reshape(count, own, x_size, cut).transpose(2, 0, 1, 3)
    mine = exchange(pieces.reshape(x_size, count * own, cut), "x")
    gathered = lax.all_gather(mine.reshape(-1, cut), "z", axis=0, tiled=True)
    eigen, rounded = sweeps(eigvecs, span_vectors, span_offsets, x_size, cut)
    others = exchange(rounded, "x").reshape(-1, cut)
    ordered, sums = products(gathered, others, (z_size, x_size, count, own))
    parts = exchange(sums.reshape(peers, order // peers, -1), ("row", "x"))
    total = jnp.sum(parts.astype(F32), axis=0).astype(BF16)
    sums = exchange(jnp.broadcast_to(total[None], (peers, *total.shape)), ("row", "x"))
    corrections = correction(sums.reshape(order, -1), ordered, x_size, count)
    return subtract(eigen, exchange(corrections, "x"))


def solution(mesh):
    finer = Mesh(mesh.devices.reshape(mesh.shape["row"], 4, 8), ("row", "x", "z"))
    placed = (P(COL, "row"), P(None, "row", None, None), P(None, "row"), P(None, COL, "row"))
    return jax.shard_map(
        local, mesh=finer, in_specs=placed, out_specs=P(COL, "row"), check_vma=False
    )
```

time: 2030 us -> 154 us (0.08)
  starting transfers between devices: 850 us -> 10.5 us
  matrix products: 416 us -> 0 us
  local copies, waits for them, and re-layouts: 375 us -> 6.11 us
  waiting for transfers between devices: 231 us -> 7.81 us
  other arithmetic: 101 us -> 0.1 us
  blocking collectives: 0 us -> 79.9 us
  loops' own time: 38 us -> 0 us
  Pallas kernels: 0 us -> 34.8 us
    ppermute x18 -> x4, starting transfers between devices: 569 us -> 10.5 us  [from_behind(): lax.ppermute(value, axis, [(source, source + steps) for source in range(f...]
    dot_general x566 -> x0, matrix products: 416 us -> none  [the longest x512 377 us: step(): partial_sum = jnp.dot(matrow, solution)]
    dynamic_slice x528 -> x0, local copies, waits for them, and re-layouts: 312 us -> none  [the longest x512 303 us: step(): pivot = lax.dynamic_index_in_dim(matrow, place, 0, keepdims=False)]
    all_to_all x4 -> x0, starting transfers between devices: 281 us -> none  [sent_to_all(): lax.all_to_all(jnp.broadcast_to(x[None], (peers, *x.shape)), axis, 0, 0,...]
    ppermute x18 -> x4, waiting for transfers between devices: 186 us -> 7.79 us  [from_behind(): lax.ppermute(value, axis, [(source, source + steps) for source in range(f...]
    div x16 -> x0, other arithmetic: 97.9 us -> none  [upper_solve(): solved[back_at] = value / matrix[back_at, back_at]]
    all_to_all x0 -> x5, blocking collectives: none -> 79.9 us  [exchange(): return lax.all_to_all(pieces, axes, 0, 0, tiled=True)]
    another operation x22 -> x0, loops' own time: 38 us -> none  [the longest x2 28.4 us: run_spans(): return lax.fori_loop(0, vectors.shape[0], advance, block)]
  transfers between devices with their start and end apart: 24 -> 5, of which waited for: 21 -> 4; matrix products, arithmetic and copies ran while one was open for 22% -> 2% of each run, Pallas kernels for 0% -> 9%
where the time goes in v1:
time: 154 us; the launch traced here: 153 us
  blocking collectives  79.9 us (52%)
  Pallas kernels  34.8 us (23%)
  between operations  13.5 us (9%)
  starting transfers between devices  10.5 us (7%)
  waiting for transfers between devices  7.81 us (5%)
  local copies, waits for them, and re-layouts  6.11 us (4%)
    all_to_all x5, blocking collectives, exchange(): return lax.all_to_all(pieces, axes, 0, 0, tiled=True)  79.9 us
    ppermute x4, starting transfers between devices, from_behind(): lax.ppermute(value, axis, [(source, source + steps) for source in range(f...  10.5 us
    pallas_call x1, Pallas kernels, correction(): pl.pallas_call(functools.partial(correction_kernel, panels=panels), grid=...  9.69 us
    pallas_call x2, Pallas kernels, sweep(): pl.pallas_call(functools.partial(sweep_kernel, cut=cut), out_shape=shapes...  7.8 us
    ppermute x4, waiting for transfers between devices, from_behind(): lax.ppermute(value, axis, [(source, source + steps) for source in range(f...  7.79 us
    pallas_call x1, Pallas kernels, products(): pl.pallas_call(functools.partial(products_kernel, dims=dims), grid=(colum...  7.56 us
    pallas_call x2, Pallas kernels, overhang(): pl.pallas_call(overhang_kernel, out_shape=jax.ShapeDtypeStruct(below.shap...  6.08 us
    pallas_call x1, Pallas kernels, subtract(): pl.pallas_call(subtract_kernel, grid=(count,), in_specs=[pl.BlockSpec((ro...  3.71 us
  transfers between devices with their start and end apart: 5, of which 4 were waited for; matrix products, arithmetic and copies ran while one was open for 2% of the time, Pallas kernels for 9%

profile of v1, /device:TPU:1, one launch (start us, length us, event | category | flops | bytes accessed | tf_op | source)
XLA Modules:
  0.0 152.7 jit_solution(1069010933129966412)
XLA Ops:
  6.5 1.0 pad.4
  7.6 11.3 %all_to_all.25 = bf16[4,16,3200]{2,1,0:T(8,128)(2,1)} all-to-all(bf16[4,16,3200]{2,1,0:T(8,128)(2,1)S(1)} %bitcast.21), channel_id=1, replica_groups=mesh['row'=8,'x'=4,'z'=8] {'x'}, dimensions={0} | all-to-all | bytes 819200 | tf_op jit(solution)/shard_map/all_to_all | solution.py:305
  18.9 0.0 all-gather.2.cloned.1.call-update
  18.9 0.7 slice.26
  19.6 4.6 %collective-permute-start = (f32[32,128]{1,0:T(8,128)S(1)}, f32[32,128]{1,0:T(8,128)S(1)}, u32[]{:S(2)}, u32[]{:S(2)}) collective-permute-start(f32[32,128]{1,0:T(8,128)S(1)} %slice.26), channel_id=1, source_target_pairs={{32,0},{64,32},{96,64},{128,96},{160,128},{192,160},{224,192},{33,... | collective-permute-start | bytes 49160 | tf_op jit(solution)/shard_map/ppermute | solution.py:22
  24.2 0.6 slice_bitcast_fusion
  24.8 0.5 slice_bitcast_fusion.2
  25.4 1.4 collective-permute-done.below_ref
  26.8 0.6 copy-done
  27.4 3.0 %shard_map.46 = f32[32,128]{1,0:T(8,128)} custom-call(s32[8]{0:T(128)} %get-tuple-element.15.offsets_ref, f32[8,4,128]{2,1,0:T(4,128)} %get-tuple-element.13.vectors_ref, f32[32,12544]{1,0:T(8,128)} %own_ref.3, f32[32,128]{1,0:T(8,128)} %copy-done), custom_call_target="tpu_custom_call" | custom-call | flops 3211264 | bytes 3211264 | tf_op jit(solution)/shard_map/pallas_call | solution.py:105
  30.4 1.9 %collective-permute-start.1 = (f32[32,128]{1,0:T(8,128)}, f32[32,128]{1,0:T(8,128)S(1)}, u32[]{:S(2)}, u32[]{:S(2)}) collective-permute-start(f32[32,128]{1,0:T(8,128)} %shard_map.46), channel_id=1, source_target_pairs={{0,32},{32,64},{64,96},{96,128},{128,160},{160,192},{192,224},{1,3... | collective-permute-start | bytes 49160 | tf_op jit(solution)/shard_map/ppermute | solution.py:22
  32.4 1.3 collective-permute-done.1.above_ref
  33.7 0.6 copy-done.3
  34.3 3.8 %shard_map.47.own_ref = f32[32,12544]{1,0:T(8,128)} custom-call(s32[1]{0:T(128)} %bitcast.place_ref, s32[8]{0:T(128)} %get-tuple-element.15.offsets_ref, f32[8,4,128]{2,1,0:T(4,128)} %get-tuple-element.13.vectors_ref, f32[32,12544]{1,0:T(8,128)} %own_ref.3, f32[32,128]{1,0:T(8,128)} %copy-done.3, f32[32,128]{1,0:T(8,128)} %copy-done), custom_call_target="tpu_custom_call" | custom-call | flops 3211264 | bytes 3211264 | tf_op jit(solution)/shard_map/pallas_call | solution.py:119
  38.1 0.7 slice.28
  38.8 2.1 %collective-permute-start.2 = (f32[32,128]{1,0:T(8,128)S(1)}, f32[32,128]{1,0:T(8,128)S(1)}, u32[]{:S(2)}, u32[]{:S(2)}) collective-permute-start(f32[32,128]{1,0:T(8,128)S(1)} %slice.28), channel_id=1, source_target_pairs={{32,0},{64,32},{96,64},{128,96},{160,128},{192,160},{224,192},{33,... | collective-permute-start | bytes 49160 | tf_op jit(solution)/shard_map/ppermute | solution.py:22
  40.9 3.7 %collective-permute-done.2.below_ref = f32[32,128]{1,0:T(8,128)S(1)} collective-permute-done((f32[32,128]{1,0:T(8,128)S(1)}, f32[32,128]{1,0:T(8,128)S(1)}, u32[]{:S(2)}, u32[]{:S(2)}) %collective-permute-start.2) | collective-permute-done | bytes 16416 | tf_op jit(solution)/shard_map/ppermute | solution.py:22
  44.5 0.6 copy-done.1
  45.1 3.0 %shard_map.48 = f32[32,128]{1,0:T(8,128)} custom-call(s32[8]{0:T(128)} %get-tuple-element.16.offsets_ref, f32[8,4,128]{2,1,0:T(4,128)} %get-tuple-element.14.vectors_ref, f32[32,12544]{1,0:T(8,128)} %shard_map.47.own_ref, f32[32,128]{1,0:T(8,128)} %copy-done.1), custom_call_target="tpu_custom_call" | custom-call | flops 3211264 | bytes 3211264 | tf_op jit(solution)/shard_map/pallas_call | solution.py:105
  48.2 1.9 %collective-permute-start.3 = (f32[32,128]{1,0:T(8,128)}, f32[32,128]{1,0:T(8,128)S(1)}, u32[]{:S(2)}, u32[]{:S(2)}) collective-permute-start(f32[32,128]{1,0:T(8,128)} %shard_map.48), channel_id=1, source_target_pairs={{0,32},{32,64},{64,96},{96,128},{128,160},{160,192},{192,224},{1,3... | collective-permute-start | bytes 49160 | tf_op jit(solution)/shard_map/ppermute | solution.py:22
  50.1 1.4 collective-permute-done.3.above_ref
  51.5 0.6 copy-done.4
  52.1 4.0 %shard_map.49 = (f32[32,12544]{1,0:T(8,128)}, bf16[4,32,3200]{2,1,0:T(8,128)(2,1)}) custom-call(s32[1]{0:T(128)} %bitcast.place_ref, s32[8]{0:T(128)} %get-tuple-element.16.offsets_ref, f32[8,4,128]{2,1,0:T(4,128)} %get-tuple-element.14.vectors_ref, f32[32,12544]{1,0:T(8,128)} %shard_map.47.own_ref, f32[32,128]{1,0:T(8,128)} %copy-done.4, f32[32,128]{1,0:T(8,128)} %copy-done.1), custom_call_target="tpu_custom_call" | custom-call | flops 3211264 | bytes 3211264 | tf_op jit(solution)/shard_map/pallas_call | solution.py:119
  56.1 16.5 %all_to_all.26 = bf16[4,32,3200]{2,1,0:T(8,128)(2,1)} all-to-all(bf16[4,32,3200]{2,1,0:T(8,128)(2,1)} %get-tuple-element.10), channel_id=1, replica_groups=mesh['row'=8,'x'=4,'z'=8] {'x'}, dimensions={0} | all-to-all | bytes 1638400 | tf_op jit(solution)/shard_map/all_to_all | solution.py:305
  72.6 7.6 %shard_map.50 = (bf16[512,3200]{1,0:T(8,128)(2,1)}, bf16[512,640]{1,0:T(8,128)(2,1)}) custom-call(bf16[512,3200]{1,0:T(8,128)(2,1)} %all-gather.2.cloned.1.call-done.gathered_ref, bf16[128,3200]{1,0:T(8,128)(2,1)} %bitcast.23), custom_call_target="tpu_custom_call" | custom-call | flops 2097152000 | bytes 9830400 | tf_op jit(solution)/shard_map/pallas_call | solution.py:182
  80.2 18.9 %all_to_all.27 = bf16[32,16,640]{2,1,0:T(8,128)(2,1)S(1)} all-to-all(bf16[32,16,640]{2,1,0:T(8,128)(2,1)} %bitcast.24), channel_id=1, replica_groups=mesh['row'=8,'x'=4,'z'=8] {'row','x'}, dimensions={0} | all-to-all | bytes 1310720 | tf_op jit(solution)/shard_map/all_to_all | solution.py:305
  99.1 0.1 reduce_sum.12
  99.2 0.1 broadcast_in_dim.10
  99.2 17.0 %all_to_all.28 = bf16[32,16,640]{2,1,0:T(8,128)(2,1)} all-to-all(bf16[32,16,640]{2,1,0:T(8,128)(2,1)S(1)} %broadcast_in_dim.10), channel_id=1, replica_groups=mesh['row'=8,'x'=4,'z'=8] {'row','x'}, dimensions={0} | all-to-all | bytes 1310720 | tf_op jit(solution)/shard_map/all_to_all | solution.py:305
  116.2 9.7 %shard_map.51 = bf16[4,32,3200]{2,1,0:T(8,128)(2,1)} custom-call(bf16[512,640]{1,0:T(8,128)(2,1)} %bitcast.19, bf16[512,3200]{1,0:T(8,128)(2,1)} %get-tuple-element.12.ordered_ref), custom_call_target="tpu_custom_call" | custom-call | flops 419430400 | bytes 3276800 | tf_op jit(solution)/shard_map/pallas_call | solution.py:269
  125.9 16.3 %all_to_all.29.piece_ref = bf16[4,32,3200]{2,1,0:T(8,128)(2,1)} all-to-all(bf16[4,32,3200]{2,1,0:T(8,128)(2,1)} %shard_map.51), channel_id=1, replica_groups=mesh['row'=8,'x'=4,'z'=8] {'x'}, dimensions={0} | all-to-all | bytes 1638400 | tf_op jit(solution)/shard_map/all_to_all | solution.py:305
  142.2 3.7 %shard_map.52 = f32[32,12544]{1,0:T(8,128)} custom-call(f32[32,12544]{1,0:T(8,128)} %get-tuple-element.9.eigen_ref, bf16[4,32,3200]{2,1,0:T(8,128)(2,1)} %all_to_all.29.piece_ref), custom_call_target="tpu_custom_call" | custom-call | flops 401408 | bytes 4014080 | tf_op jit(solution)/shard_map/pallas_call | solution.py:290
  (11 shorter events, 0.0 us)
Async XLA Ops:
  6.5 17.7 %copy-start.2 = (f32[2,8,4,128]{3,2,1,0:T(4,128)S(1)}, f32[2,8,4,128]{3,2,1,0:T(4,128)}, u32[]{:S(2)}) copy-start(f32[2,8,4,128]{3,2,1,0:T(4,128)} %param.5) | copy-start | bytes 98308
  6.5 18.3 %copy-start.5 = (s32[2,8]{1,0:T(2,128)S(1)}, s32[2,8]{1,0:T(2,128)}, u32[]{:S(2)}) copy-start(s32[2,8]{1,0:T(2,128)} %param.6) | copy-start | bytes 196
  6.5 66.1 %all-gather.2.cloned.1.call-start = ((), (), s32[]{:S(2)}) async-start(), calls=%async_computation.5 | async-start | bytes 3686400 | tf_op jit(solution)/shard_map/all_gather | solution.py:317
  19.6 7.2 %collective-permute-start = (f32[32,128]{1,0:T(8,128)S(1)}, f32[32,128]{1,0:T(8,128)S(1)}, u32[]{:S(2)}, u32[]{:S(2)}) collective-permute-start(f32[32,128]{1,0:T(8,128)S(1)} %slice.26), channel_id=1, source_target_pairs={{32,0},{64,32},{96,64},{128,96},{160,128},{192,160},{224,192},{33,... | collective-permute-start | bytes 49160 | tf_op jit(solution)/shard_map/ppermute | solution.py:22
  26.8 0.6 copy-start
  30.4 3.3 %collective-permute-start.1 = (f32[32,128]{1,0:T(8,128)}, f32[32,128]{1,0:T(8,128)S(1)}, u32[]{:S(2)}, u32[]{:S(2)}) collective-permute-start(f32[32,128]{1,0:T(8,128)} %shard_map.46), channel_id=1, source_target_pairs={{0,32},{32,64},{64,96},{96,128},{128,160},{160,192},{192,224},{1,3... | collective-permute-start | bytes 49160 | tf_op jit(solution)/shard_map/ppermute | solution.py:22
  33.7 0.6 copy-start.3
  38.8 5.7 %collective-permute-start.2 = (f32[32,128]{1,0:T(8,128)S(1)}, f32[32,128]{1,0:T(8,128)S(1)}, u32[]{:S(2)}, u32[]{:S(2)}) collective-permute-start(f32[32,128]{1,0:T(8,128)S(1)} %slice.28), channel_id=1, source_target_pairs={{32,0},{64,32},{96,64},{128,96},{160,128},{192,160},{224,192},{33,... | collective-permute-start | bytes 49160 | tf_op jit(solution)/shard_map/ppermute | solution.py:22
  44.5 0.6 copy-start.1
  48.2 3.3 %collective-permute-start.3 = (f32[32,128]{1,0:T(8,128)}, f32[32,128]{1,0:T(8,128)S(1)}, u32[]{:S(2)}, u32[]{:S(2)}) collective-permute-start(f32[32,128]{1,0:T(8,128)} %shard_map.48), channel_id=1, source_target_pairs={{0,32},{32,64},{64,96},{96,128},{128,160},{160,192},{192,224},{1,3... | collective-permute-start | bytes 49160 | tf_op jit(solution)/shard_map/ppermute | solution.py:22
  51.5 0.6 copy-start.4
Sparse Core Ops, SparseCore 0:
  19.0 49.0 all-gather.1

commit v2 on v0

v2 whole, which is shorter than its diff:
```python
import functools

import jax
import jax.numpy as jnp
from jax import lax
from jax.experimental import pallas as pl
from jax.experimental.pallas import tpu as pltpu
from jax.sharding import Mesh
from jax.sharding import PartitionSpec as P


COL = ("x", "z")
X_SIZE, Z_SIZE = 4, 8
LANE = 128
UNIT = 8
F32 = jnp.float32
BF16 = jnp.bfloat16
CONTRACT_LAST = (((1,), (1,)), ((), ()))
VM = pl.BlockSpec(memory_space=pltpu.VMEM)
SM = pl.BlockSpec(memory_space=pltpu.SMEM)
ANY = pl.BlockSpec(memory_space=pl.ANY)
PEERS = (1, 3, 2)


def call(kernel, out_shape, in_specs, args, scratch=(), flops=0, size=0, vmem=0, outs=None):
    outs = outs or jax.tree.map(lambda _: VM, out_shape)
    return pl.pallas_call(
        kernel,
        out_shape=out_shape,
        in_specs=in_specs,
        out_specs=outs,
        scratch_shapes=list(scratch),
        compiler_params=pltpu.CompilerParams(vmem_limit_bytes=vmem << 20) if vmem else None,
        cost_estimate=pl.CostEstimate(flops=flops, bytes_accessed=size, transcendentals=0),
    )(*args)


def shifted(value, axis, steps):
    count = lax.axis_size(axis)
    return lax.ppermute(value, axis, [(at, (at + steps) % count) for at in range(count)])


def from_behind(value, axis, steps):
    count = lax.axis_size(axis)
    first, last = (max(0, -steps), min(count, count - steps))
    return lax.ppermute(value, axis, [(source, source + steps) for source in range(first, last)])


def span_factors(vectors):
    solved = []
    for i in range(len(vectors)):
        value = vectors[i]
        for j in range(i):
            value = value - jnp.sum(vectors[j] * vectors[i], axis=1, keepdims=True) * solved[j]
        pivot = 0.5 * jnp.sum(vectors[i] * vectors[i], axis=1, keepdims=True)
        solved.append(value / pivot)
    return solved


def lay_pairs(vectors, pairs_ref):
    refl, (spans, band) = len(vectors), vectors[0].shape
    factors = span_factors(vectors)
    for i in range(refl):
        pairs_ref[:, i, 0:band] = vectors[i]
        pairs_ref[:, refl + i, 0:band] = factors[i]
        pairs_ref[:, i, band:] = jnp.zeros((spans, band), F32)
        pairs_ref[:, refl + i, band:] = jnp.zeros((spans, band), F32)


def apply_span(begin, pair, state_ref):
    refl = pair.shape[0] // 2
    base = pl.multiple_of(begin // LANE * LANE, LANE)
    moved = pltpu.roll(pair, begin - base, 1)
    window = state_ref[:, pl.ds(base, pair.shape[1])]
    update = window
    for i in range(refl):
        inner = jnp.sum(window * moved[i : i + 1, :], axis=1, keepdims=True)
        update = update - inner * moved[refl + i : refl + i + 1, :]
    state_ref[:, pl.ds(base, pair.shape[1])] = update


def halo_kernel(offsets_ref, vectors_ref, eigen_ref, down_ref, up_ref, sems):
    sweeps, spans, refl, band = vectors_ref.shape
    rows, columns = eigen_ref.shape
    copies = []
    for at, (ref, begin, count) in enumerate(((down_ref, None, sweeps), (up_ref, 0, sweeps - 1))):
        width = ref.shape[1] - count * band - LANE
        begin = columns - width if begin is None else begin
        copies.append(
            pltpu.make_async_copy(
                eigen_ref.at[:, begin : begin + width], ref.at[:, 0:width], sems.at[at]
            )
        )
        copies[-1].start()
        for sweep in range(count):
            for i in range(refl):
                ref[i * spans : (i + 1) * spans, width + sweep * band : width + (sweep + 1) * band] = (
                    vectors_ref[sweep, :, i, :]
                )
        ref[:, width + count * band :] = jnp.zeros((rows, LANE), F32)
        ref[0:sweeps, width + count * band : width + count * band + spans] = offsets_ref[...].astype(F32)
    for copy in copies:
        copy.wait()


def sweep_kernel(
    place_ref, offsets_ref, upper_offsets_ref, lower_offsets_ref,
    vectors_ref, own_ref, upper_ref, lower_ref,
    out_ref, mine_ref, next_ref, last_ref, far_ref,
    state_ref, pairs_ref, rounded_ref,
):
    sweeps, spans, refl, band = vectors_ref.shape
    rows, columns = own_ref.shape
    left = upper_ref.shape[1] - sweeps * band - LANE
    right = lower_ref.shape[1] - (sweeps - 1) * band - LANE
    state_ref[:, 0:left] = upper_ref[:, 0:left]
    state_ref[:, left : left + columns] = own_ref[...]
    state_ref[:, left + columns :] = lower_ref[:, 0:right]
    first = place_ref[0] == 0
    final = place_ref[0] == place_ref[1] - 1

    def beside(ref, width, sweep, i):
        return ref[i * spans : (i + 1) * spans, width + sweep * band : width + (sweep + 1) * band]

    for sweep in range(sweeps):
        lay_pairs([beside(upper_ref, left, sweep, i) for i in range(refl)], pairs_ref.at[sweep * 3])
        lay_pairs([vectors_ref[sweep, :, i, :] for i in range(refl)], pairs_ref.at[sweep * 3 + 1])
        if sweep < sweeps - 1:
            lay_pairs([beside(lower_ref, right, sweep, i) for i in range(refl)], pairs_ref.at[sweep * 3 + 2])
    for sweep in range(sweeps):

        def from_upper(at, carry, sweep=sweep):
            begin = upper_offsets_ref[sweep, at] - (columns - left)

            @pl.when(jnp.logical_and(begin >= 0, jnp.logical_not(first)))
            def _():
                apply_span(begin, pairs_ref[sweep * 3, at], state_ref)

            return carry

        def from_lower(at, carry, sweep=sweep):
            begin = lower_offsets_ref[sweep, at]

            @pl.when(jnp.logical_and(begin <= right - band, jnp.logical_not(final)))
            def _():
                apply_span(left + columns + begin, pairs_ref[sweep * 3 + 2, at], state_ref)

            return carry

        lax.fori_loop(0, spans, from_upper, 0)
        for at in range(spans):
            apply_span(left + offsets_ref[sweep, at], pairs_ref[sweep * 3 + 1, at], state_ref)
        if sweep < sweeps - 1:
            lax.fori_loop(0, spans, from_lower, 0)
    out_ref[...] = state_ref[:, left : left + columns]
    padded = rounded_ref.shape[1]
    rounded_ref[:, 0:columns] = state_ref[:, left : left + columns].astype(BF16)
    rounded_ref[:, columns:] = jnp.zeros((rows, padded - columns), BF16)
    cut = mine_ref.shape[1]
    for step, ref in ((0, mine_ref), (PEERS[0], next_ref), (PEERS[1], last_ref), (PEERS[2], far_ref)):
        at = pl.multiple_of((place_ref[2] + step) % X_SIZE * cut, LANE)
        ref[...] = rounded_ref[:, pl.ds(at, cut)]


def sweep_all(place, eigen, vectors, offsets, cut):
    sweeps, spans, refl, band = vectors.shape
    rows, columns = eigen.shape
    left, right = sweeps * spans * band, ((sweeps - 1) * spans + 1) * band
    assert left + right + band < columns and spans * refl == rows
    wide = lambda width: jax.ShapeDtypeStruct((rows, width), F32)
    down, up = call(
        halo_kernel,
        [wide(left + sweeps * band + LANE), wide(right + (sweeps - 1) * band + LANE)],
        [VM, VM, ANY],
        (offsets, vectors, eigen),
        [pltpu.SemaphoreType.DMA((2,))],
        flops=eigen.size,
        size=4 * eigen.size,
        vmem=8,
    )
    upper = from_behind(down, "row", 1)
    lower = from_behind(up, "row", -1)
    upper_offsets = upper[0:sweeps, -LANE : spans - LANE].astype(jnp.int32)
    lower_offsets = lower[0:sweeps, -LANE : spans - LANE].astype(jnp.int32)
    return call(
        sweep_kernel,
        [jax.ShapeDtypeStruct(eigen.shape, F32)]
        + [jax.ShapeDtypeStruct((rows, cut), BF16)] * 4,
        [SM] * 4 + [VM] * 4,
        (place, offsets, upper_offsets, lower_offsets, vectors, eigen, upper, lower),
        [
            pltpu.VMEM((rows, left + columns + right), F32),
            pltpu.VMEM((3 * sweeps, spans, 2 * refl, 2 * band), F32),
            pltpu.VMEM((rows, X_SIZE * cut), BF16),
        ],
        flops=40 * eigen.size,
        size=12 * eigen.size,
        vmem=14,
    )


def pack_kernel(place_ref, panels_ref, *refs):
    wide_ref = refs[-1]
    panels, own, columns = panels_ref.shape
    for p in range(panels):
        wide_ref[p * own : (p + 1) * own, 0:columns] = panels_ref[p]
    wide_ref[:, columns:] = jnp.zeros((panels * own, wide_ref.shape[1] - columns), BF16)
    for step, ref in zip((0, *PEERS), refs):
        cut = ref.shape[1]
        at = pl.multiple_of((place_ref[2] + step) % X_SIZE * cut, LANE)
        ref[...] = wide_ref[:, pl.ds(at, cut)]


def pack(place, panels, cut):
    rows = panels.shape[0] * panels.shape[1]
    return call(
        pack_kernel,
        [jax.ShapeDtypeStruct((rows, cut), BF16)] * 4,
        [SM, VM],
        (place, panels),
        [pltpu.VMEM((rows, X_SIZE * cut), BF16)],
        flops=panels.size,
        size=4 * panels.size,
        vmem=4,
    )


def piece_shapes(rows, cut):
    full, half = jax.ShapeDtypeStruct((rows, cut), BF16), jax.ShapeDtypeStruct((rows // 2, cut), BF16)
    return [full, full, full, half, half]


def traded(pieces):
    steps = (1, -1, 2) if len(pieces) == 4 else (1, -1, 2, -2)
    got = []
    for piece, step in zip(pieces[1:], steps):
        got.append(shifted(piece, "x", step))
    return got


def ring(block, far):
    ahead = behind = block
    found = [(0, block)]
    for step in range(1, Z_SIZE // 2):
        ahead = shifted(ahead, "z", 1)
        behind = shifted(behind, "z", -1)
        found += [(step, ahead), (Z_SIZE - step, behind)]
    found.append((Z_SIZE // 2, shifted(ahead if far > 0 else behind, "z", far)))
    return found


def products_kernel(place_ref, *refs, spots, own, rows):
    blocks, (mine, one, two, far) = refs[: len(spots)], refs[len(spots) : len(spots) + 4]
    ordered_ref, sums_ref, eigen_ref = refs[len(spots) + 4 :]
    order = ordered_ref.shape[0]
    x, z = place_ref[2], place_ref[3]
    for ref, units in zip(blocks, spots):
        for at, (back_z, back_x, panel) in enumerate(units):
            source = (x + X_SIZE - back_x) % X_SIZE * Z_SIZE + (z + Z_SIZE - back_z) % Z_SIZE
            to = pl.multiple_of(panel * (order // 2) + source * own, UNIT)
            ordered_ref[pl.ds(to, own), :] = ref[at * own : (at + 1) * own, :]
    for back, ref in ((0, mine), (1, one), (3, two), (2, far)):
        to = pl.multiple_of((x + X_SIZE - back) % X_SIZE * rows, UNIT)
        eigen_ref[pl.ds(to, ref.shape[0]), :] = ref[...]

    def put(value, at):
        sums_ref[at * LANE : (at + 1) * LANE] = value.astype(BF16)

    def dot(first, count, other):
        return lax.dot_general(
            ordered_ref[first : first + count, :], other, CONTRACT_LAST, preferred_element_type=F32
        )

    width = order // 2
    early = dot(0, order, ordered_ref[0:width, :])
    late = dot(width, width, ordered_ref[width:, :])
    inner = dot(0, order, eigen_ref[...])
    tile = lambda value, i, j: value[i * LANE : (i + 1) * LANE, j * LANE : (j + 1) * LANE]
    for i in range(4):
        put(tile(inner, i, 0), i)
    for at, (i, j) in enumerate(((0, 0), (0, 1), (1, 1), (2, 0), (2, 1), (3, 0), (3, 1))):
        put(tile(early, i, j), 4 + at)
    for at, (i, j) in enumerate(((0, 0), (0, 1), (1, 1))):
        put(tile(late, i, j), 11 + at)


TILES = {
    at: 4 + k
    for k, at in enumerate(
        ((0, 0), (0, 1), (1, 1), (2, 0), (2, 1), (3, 0), (3, 1), (2, 2), (2, 3), (3, 3))
    )
}


def products(place, found, pieces, spots, own, order, rows):
    cut = pieces[0].shape[1]
    return call(
        functools.partial(products_kernel, spots=spots, own=own, rows=rows),
        [
            jax.ShapeDtypeStruct((order, cut), BF16),
            jax.ShapeDtypeStruct(((4 + len(TILES)) * LANE, LANE), BF16),
        ],
        [SM] + [VM] * (len(found) + len(pieces)),
        (place, *found, *pieces),
        [pltpu.VMEM((LANE, cut), BF16)],
        flops=2 * order * (order + LANE) * cut,
        size=6 * order * cut,
        vmem=18,
    )


def split(value):
    high = value.astype(BF16)
    return high, (value - high.astype(F32)).astype(BF16)


def fine_dot(a, b):
    a0, a1 = a if isinstance(a, tuple) else split(a)
    b0, b1 = b if isinstance(b, tuple) else split(b)
    dot = functools.partial(jnp.dot, preferred_element_type=F32)
    total = dot(a0, b0)
    if b1 is not None:
        total = total + dot(a0, b1)
    if a1 is not None:
        total = total + dot(a1, b0)
    return total


def small_inverses(grams):
    order = grams[0].shape[0]
    row = lax.broadcasted_iota(jnp.int32, (order, order), 0)
    col = lax.broadcasted_iota(jnp.int32, (order, order), 1)
    eye = row == col
    wide = [gram.astype(F32) for gram in grams]
    found = [jnp.where(eye, 2.0 / jnp.where(eye, gram, 1.0), 0.0) for gram in wide]
    size = 1
    while size < order:
        pick = (row // (2 * size) == col // (2 * size)) & (row // size < col // size)
        parts = [jnp.where(pick, gram, 0.0) for gram in wide]
        if size == 1:
            steps = [
                jnp.sum(f, axis=1, keepdims=True) * part * jnp.sum(f, axis=0, keepdims=True)
                for f, part in zip(found, parts)
            ]
        else:
            halves = [split(f) for f in found]
            steps = [fine_dot((part.astype(BF16), None), f) for part, f in zip(parts, halves)]
            steps = [fine_dot(f, step) for f, step in zip(halves, steps)]
        found = [f - step for f, step in zip(found, steps)]
        size *= 2
    return found


def correction_kernel(
    place_ref, sums_ref, ordered_ref, mine_ref, next_ref, last_ref, one_ref, two_ref, coeffs_ref
):
    tile = lambda at: sums_ref[at * LANE : (at + 1) * LANE, :]
    gram = lambda i, j: tile(TILES[i, j])
    inverses = [split(f) for f in small_inverses([gram(i, i) for i in range(4)])]
    solved = {}
    for i in (1, 0, 3, 2):
        value = tile(i).astype(F32)
        for j in solved:
            if j // 2 < i // 2:
                known = (solved[j].astype(BF16), None)
            else:
                known = solved[j]
            value = value - fine_dot((gram(i, j), None), known)
        solved[i] = fine_dot(inverses[i], value)
        coeffs_ref[:, i * LANE : (i + 1) * LANE] = solved[i].T.astype(BF16)
    rows = mine_ref.shape[0]
    x = place_ref[2]

    def product(step, shift, count):
        at = pl.multiple_of((x + step) % X_SIZE * rows + shift, UNIT)
        return jnp.dot(
            coeffs_ref[pl.ds(at, count), :], ordered_ref[...], preferred_element_type=F32
        )

    next_ref[...] = product(PEERS[0], 0, rows).astype(BF16)
    last_ref[...] = product(PEERS[1], 0, rows).astype(BF16)
    far = product(PEERS[2], 0, rows).astype(BF16)
    one_ref[...] = far[0 : rows // 2]
    two_ref[...] = far[rows // 2 :]
    mine_ref[...] = product(0, 0, rows).astype(BF16)


def correction(place, sums, ordered, rows):
    order, cut = ordered.shape
    return call(
        correction_kernel,
        piece_shapes(rows, cut),
        [SM, VM, VM],
        (place, sums, ordered),
        [pltpu.VMEM((LANE, order), BF16)],
        flops=2 * order * LANE * cut,
        size=4 * order * cut,
        vmem=24,
    )


def subtract_kernel(place_ref, eigen_ref, mine, one, two, half0, half1, out_ref):
    rows, columns = eigen_ref.shape
    cut = mine.shape[1]
    half = rows // 2
    sources = {0: ((0, mine),), 1: ((0, one),), 3: ((0, two),), 2: ((0, half0), (half, half1))}
    for at in range(X_SIZE):
        begin, span = at * cut, min(cut, columns - at * cut)
        for back, refs in sources.items():

            @pl.when((place_ref[2] + X_SIZE - back) % X_SIZE == at)
            def _(refs=refs, begin=begin, span=span):
                for row, ref in refs:
                    high = row + ref.shape[0]
                    out_ref[row:high, begin : begin + span] = (
                        eigen_ref[row:high, begin : begin + span] - ref[:, 0:span].astype(F32)
                    )


def subtract(place, eigen, pieces):
    return call(
        subtract_kernel,
        jax.ShapeDtypeStruct(eigen.shape, F32),
        [SM] + [VM] * 6,
        (place, eigen, *pieces),
        flops=eigen.size,
        size=10 * eigen.size,
        vmem=10,
    )


def total_kernel(parts_ref, out_ref):
    total = parts_ref[0].astype(F32)
    for at in range(1, parts_ref.shape[0]):
        total = total + parts_ref[at].astype(F32)
    total = total.astype(BF16)
    for at in range(parts_ref.shape[0]):
        out_ref[at] = total


def total_for_all(parts):
    return call(
        total_kernel,
        jax.ShapeDtypeStruct(parts.shape, BF16),
        [VM],
        (parts,),
        flops=parts.size,
        size=4 * parts.size,
        vmem=4,
    )


def exchange(pieces, axes):
    return lax.all_to_all(pieces, axes, 0, 0, tiled=True)


def inner(eigvecs, span_vectors, span_offsets, panels):
    assert (lax.axis_size("x"), lax.axis_size("z")) == (X_SIZE, Z_SIZE)
    peers = lax.axis_size("row") * X_SIZE
    count, own, columns = panels.shape
    rows = eigvecs.shape[0]
    order = count * own * X_SIZE * Z_SIZE
    cut = -(-columns // (LANE * X_SIZE)) * LANE
    place = jnp.stack(
        [lax.axis_index("row"), lax.axis_size("row"), lax.axis_index("x"), lax.axis_index("z")]
    ).astype(jnp.int32)

    packed = pack(place, panels, cut)
    swept = sweep_all(place, eigvecs, span_vectors, span_offsets, cut)
    eigen, pieces = swept[0], swept[1:]
    one, two, far = traded(packed)
    found, spots = [], []
    for at, (pair, sources) in enumerate((((packed[0], one), (0, 1)), ((two, far), (3, 2)))):
        unit = [(back_x, panel) for back_x in sources for panel in range(count)]
        for back, block in ring(jnp.concatenate(pair, axis=0), 1 - 2 * at):
            found.append(block)
            spots.append([(back, back_x, panel) for back_x, panel in unit])
    others = [pieces[0], *traded(pieces)]
    ordered, sums = products(place, found, others, spots, own, order, rows)

    parts = exchange(sums.reshape(peers, -1, LANE), ("row", "x"))
    sums = exchange(total_for_all(parts), ("row", "x"))
    corrections = correction(place, sums.reshape(-1, LANE), ordered, rows)
    return subtract(place, eigen, [corrections[0], *traded(corrections)])


def solution(mesh):
    finer = Mesh(
        mesh.devices.reshape(mesh.shape["row"], X_SIZE, Z_SIZE), ("row", "x", "z")
    )
    placed = (P(COL, "row"), P(None, "row", None, None), P(None, "row"), P(None, COL, "row"))
    return jax.shard_map(
        inner, mesh=finer, in_specs=placed, out_specs=P(COL, "row"), check_vma=False
    )
```

time: 2030 us -> 118 us (0.06)
  starting transfers between devices: 850 us -> 43.1 us
  matrix products: 416 us -> 0 us
  local copies, waits for them, and re-layouts: 375 us -> 3.91 us
  waiting for transfers between devices: 231 us -> 18.4 us
  other arithmetic: 101 us -> 0.08 us
  loops' own time: 38 us -> 0 us
  blocking collectives: 0 us -> 35.8 us
    ppermute x18 -> x2, starting transfers between devices: 569 us -> 6.66 us  [from_behind(): lax.ppermute(value, axis, [(source, source + steps) for source in range(f...]
    dot_general x566 -> x0, matrix products: 416 us -> none  [the longest x512 377 us: step(): partial_sum = jnp.dot(matrow, solution)]
    dynamic_slice x528 -> x0, local copies, waits for them, and re-layouts: 312 us -> none  [the longest x512 303 us: step(): pivot = lax.dynamic_index_in_dim(matrow, place, 0, keepdims=False)]
    all_to_all x4 -> x0, starting transfers between devices: 281 us -> none  [sent_to_all(): lax.all_to_all(jnp.broadcast_to(x[None], (peers, *x.shape)), axis, 0, 0,...]
    ppermute x18 -> x2, waiting for transfers between devices: 186 us -> 0.01 us  [from_behind(): lax.ppermute(value, axis, [(source, source + steps) for source in range(f...]
    div x16 -> x0, other arithmetic: 97.9 us -> none  [upper_solve(): solved[back_at] = value / matrix[back_at, back_at]]
    another operation x22 -> x0, loops' own time: 38 us -> none  [the longest x2 28.4 us: run_spans(): return lax.fori_loop(0, vectors.shape[0], advance, block)]
    ppermute x0 -> x24, starting transfers between devices: none -> 36.5 us  [shifted(): lax.ppermute(value, axis, [(at, (at + steps) % count) for at in range(cou...]
  transfers between devices with their start and end apart: 24 -> 26, of which waited for: 21 -> 9; matrix products, arithmetic and copies ran while one was open for 22% -> 0% of each run, Pallas kernels for 0% -> 3%
where the time goes in v2:
time: 118 us; the launch traced here: 117 us
  starting transfers between devices  43.1 us (37%)
  blocking collectives  35.8 us (30%)
  waiting for transfers between devices  18.4 us (16%)
  Pallas kernels  15.9 us (13%)
  local copies, waits for them, and re-layouts  3.91 us (3%)
    ppermute x24, starting transfers between devices, shifted(): lax.ppermute(value, axis, [(at, (at + steps) % count) for at in range(cou...  36.5 us
    all_to_all x2, blocking collectives, exchange(): return lax.all_to_all(pieces, axes, 0, 0, tiled=True)  35.8 us
    ppermute x24, waiting for transfers between devices, shifted(): lax.ppermute(value, axis, [(at, (at + steps) % count) for at in range(cou...  18.4 us
    pallas_call x7, Pallas kernels, call(): pl.pallas_call(kernel, out_shape=out_shape, in_specs=in_specs, out_specs=...  15.9 us
    ppermute x2, starting transfers between devices, from_behind(): lax.ppermute(value, axis, [(source, source + steps) for source in range(f...  6.66 us
    unnamed x16, local copies, waits for them, and re-layouts  3.88 us
  transfers between devices with their start and end apart: 26, of which 9 were waited for; matrix products, arithmetic and copies ran while one was open for 0% of the time, Pallas kernels for 3%

profile of v2, /device:TPU:1, one launch (start us, length us, event | category | flops | bytes accessed | tf_op | source)
XLA Modules:
  0.0 117.3 jit_solution(5578208024275351066)
XLA Ops:
  0.1 1.0 copy-done.2
  1.7 2.1 %collective-permute-start.2 = (bf16[16,3200]{1,0:T(8,128)(2,1)S(1)}, bf16[16,3200]{1,0:T(8,128)(2,1)S(1)}, u32[]{:S(2)}, u32[]{:S(2)}) collective-permute-start(bf16[16,3200]{1,0:T(8,128)(2,1)S(1)} %get-tuple-element.27), channel_id=1, source_target_pairs={{0,8},{8,16},{16,24},{24,0},{1,9},{9,17},{17,25},{25,1},{2,10},{10... | collective-permute-start | bytes 307208 | tf_op jit(solution)/shard_map/ppermute | solution.py:40
  3.8 1.4 %collective-permute-start.10 = (bf16[16,3200]{1,0:T(8,128)(2,1)S(1)}, bf16[16,3200]{1,0:T(8,128)(2,1)S(1)}, u32[]{:S(2)}, u32[]{:S(2)}) collective-permute-start(bf16[16,3200]{1,0:T(8,128)(2,1)S(1)} %get-tuple-element.28), channel_id=1, source_target_pairs={{0,24},{8,0},{16,8},{24,16},{1,25},{9,1},{17,9},{25,17},{2,26},{10... | collective-permute-start | bytes 307208 | tf_op jit(solution)/shard_map/ppermute | solution.py:40
  5.2 1.6 %collective-permute-start.11 = (bf16[16,3200]{1,0:T(8,128)(2,1)S(1)}, bf16[16,3200]{1,0:T(8,128)(2,1)S(1)}, u32[]{:S(2)}, u32[]{:S(2)}) collective-permute-start(bf16[16,3200]{1,0:T(8,128)(2,1)S(1)} %get-tuple-element.29), channel_id=1, source_target_pairs={{0,16},{8,24},{16,0},{24,8},{1,17},{9,25},{17,1},{25,9},{2,18},{10... | collective-permute-start | bytes 307208 | tf_op jit(solution)/shard_map/ppermute | solution.py:40
  6.8 1.4 %copy-done = f32[32,12544]{1,0:T(8,128)S(1)} copy-done((f32[32,12544]{1,0:T(8,128)S(1)}, f32[32,12544]{1,0:T(8,128)}, u32[]{:S(2)}) %copy-start) | copy-done | bytes 1605656
  8.2 0.8 copy-done.3
  9.8 3.6 %collective-permute-start.1 = (f32[32,1408]{1,0:T(8,128)S(1)}, f32[32,1408]{1,0:T(8,128)S(1)}, u32[]{:S(2)}, u32[]{:S(2)}) collective-permute-start(f32[32,1408]{1,0:T(8,128)S(1)} %get-tuple-element.24), channel_id=1, source_target_pairs={{32,0},{64,32},{96,64},{128,96},{160,128},{192,160},{224,192},{33,... | collective-permute-start | bytes 540680 | tf_op jit(solution)/shard_map/ppermute | solution.py:46
  13.3 3.1 %collective-permute-start = (f32[32,2432]{1,0:T(8,128)S(1)}, f32[32,2432]{1,0:T(8,128)S(1)}, u32[]{:S(2)}, u32[]{:S(2)}) collective-permute-start(f32[32,2432]{1,0:T(8,128)S(1)} %get-tuple-element.23), channel_id=1, source_target_pairs={{0,32},{32,64},{64,96},{96,128},{128,160},{160,192},{192,224},{1,3... | collective-permute-start | bytes 933896 | tf_op jit(solution)/shard_map/ppermute | solution.py:46
  16.5 5.7 %collective-permute-start.13 = (bf16[32,3200]{1,0:T(8,128)(2,1)S(1)}, bf16[32,3200]{1,0:T(8,128)(2,1)S(1)}, u32[]{:S(2)}, u32[]{:S(2)}) collective-permute-start(bf16[32,3200]{1,0:T(8,128)(2,1)S(1)} %constant_dynamic-update-slice_fusion.2.refs_8_), channel_id=1, source_target_pairs={{0,7},{1,0},{2,1},{3,2},{4,3},{5,4},{6,5},{7,6},{8,15},{9,8},{10,9... | collective-permute-start | bytes 614408 | tf_op jit(solution)/shard_map/ppermute | solution.py:40
  22.2 2.7 %collective-permute-start.4 = (bf16[32,3200]{1,0:T(8,128)(2,1)S(1)}, bf16[32,3200]{1,0:T(8,128)(2,1)S(1)}, u32[]{:S(2)}, u32[]{:S(2)}) collective-permute-start(bf16[32,3200]{1,0:T(8,128)(2,1)S(1)} %constant_dynamic-update-slice_fusion.refs_0_), channel_id=1, source_target_pairs={{0,7},{1,0},{2,1},{3,2},{4,3},{5,4},{6,5},{7,6},{8,15},{9,8},{10,9... | collective-permute-start | bytes 614408 | tf_op jit(solution)/shard_map/ppermute | solution.py:40
  25.0 2.1 %collective-permute-done.13.refs_10_ = bf16[32,3200]{1,0:T(8,128)(2,1)S(1)} collective-permute-done((bf16[32,3200]{1,0:T(8,128)(2,1)S(1)}, bf16[32,3200]{1,0:T(8,128)(2,1)S(1)}, u32[]{:S(2)}, u32[]{:S(2)}) %collective-permute-start.13) | collective-permute-done | bytes 204832 | tf_op jit(solution)/shard_map/ppermute | solution.py:40
  27.1 3.4 %collective-permute-start.15 = (bf16[32,3200]{1,0:T(8,128)(2,1)S(1)}, bf16[32,3200]{1,0:T(8,128)(2,1)S(1)}, u32[]{:S(2)}, u32[]{:S(2)}) collective-permute-start(bf16[32,3200]{1,0:T(8,128)(2,1)S(1)} %collective-permute-done.13.refs_10_), channel_id=1, source_target_pairs={{0,7},{1,0},{2,1},{3,2},{4,3},{5,4},{6,5},{7,6},{8,15},{9,8},{10,9... | collective-permute-start | bytes 614408 | tf_op jit(solution)/shard_map/ppermute | solution.py:40
  30.5 0.8 collective-permute-done.4.refs_2_
  31.3 3.2 %collective-permute-start.6 = (bf16[32,3200]{1,0:T(8,128)(2,1)S(1)}, bf16[32,3200]{1,0:T(8,128)(2,1)S(1)}, u32[]{:S(2)}, u32[]{:S(2)}) collective-permute-start(bf16[32,3200]{1,0:T(8,128)(2,1)S(1)} %collective-permute-done.4.refs_2_), channel_id=1, source_target_pairs={{0,7},{1,0},{2,1},{3,2},{4,3},{5,4},{6,5},{7,6},{8,15},{9,8},{10,9... | collective-permute-start | bytes 614408 | tf_op jit(solution)/shard_map/ppermute | solution.py:40
  34.8 3.7 %shard_map.47 = (f32[32,12544]{1,0:T(8,128)S(1)}, bf16[32,3200]{1,0:T(8,128)(2,1)S(1)}, bf16[32,3200]{1,0:T(8,128)(2,1)S(1)}, bf16[32,3200]{1,0:T(8,128)(2,1)S(1)}, bf16[32,3200]{1,0:T(8,128)(2,1)S(1)}) custom-call(s32[4]{0:T(128)S(1)} %pad_add_fusion.place_ref, s32[2,8]{1,0:T(2,128)S(1)} %copy-done.6, s32[2,8]{1,0:T(2,128)S(1)} %slice_convert_fusion.1.upper_offsets_ref, ...), custom_call_target="tpu_custom_call" | custom-call | flops 16056320 | bytes 4816896 | tf_op jit(solution)/shard_map/pallas_call | solution.py:27
  38.9 2.4 %collective-permute-start.20 = (bf16[32,3200]{1,0:T(8,128)(2,1)S(1)}, bf16[32,3200]{1,0:T(8,128)(2,1)S(1)}, u32[]{:S(2)}, u32[]{:S(2)}) collective-permute-start(bf16[32,3200]{1,0:T(8,128)(2,1)S(1)} %get-tuple-element.32), channel_id=1, source_target_pairs={{0,24},{8,0},{16,8},{24,16},{1,25},{9,1},{17,9},{25,17},{2,26},{10... | collective-permute-start | bytes 614408 | tf_op jit(solution)/shard_map/ppermute | solution.py:40
  41.3 2.7 %collective-permute-start.17 = (bf16[32,3200]{1,0:T(8,128)(2,1)S(1)}, bf16[32,3200]{1,0:T(8,128)(2,1)S(1)}, u32[]{:S(2)}, u32[]{:S(2)}) collective-permute-start(bf16[32,3200]{1,0:T(8,128)(2,1)S(1)} %collective-permute-done.15.refs_12_), channel_id=1, source_target_pairs={{0,7},{1,0},{2,1},{3,2},{4,3},{5,4},{6,5},{7,6},{8,15},{9,8},{10,9... | collective-permute-start | bytes 614408 | tf_op jit(solution)/shard_map/ppermute | solution.py:40
  43.9 0.7 collective-permute-start.21
  44.6 1.4 %collective-permute-done.19.refs_17_ = bf16[32,3200]{1,0:T(8,128)(2,1)S(1)} collective-permute-done((bf16[32,3200]{1,0:T(8,128)(2,1)S(1)}, bf16[32,3200]{1,0:T(8,128)(2,1)S(1)}, u32[]{:S(2)}, u32[]{:S(2)}) %collective-permute-start.19) | collective-permute-done | bytes 204832 | tf_op jit(solution)/shard_map/ppermute | solution.py:40
  46.1 2.7 %collective-permute-start.8 = (bf16[32,3200]{1,0:T(8,128)(2,1)S(1)}, bf16[32,3200]{1,0:T(8,128)(2,1)S(1)}, u32[]{:S(2)}, u32[]{:S(2)}) collective-permute-start(bf16[32,3200]{1,0:T(8,128)(2,1)S(1)} %collective-permute-done.6.refs_4_), channel_id=1, source_target_pairs={{0,7},{1,0},{2,1},{3,2},{4,3},{5,4},{6,5},{7,6},{8,15},{9,8},{10,9... | collective-permute-start | bytes 614408 | tf_op jit(solution)/shard_map/ppermute | solution.py:40
  48.8 1.8 %collective-permute-start.18 = (bf16[32,3200]{1,0:T(8,128)(2,1)S(1)}, bf16[32,3200]{1,0:T(8,128)(2,1)S(1)}, u32[]{:S(2)}, u32[]{:S(2)}) collective-permute-start(bf16[32,3200]{1,0:T(8,128)(2,1)S(1)} %collective-permute-done.17.refs_14_), channel_id=1, source_target_pairs={{0,7},{1,0},{2,1},{3,2},{4,3},{5,4},{6,5},{7,6},{8,15},{9,8},{10,9... | collective-permute-start | bytes 614408 | tf_op jit(solution)/shard_map/ppermute | solution.py:40
  50.7 4.0 %collective-permute-done.16.refs_13_ = bf16[32,3200]{1,0:T(8,128)(2,1)S(1)} collective-permute-done((bf16[32,3200]{1,0:T(8,128)(2,1)S(1)}, bf16[32,3200]{1,0:T(8,128)(2,1)S(1)}, u32[]{:S(2)}, u32[]{:S(2)}) %collective-permute-start.16) | collective-permute-done | bytes 204832 | tf_op jit(solution)/shard_map/ppermute | solution.py:40
  54.7 3.9 %collective-permute-done.9.refs_7_ = bf16[32,3200]{1,0:T(8,128)(2,1)S(1)} collective-permute-done((bf16[32,3200]{1,0:T(8,128)(2,1)S(1)}, bf16[32,3200]{1,0:T(8,128)(2,1)S(1)}, u32[]{:S(2)}, u32[]{:S(2)}) %collective-permute-start.9) | collective-permute-done | bytes 204832 | tf_op jit(solution)/shard_map/ppermute | solution.py:40
  58.6 3.2 %shard_map.49 = (bf16[512,3200]{1,0:T(8,128)(2,1)S(1)}, bf16[1792,128]{1,0:T(8,128)(2,1)S(1)}) custom-call(s32[4]{0:T(128)S(1)} %pad_add_fusion.place_ref, bf16[32,3200]{1,0:T(8,128)(2,1)S(1)} %constant_dynamic-update-slice_fusion.refs_0_, bf16[32,3200]{1,0:T(8,128)(2,1)S(1)} %collective-permute-done.3.refs_1_, ...), custom_call_target="tpu_custom_call" | custom-call | flops 2097152000 | bytes 9830400 | tf_op jit(solution)/shard_map/pallas_call | solution.py:27
  61.8 20.9 %all_to_all.10.parts_ref = bf16[32,56,128]{2,1,0:T(8,128)(2,1)S(1)} all-to-all(bf16[32,56,128]{2,1,0:T(8,128)(2,1)S(1)} %bitcast.6), channel_id=1, replica_groups=mesh['row'=8,'x'=4,'z'=8] {'row','x'}, dimensions={0} | all-to-all | bytes 917504 | tf_op jit(solution)/shard_map/all_to_all | solution.py:454
  82.8 14.8 %all_to_all.11 = bf16[32,56,128]{2,1,0:T(8,128)(2,1)S(1)} all-to-all(bf16[32,56,128]{2,1,0:T(8,128)(2,1)S(1)} %shard_map.50), channel_id=1, replica_groups=mesh['row'=8,'x'=4,'z'=8] {'row','x'}, dimensions={0} | all-to-all | bytes 917504 | tf_op jit(solution)/shard_map/all_to_all | solution.py:454
  97.6 6.3 %shard_map.51 = (bf16[32,3200]{1,0:T(8,128)(2,1)S(1)}, bf16[32,3200]{1,0:T(8,128)(2,1)S(1)}, bf16[32,3200]{1,0:T(8,128)(2,1)S(1)}, bf16[16,3200]{1,0:T(8,128)(2,1)S(1)}, bf16[16,3200]{1,0:T(8,128)(2,1)S(1)}) custom-call(s32[4]{0:T(128)S(1)} %pad_add_fusion.place_ref, bf16[1792,128]{1,0:T(8,128)(2,1)S(1)} %bitcast.5, ...), custom_call_target="tpu_custom_call" | custom-call | flops 419430400 | bytes 6553600 | tf_op jit(solution)/shard_map/pallas_call | solution.py:27
  104.3 2.4 %collective-permute-start.23 = (bf16[32,3200]{1,0:T(8,128)(2,1)S(1)}, bf16[32,3200]{1,0:T(8,128)(2,1)S(1)}, u32[]{:S(2)}, u32[]{:S(2)}) collective-permute-start(bf16[32,3200]{1,0:T(8,128)(2,1)S(1)} %get-tuple-element.38), channel_id=1, source_target_pairs={{0,24},{8,0},{16,8},{24,16},{1,25},{9,1},{17,9},{25,17},{2,26},{10... | collective-permute-start | bytes 614408 | tf_op jit(solution)/shard_map/ppermute | solution.py:40
  106.7 3.0 %collective-permute-start.25 = (bf16[16,3200]{1,0:T(8,128)(2,1)S(1)}, bf16[16,3200]{1,0:T(8,128)(2,1)S(1)}, u32[]{:S(2)}, u32[]{:S(2)}) collective-permute-start(bf16[16,3200]{1,0:T(8,128)(2,1)S(1)} %get-tuple-element.40), channel_id=1, source_target_pairs={{0,16},{8,24},{16,0},{24,8},{1,17},{9,25},{17,1},{25,9},{2,18},{10... | collective-permute-start | bytes 307208 | tf_op jit(solution)/shard_map/ppermute | solution.py:40
  109.6 3.4 %collective-permute-done.24.half0 = bf16[16,3200]{1,0:T(8,128)(2,1)S(1)} collective-permute-done((bf16[16,3200]{1,0:T(8,128)(2,1)S(1)}, bf16[16,3200]{1,0:T(8,128)(2,1)S(1)}, u32[]{:S(2)}, u32[]{:S(2)}) %collective-permute-start.24) | collective-permute-done | bytes 102432 | tf_op jit(solution)/shard_map/ppermute | solution.py:40
  113.1 2.2 %collective-permute-done.25.half1 = bf16[16,3200]{1,0:T(8,128)(2,1)S(1)} collective-permute-done((bf16[16,3200]{1,0:T(8,128)(2,1)S(1)}, bf16[16,3200]{1,0:T(8,128)(2,1)S(1)}, u32[]{:S(2)}, u32[]{:S(2)}) %collective-permute-start.25) | collective-permute-done | bytes 102432 | tf_op jit(solution)/shard_map/ppermute | solution.py:40
  115.3 2.0 %shard_map.52 = f32[32,12544]{1,0:T(8,128)} custom-call(s32[4]{0:T(128)S(1)} %pad_add_fusion.place_ref, f32[32,12544]{1,0:T(8,128)S(1)} %get-tuple-element.25.eigen_ref, bf16[32,3200]{1,0:T(8,128)(2,1)S(1)} %get-tuple-element.36.mine, bf16[32,3200]{1,0:T(8,128)(2,1)S(1)} %collective-permute-done.22.one, bf16[32,3200]{1,0:T(8,128)(2,1)S(1)} %collective-permute-done.23.two, ...), custom_call_target="tpu_custom_call" | custom-call | flops 401408 | bytes 4014080 | tf_op jit(solution)/shard_map/pallas_call | solution.py:27
  (50 shorter events, 2.9 us)
Async XLA Ops:
  0.0 34.8 %copy-start.6 = (s32[2,8]{1,0:T(2,128)S(1)}, s32[2,8]{1,0:T(2,128)}, u32[]{:S(2)}) copy-start(s32[2,8]{1,0:T(2,128)} %offsets_ref.3) | copy-start | bytes 196
  0.1 1.0 copy-start.2
  1.1 33.7 %copy-start.4 = (f32[2,8,4,128]{3,2,1,0:T(4,128)S(1)}, f32[2,8,4,128]{3,2,1,0:T(4,128)}, u32[]{:S(2)}) copy-start(f32[2,8,4,128]{3,2,1,0:T(4,128)} %vectors_ref.3) | copy-start | bytes 98308
  1.7 20.5 %collective-permute-start.2 = (bf16[16,3200]{1,0:T(8,128)(2,1)S(1)}, bf16[16,3200]{1,0:T(8,128)(2,1)S(1)}, u32[]{:S(2)}, u32[]{:S(2)}) collective-permute-start(bf16[16,3200]{1,0:T(8,128)(2,1)S(1)} %get-tuple-element.27), channel_id=1, source_target_pairs={{0,8},{8,16},{16,24},{24,0},{1,9},{9,17},{17,25},{25,1},{2,10},{10... | collective-permute-start | bytes 307208 | tf_op jit(solution)/shard_map/ppermute | solution.py:40
  3.8 12.7 %collective-permute-start.10 = (bf16[16,3200]{1,0:T(8,128)(2,1)S(1)}, bf16[16,3200]{1,0:T(8,128)(2,1)S(1)}, u32[]{:S(2)}, u32[]{:S(2)}) collective-permute-start(bf16[16,3200]{1,0:T(8,128)(2,1)S(1)} %get-tuple-element.28), channel_id=1, source_target_pairs={{0,24},{8,0},{16,8},{24,16},{1,25},{9,1},{17,9},{25,17},{2,26},{10... | collective-permute-start | bytes 307208 | tf_op jit(solution)/shard_map/ppermute | solution.py:40
  5.2 11.3 %collective-permute-start.11 = (bf16[16,3200]{1,0:T(8,128)(2,1)S(1)}, bf16[16,3200]{1,0:T(8,128)(2,1)S(1)}, u32[]{:S(2)}, u32[]{:S(2)}) collective-permute-start(bf16[16,3200]{1,0:T(8,128)(2,1)S(1)} %get-tuple-element.29), channel_id=1, source_target_pairs={{0,16},{8,24},{16,0},{24,8},{1,17},{9,25},{17,1},{25,9},{2,18},{10... | collective-permute-start | bytes 307208 | tf_op jit(solution)/shard_map/ppermute | solution.py:40
  6.8 1.4 %copy-start = (f32[32,12544]{1,0:T(8,128)S(1)}, f32[32,12544]{1,0:T(8,128)}, u32[]{:S(2)}) copy-start(f32[32,12544]{1,0:T(8,128)} %own_ref.1) | copy-start | bytes 4816900
  8.2 0.8 copy-start.3
  9.6 25.2 %copy-start.1 = (f32[32,12544]{1,0:T(8,128)S(1)}, f32[32,12544]{1,0:T(8,128)}, u32[]{:S(2)}) copy-start(f32[32,12544]{1,0:T(8,128)} %own_ref.1) | copy-start | bytes 4816900
  9.8 15.2 %collective-permute-start.1 = (f32[32,1408]{1,0:T(8,128)S(1)}, f32[32,1408]{1,0:T(8,128)S(1)}, u32[]{:S(2)}, u32[]{:S(2)}) collective-permute-start(f32[32,1408]{1,0:T(8,128)S(1)} %get-tuple-element.24), channel_id=1, source_target_pairs={{32,0},{64,32},{96,64},{128,96},{160,128},{192,160},{224,192},{33,... | collective-permute-start | bytes 540680 | tf_op jit(solution)/shard_map/ppermute | solution.py:46
  13.3 21.5 %collective-permute-start = (f32[32,2432]{1,0:T(8,128)S(1)}, f32[32,2432]{1,0:T(8,128)S(1)}, u32[]{:S(2)}, u32[]{:S(2)}) collective-permute-start(f32[32,2432]{1,0:T(8,128)S(1)} %get-tuple-element.23), channel_id=1, source_target_pairs={{0,32},{32,64},{64,96},{96,128},{128,160},{160,192},{192,224},{1,3... | collective-permute-start | bytes 933896 | tf_op jit(solution)/shard_map/ppermute | solution.py:46
  16.5 10.5 %collective-permute-start.13 = (bf16[32,3200]{1,0:T(8,128)(2,1)S(1)}, bf16[32,3200]{1,0:T(8,128)(2,1)S(1)}, u32[]{:S(2)}, u32[]{:S(2)}) collective-permute-start(bf16[32,3200]{1,0:T(8,128)(2,1)S(1)} %constant_dynamic-update-slice_fusion.2.refs_8_), channel_id=1, source_target_pairs={{0,7},{1,0},{2,1},{3,2},{4,3},{5,4},{6,5},{7,6},{8,15},{9,8},{10,9... | collective-permute-start | bytes 614408 | tf_op jit(solution)/shard_map/ppermute | solution.py:40
  22.2 8.3 %collective-permute-start.12 = (bf16[32,3200]{1,0:T(8,128)(2,1)S(1)}, bf16[32,3200]{1,0:T(8,128)(2,1)S(1)}, u32[]{:S(2)}, u32[]{:S(2)}) collective-permute-start(bf16[32,3200]{1,0:T(8,128)(2,1)S(1)} %constant_dynamic-update-slice_fusion.2.refs_8_), channel_id=1, source_target_pairs={{0,1},{1,2},{2,3},{3,4},{4,5},{5,6},{6,7},{7,0},{8,9},{9,10},{10,1... | collective-permute-start | bytes 614408 | tf_op jit(solution)/shard_map/ppermute | solution.py:40
  22.2 9.1 %collective-permute-start.4 = (bf16[32,3200]{1,0:T(8,128)(2,1)S(1)}, bf16[32,3200]{1,0:T(8,128)(2,1)S(1)}, u32[]{:S(2)}, u32[]{:S(2)}) collective-permute-start(bf16[32,3200]{1,0:T(8,128)(2,1)S(1)} %constant_dynamic-update-slice_fusion.refs_0_), channel_id=1, source_target_pairs={{0,7},{1,0},{2,1},{3,2},{4,3},{5,4},{6,5},{7,6},{8,15},{9,8},{10,9... | collective-permute-start | bytes 614408 | tf_op jit(solution)/shard_map/ppermute | solution.py:40
  24.9 9.9 %collective-permute-start.3 = (bf16[32,3200]{1,0:T(8,128)(2,1)S(1)}, bf16[32,3200]{1,0:T(8,128)(2,1)S(1)}, u32[]{:S(2)}, u32[]{:S(2)}) collective-permute-start(bf16[32,3200]{1,0:T(8,128)(2,1)S(1)} %constant_dynamic-update-slice_fusion.refs_0_), channel_id=1, source_target_pairs={{0,1},{1,2},{2,3},{3,4},{4,5},{5,6},{6,7},{7,0},{8,9},{9,10},{10,1... | collective-permute-start | bytes 614408 | tf_op jit(solution)/shard_map/ppermute | solution.py:40
  27.1 11.8 %collective-permute-start.15 = (bf16[32,3200]{1,0:T(8,128)(2,1)S(1)}, bf16[32,3200]{1,0:T(8,128)(2,1)S(1)}, u32[]{:S(2)}, u32[]{:S(2)}) collective-permute-start(bf16[32,3200]{1,0:T(8,128)(2,1)S(1)} %collective-permute-done.13.refs_10_), channel_id=1, source_target_pairs={{0,7},{1,0},{2,1},{3,2},{4,3},{5,4},{6,5},{7,6},{8,15},{9,8},{10,9... | collective-permute-start | bytes 614408 | tf_op jit(solution)/shard_map/ppermute | solution.py:40
  30.5 10.8 %collective-permute-start.14 = (bf16[32,3200]{1,0:T(8,128)(2,1)S(1)}, bf16[32,3200]{1,0:T(8,128)(2,1)S(1)}, u32[]{:S(2)}, u32[]{:S(2)}) collective-permute-start(bf16[32,3200]{1,0:T(8,128)(2,1)S(1)} %collective-permute-done.12.refs_9_), channel_id=1, source_target_pairs={{0,1},{1,2},{2,3},{3,4},{4,5},{5,6},{6,7},{7,0},{8,9},{9,10},{10,1... | collective-permute-start | bytes 614408 | tf_op jit(solution)/shard_map/ppermute | solution.py:40
  31.3 12.7 %collective-permute-start.6 = (bf16[32,3200]{1,0:T(8,128)(2,1)S(1)}, bf16[32,3200]{1,0:T(8,128)(2,1)S(1)}, u32[]{:S(2)}, u32[]{:S(2)}) collective-permute-start(bf16[32,3200]{1,0:T(8,128)(2,1)S(1)} %collective-permute-done.4.refs_2_), channel_id=1, source_target_pairs={{0,7},{1,0},{2,1},{3,2},{4,3},{5,4},{6,5},{7,6},{8,15},{9,8},{10,9... | collective-permute-start | bytes 614408 | tf_op jit(solution)/shard_map/ppermute | solution.py:40
  34.8 9.1 %collective-permute-start.5 = (bf16[32,3200]{1,0:T(8,128)(2,1)S(1)}, bf16[32,3200]{1,0:T(8,128)(2,1)S(1)}, u32[]{:S(2)}, u32[]{:S(2)}) collective-permute-start(bf16[32,3200]{1,0:T(8,128)(2,1)S(1)} %collective-permute-done.3.refs_1_), channel_id=1, source_target_pairs={{0,1},{1,2},{2,3},{3,4},{4,5},{5,6},{6,7},{7,0},{8,9},{9,10},{10,1... | collective-permute-start | bytes 614408 | tf_op jit(solution)/shard_map/ppermute | solution.py:40
  38.5 7.6 %collective-permute-start.19 = (bf16[32,3200]{1,0:T(8,128)(2,1)S(1)}, bf16[32,3200]{1,0:T(8,128)(2,1)S(1)}, u32[]{:S(2)}, u32[]{:S(2)}) collective-permute-start(bf16[32,3200]{1,0:T(8,128)(2,1)S(1)} %get-tuple-element.31), channel_id=1, source_target_pairs={{0,8},{8,16},{16,24},{24,0},{1,9},{9,17},{17,25},{25,1},{2,10},{10... | collective-permute-start | bytes 614408 | tf_op jit(solution)/shard_map/ppermute | solution.py:40
  38.9 7.2 %collective-permute-start.20 = (bf16[32,3200]{1,0:T(8,128)(2,1)S(1)}, bf16[32,3200]{1,0:T(8,128)(2,1)S(1)}, u32[]{:S(2)}, u32[]{:S(2)}) collective-permute-start(bf16[32,3200]{1,0:T(8,128)(2,1)S(1)} %get-tuple-element.32), channel_id=1, source_target_pairs={{0,24},{8,0},{16,8},{24,16},{1,25},{9,1},{17,9},{25,17},{2,26},{10... | collective-permute-start | bytes 614408 | tf_op jit(solution)/shard_map/ppermute | solution.py:40
  41.3 7.5 %collective-permute-start.17 = (bf16[32,3200]{1,0:T(8,128)(2,1)S(1)}, bf16[32,3200]{1,0:T(8,128)(2,1)S(1)}, u32[]{:S(2)}, u32[]{:S(2)}) collective-permute-start(bf16[32,3200]{1,0:T(8,128)(2,1)S(1)} %collective-permute-done.15.refs_12_), channel_id=1, source_target_pairs={{0,7},{1,0},{2,1},{3,2},{4,3},{5,4},{6,5},{7,6},{8,15},{9,8},{10,9... | collective-permute-start | bytes 614408 | tf_op jit(solution)/shard_map/ppermute | solution.py:40
  43.9 6.6 %collective-permute-start.7 = (bf16[32,3200]{1,0:T(8,128)(2,1)S(1)}, bf16[32,3200]{1,0:T(8,128)(2,1)S(1)}, u32[]{:S(2)}, u32[]{:S(2)}) collective-permute-start(bf16[32,3200]{1,0:T(8,128)(2,1)S(1)} %collective-permute-done.5.refs_3_), channel_id=1, source_target_pairs={{0,1},{1,2},{2,3},{3,4},{4,5},{5,6},{6,7},{7,0},{8,9},{9,10},{10,1... | collective-permute-start | bytes 614408 | tf_op jit(solution)/shard_map/ppermute | solution.py:40
  43.9 6.7 %collective-permute-start.21 = (bf16[32,3200]{1,0:T(8,128)(2,1)S(1)}, bf16[32,3200]{1,0:T(8,128)(2,1)S(1)}, u32[]{:S(2)}, u32[]{:S(2)}) collective-permute-start(bf16[32,3200]{1,0:T(8,128)(2,1)S(1)} %get-tuple-element.33), channel_id=1, source_target_pairs={{0,16},{8,24},{16,0},{24,8},{1,17},{9,25},{17,1},{25,9},{2,18},{10... | collective-permute-start | bytes 614408 | tf_op jit(solution)/shard_map/ppermute | solution.py:40
  46.1 8.6 %collective-permute-start.16 = (bf16[32,3200]{1,0:T(8,128)(2,1)S(1)}, bf16[32,3200]{1,0:T(8,128)(2,1)S(1)}, u32[]{:S(2)}, u32[]{:S(2)}) collective-permute-start(bf16[32,3200]{1,0:T(8,128)(2,1)S(1)} %collective-permute-done.14.refs_11_), channel_id=1, source_target_pairs={{0,1},{1,2},{2,3},{3,4},{4,5},{5,6},{6,7},{7,0},{8,9},{9,10},{10,1... | collective-permute-start | bytes 614408 | tf_op jit(solution)/shard_map/ppermute | solution.py:40
  46.1 8.6 %collective-permute-start.8 = (bf16[32,3200]{1,0:T(8,128)(2,1)S(1)}, bf16[32,3200]{1,0:T(8,128)(2,1)S(1)}, u32[]{:S(2)}, u32[]{:S(2)}) collective-permute-start(bf16[32,3200]{1,0:T(8,128)(2,1)S(1)} %collective-permute-done.6.refs_4_), channel_id=1, source_target_pairs={{0,7},{1,0},{2,1},{3,2},{4,3},{5,4},{6,5},{7,6},{8,15},{9,8},{10,9... | collective-permute-start | bytes 614408 | tf_op jit(solution)/shard_map/ppermute | solution.py:40
  48.8 5.9 %collective-permute-start.18 = (bf16[32,3200]{1,0:T(8,128)(2,1)S(1)}, bf16[32,3200]{1,0:T(8,128)(2,1)S(1)}, u32[]{:S(2)}, u32[]{:S(2)}) collective-permute-start(bf16[32,3200]{1,0:T(8,128)(2,1)S(1)} %collective-permute-done.17.refs_14_), channel_id=1, source_target_pairs={{0,7},{1,0},{2,1},{3,2},{4,3},{5,4},{6,5},{7,6},{8,15},{9,8},{10,9... | collective-permute-start | bytes 614408 | tf_op jit(solution)/shard_map/ppermute | solution.py:40
  50.6 8.0 %collective-permute-start.9 = (bf16[32,3200]{1,0:T(8,128)(2,1)S(1)}, bf16[32,3200]{1,0:T(8,128)(2,1)S(1)}, u32[]{:S(2)}, u32[]{:S(2)}) collective-permute-start(bf16[32,3200]{1,0:T(8,128)(2,1)S(1)} %collective-permute-done.7.refs_5_), channel_id=1, source_target_pairs={{0,1},{1,2},{2,3},{3,4},{4,5},{5,6},{6,7},{7,0},{8,9},{9,10},{10,1... | collective-permute-start | bytes 614408 | tf_op jit(solution)/shard_map/ppermute | solution.py:40
  103.9 11.4 %collective-permute-start.22 = (bf16[32,3200]{1,0:T(8,128)(2,1)S(1)}, bf16[32,3200]{1,0:T(8,128)(2,1)S(1)}, u32[]{:S(2)}, u32[]{:S(2)}) collective-permute-start(bf16[32,3200]{1,0:T(8,128)(2,1)S(1)} %get-tuple-element.37), channel_id=1, source_target_pairs={{0,8},{8,16},{16,24},{24,0},{1,9},{9,17},{17,25},{25,1},{2,10},{10... | collective-permute-start | bytes 614408 | tf_op jit(solution)/shard_map/ppermute | solution.py:40
  104.3 11.0 %collective-permute-start.23 = (bf16[32,3200]{1,0:T(8,128)(2,1)S(1)}, bf16[32,3200]{1,0:T(8,128)(2,1)S(1)}, u32[]{:S(2)}, u32[]{:S(2)}) collective-permute-start(bf16[32,3200]{1,0:T(8,128)(2,1)S(1)} %get-tuple-element.38), channel_id=1, source_target_pairs={{0,24},{8,0},{16,8},{24,16},{1,25},{9,1},{17,9},{25,17},{2,26},{10... | collective-permute-start | bytes 614408 | tf_op jit(solution)/shard_map/ppermute | solution.py:40
  106.7 6.4 %collective-permute-start.24 = (bf16[16,3200]{1,0:T(8,128)(2,1)S(1)}, bf16[16,3200]{1,0:T(8,128)(2,1)S(1)}, u32[]{:S(2)}, u32[]{:S(2)}) collective-permute-start(bf16[16,3200]{1,0:T(8,128)(2,1)S(1)} %get-tuple-element.39), channel_id=1, source_target_pairs={{0,16},{8,24},{16,0},{24,8},{1,17},{9,25},{17,1},{25,9},{2,18},{10... | collective-permute-start | bytes 307208 | tf_op jit(solution)/shard_map/ppermute | solution.py:40
  106.7 8.6 %collective-permute-start.25 = (bf16[16,3200]{1,0:T(8,128)(2,1)S(1)}, bf16[16,3200]{1,0:T(8,128)(2,1)S(1)}, u32[]{:S(2)}, u32[]{:S(2)}) collective-permute-start(bf16[16,3200]{1,0:T(8,128)(2,1)S(1)} %get-tuple-element.40), channel_id=1, source_target_pairs={{0,16},{8,24},{16,0},{24,8},{1,17},{9,25},{17,1},{25,9},{2,18},{10... | collective-permute-start | bytes 307208 | tf_op jit(solution)/shard_map/ppermute | solution.py:40
  (1 other events, 0.7 us)

commit v3 on v2

--- a/solution.py
+++ b/solution.py
@@ -12,6 +12,7 @@
 COL = ("x", "z")
 X_SIZE, Z_SIZE = 4, 8
 LANE = 128
+FRONT_MB = 60
 UNIT = 8
 F32 = jnp.float32
 BF16 = jnp.bfloat16
@@ -79,19 +80,33 @@
     state_ref[:, pl.ds(base, pair.shape[1])] = update
 
 
-def halo_kernel(offsets_ref, vectors_ref, eigen_ref, down_ref, up_ref, sems):
+def front_kernel(
+    offsets_ref, vectors_ref, panels_ref, eigen_ref, *refs
+):
+    down_ref, up_ref, wide_ref, sems = refs[-4:]
     sweeps, spans, refl, band = vectors_ref.shape
     rows, columns = eigen_ref.shape
-    copies = []
-    for at, (ref, begin, count) in enumerate(((down_ref, None, sweeps), (up_ref, 0, sweeps - 1))):
+    panels, own, _ = panels_ref.shape
+    moves = [
+        pltpu.make_async_copy(
+            panels_ref.at[p], wide_ref.at[p * own : (p + 1) * own, 0:columns], sems.at[p]
+        )
+        for p in range(panels)
+    ]
+    halos = ((down_ref, None, sweeps), (up_ref, 0, sweeps - 1))
+    for ref, begin, count in halos:
         width = ref.shape[1] - count * band - LANE
         begin = columns - width if begin is None else begin
-        copies.append(
+        moves.append(
             pltpu.make_async_copy(
-                eigen_ref.at[:, begin : begin + width], ref.at[:, 0:width], sems.at[at]
+                eigen_ref.at[:, begin : begin + width], ref.at[:, 0:width], sems.at[len(moves)]
             )
         )
-        copies[-1].start()
+    for move in moves:
+        move.start()
+    wide_ref[:, columns:] = jnp.zeros((panels * own, wide_ref.shape[1] - columns), BF16)
+    for ref, _, count in halos:
+        width = ref.shape[1] - count * band - LANE
         for sweep in range(count):
             for i in range(refl):
                 ref[i * spans : (i + 1) * spans, width + sweep * band : width + (sweep + 1) * band] = (
@@ -99,12 +114,42 @@
                 )
         ref[:, width + count * band :] = jnp.zeros((rows, LANE), F32)
         ref[0:sweeps, width + count * band : width + count * band + spans] = offsets_ref[...].astype(F32)
-    for copy in copies:
-        copy.wait()
+    for move in moves[:panels]:
+        move.wait()
+    for step, ref in zip((0, *PEERS), refs):
+        cut = ref.shape[1]
+        at = pl.multiple_of((lax.axis_index("x") + step) % X_SIZE * cut, LANE)
+        ref[...] = wide_ref[:, pl.ds(at, cut)]
+    for move in moves[panels:]:
+        move.wait()
+
+
+def halo_sizes(vectors):
+    sweeps, spans, _, band = vectors.shape
+    return sweeps * spans * band, ((sweeps - 1) * spans + 1) * band
+
+
+def front(eigen, vectors, offsets, panels, cut):
+    sweeps, _, _, band = vectors.shape
+    rows = eigen.shape[0]
+    left, right = halo_sizes(vectors)
+    wide = lambda width: jax.ShapeDtypeStruct((rows, width), F32)
+    high = panels.shape[0] * panels.shape[1]
+    return call(
+        front_kernel,
+        [jax.ShapeDtypeStruct((high, cut), BF16)] * 4
+        + [wide(left + sweeps * band + LANE), wide(right + (sweeps - 1) * band + LANE)],
+        [VM, VM, ANY, ANY],
+        (offsets, vectors, panels, eigen),
+        [pltpu.VMEM((high, X_SIZE * cut), BF16), pltpu.SemaphoreType.DMA((panels.shape[0] + 2,))],
+        flops=panels.size,
+        size=4 * panels.size,
+        vmem=FRONT_MB,
+    )
 
 
 def sweep_kernel(
-    place_ref, offsets_ref, upper_offsets_ref, lower_offsets_ref,
+    offsets_ref, upper_offsets_ref, lower_offsets_ref,
     vectors_ref, own_ref, upper_ref, lower_ref,
     out_ref, mine_ref, next_ref, last_ref, far_ref,
     state_ref, pairs_ref, rounded_ref,
@@ -116,8 +161,8 @@
     state_ref[:, 0:left] = upper_ref[:, 0:left]
     state_ref[:, left : left + columns] = own_ref[...]
     state_ref[:, left + columns :] = lower_ref[:, 0:right]
-    first = place_ref[0] == 0
-    final = place_ref[0] == place_ref[1] - 1
+    first = lax.axis_index("row") == 0
+    final = lax.axis_index("row") == lax.axis_size("row") - 1
 
     def beside(ref, width, sweep, i):
         return ref[i * spans : (i + 1) * spans, width + sweep * band : width + (sweep + 1) * band]
@@ -158,26 +203,15 @@
     rounded_ref[:, columns:] = jnp.zeros((rows, padded - columns), BF16)
     cut = mine_ref.shape[1]
     for step, ref in ((0, mine_ref), (PEERS[0], next_ref), (PEERS[1], last_ref), (PEERS[2], far_ref)):
-        at = pl.multiple_of((place_ref[2] + step) % X_SIZE * cut, LANE)
+        at = pl.multiple_of((lax.axis_index("x") + step) % X_SIZE * cut, LANE)
         ref[...] = rounded_ref[:, pl.ds(at, cut)]
 
 
-def sweep_all(place, eigen, vectors, offsets, cut):
+def sweep_all(eigen, vectors, offsets, down, up, cut):
     sweeps, spans, refl, band = vectors.shape
     rows, columns = eigen.shape
-    left, right = sweeps * spans * band, ((sweeps - 1) * spans + 1) * band
+    left, right = halo_sizes(vectors)
     assert left + right + band < columns and spans * refl == rows
-    wide = lambda width: jax.ShapeDtypeStruct((rows, width), F32)
-    down, up = call(
-        halo_kernel,
-        [wide(left + sweeps * band + LANE), wide(right + (sweeps - 1) * band + LANE)],
-        [VM, VM, ANY],
-        (offsets, vectors, eigen),
-        [pltpu.SemaphoreType.DMA((2,))],
-        flops=eigen.size,
-        size=4 * eigen.size,
-        vmem=8,
-    )
     upper = from_behind(down, "row", 1)
     lower = from_behind(up, "row", -1)
     upper_offsets = upper[0:sweeps, -LANE : spans - LANE].astype(jnp.int32)
@@ -186,8 +220,8 @@
         sweep_kernel,
         [jax.ShapeDtypeStruct(eigen.shape, F32)]
         + [jax.ShapeDtypeStruct((rows, cut), BF16)] * 4,
-        [SM] * 4 + [VM] * 4,
-        (place, offsets, upper_offsets, lower_offsets, vectors, eigen, upper, lower),
+        [SM] * 3 + [VM] * 4,
+        (offsets, upper_offsets, lower_offsets, vectors, eigen, upper, lower),
         [
             pltpu.VMEM((rows, left + columns + right), F32),
             pltpu.VMEM((3 * sweeps, spans, 2 * refl, 2 * band), F32),
@@ -196,32 +230,6 @@
         flops=40 * eigen.size,
         size=12 * eigen.size,
         vmem=14,
-    )
-
-
-def pack_kernel(place_ref, panels_ref, *refs):
-    wide_ref = refs[-1]
-    panels, own, columns = panels_ref.shape
-    for p in range(panels):
-        wide_ref[p * own : (p + 1) * own, 0:columns] = panels_ref[p]
-    wide_ref[:, columns:] = jnp.zeros((panels * own, wide_ref.shape[1] - columns), BF16)
-    for step, ref in zip((0, *PEERS), refs):
-        cut = ref.shape[1]
-        at = pl.multiple_of((place_ref[2] + step) % X_SIZE * cut, LANE)
-        ref[...] = wide_ref[:, pl.ds(at, cut)]
-
-
-def pack(place, panels, cut):
-    rows = panels.shape[0] * panels.shape[1]
-    return call(
-        pack_kernel,
-        [jax.ShapeDtypeStruct((rows, cut), BF16)] * 4,
-        [SM, VM],
-        (place, panels),
-        [pltpu.VMEM((rows, X_SIZE * cut), BF16)],
-        flops=panels.size,
-        size=4 * panels.size,
-        vmem=4,
     )
 
 
@@ -249,11 +257,11 @@
     return found
 
 
-def products_kernel(place_ref, *refs, spots, own, rows):
+def products_kernel(*refs, spots, own, rows):
     blocks, (mine, one, two, far) = refs[: len(spots)], refs[len(spots) : len(spots) + 4]
     ordered_ref, sums_ref, eigen_ref = refs[len(spots) + 4 :]
     order = ordered_ref.shape[0]
-    x, z = place_ref[2], place_ref[3]
+    x, z = lax.axis_index("x"), lax.axis_index("z")
     for ref, units in zip(blocks, spots):
         for at, (back_z, back_x, panel) in enumerate(units):
             source = (x + X_SIZE - back_x) % X_SIZE * Z_SIZE + (z + Z_SIZE - back_z) % Z_SIZE
@@ -292,7 +300,7 @@
 }
 
 
-def products(place, found, pieces, spots, own, order, rows):
+def products(found, pieces, spots, own, order, rows):
     cut = pieces[0].shape[1]
     return call(
         functools.partial(products_kernel, spots=spots, own=own, rows=rows),
@@ -300,8 +308,8 @@
             jax.ShapeDtypeStruct((order, cut), BF16),
             jax.ShapeDtypeStruct(((4 + len(TILES)) * LANE, LANE), BF16),
         ],
-        [SM] + [VM] * (len(found) + len(pieces)),
-        (place, *found, *pieces),
+        [VM] * (len(found) + len(pieces)),
+        (*found, *pieces),
         [pltpu.VMEM((LANE, cut), BF16)],
         flops=2 * order * (order + LANE) * cut,
         size=6 * order * cut,
@@ -352,8 +360,9 @@
 
 
 def correction_kernel(
-    place_ref, sums_ref, ordered_ref, mine_ref, next_ref, last_ref, one_ref, two_ref, coeffs_ref
+    sums_ref, ordered_ref, mine_ref, next_ref, last_ref, one_ref, two_ref, coeffs_ref
 ):
+    rows = mine_ref.shape[0]
     tile = lambda at: sums_ref[at * LANE : (at + 1) * LANE, :]
     gram = lambda i, j: tile(TILES[i, j])
     inverses = [split(f) for f in small_inverses([gram(i, i) for i in range(4)])]
@@ -367,31 +376,28 @@
                 known = solved[j]
             value = value - fine_dot((gram(i, j), None), known)
         solved[i] = fine_dot(inverses[i], value)
-        coeffs_ref[:, i * LANE : (i + 1) * LANE] = solved[i].T.astype(BF16)
-    rows = mine_ref.shape[0]
-    x = place_ref[2]
-
-    def product(step, shift, count):
-        at = pl.multiple_of((x + step) % X_SIZE * rows + shift, UNIT)
-        return jnp.dot(
-            coeffs_ref[pl.ds(at, count), :], ordered_ref[...], preferred_element_type=F32
-        )
-
-    next_ref[...] = product(PEERS[0], 0, rows).astype(BF16)
-    last_ref[...] = product(PEERS[1], 0, rows).astype(BF16)
-    far = product(PEERS[2], 0, rows).astype(BF16)
-    one_ref[...] = far[0 : rows // 2]
-    two_ref[...] = far[rows // 2 :]
-    mine_ref[...] = product(0, 0, rows).astype(BF16)
-
-
-def correction(place, sums, ordered, rows):
+        turned = solved[i].T.astype(BF16)
+        for x in range(X_SIZE):
+            to = pl.multiple_of((x + X_SIZE - lax.axis_index("x")) % X_SIZE * rows, UNIT)
+            coeffs_ref[pl.ds(to, rows), i * LANE : (i + 1) * LANE] = turned[x * rows : (x + 1) * rows]
+    product = jnp.dot(
+        coeffs_ref[...], ordered_ref[...], preferred_element_type=F32
+    ).astype(BF16)
+    piece = lambda step: product[step * rows : (step + 1) * rows]
+    mine_ref[...] = piece(0)
+    next_ref[...] = piece(PEERS[0])
+    last_ref[...] = piece(PEERS[1])
+    one_ref[...] = piece(PEERS[2])[0 : rows // 2]
+    two_ref[...] = piece(PEERS[2])[rows // 2 :]
+
+
+def correction(sums, ordered, rows):
     order, cut = ordered.shape
     return call(
         correction_kernel,
         piece_shapes(rows, cut),
-        [SM, VM, VM],
-        (place, sums, ordered),
+        [VM, VM],
+        (sums, ordered),
         [pltpu.VMEM((LANE, order), BF16)],
         flops=2 * order * LANE * cut,
         size=4 * order * cut,
@@ -399,33 +405,44 @@
     )
 
 
-def subtract_kernel(place_ref, eigen_ref, mine, one, two, half0, half1, out_ref):
+def subtract_kernel(eigen_ref, mine, one, two, half0, half1, out_ref, held_ref, sems):
     rows, columns = eigen_ref.shape
     cut = mine.shape[1]
     half = rows // 2
     sources = {0: ((0, mine),), 1: ((0, one),), 3: ((0, two),), 2: ((0, half0), (half, half1))}
+    leaves = []
     for at in range(X_SIZE):
         begin, span = at * cut, min(cut, columns - at * cut)
         for back, refs in sources.items():
 
-            @pl.when((place_ref[2] + X_SIZE - back) % X_SIZE == at)
+            @pl.when((lax.axis_index("x") + X_SIZE - back) % X_SIZE == at)
             def _(refs=refs, begin=begin, span=span):
                 for row, ref in refs:
                     high = row + ref.shape[0]
-                    out_ref[row:high, begin : begin + span] = (
+                    held_ref[row:high, begin : begin + span] = (
                         eigen_ref[row:high, begin : begin + span] - ref[:, 0:span].astype(F32)
                     )
 
-
-def subtract(place, eigen, pieces):
+        chunk = slice(begin, begin + span)
+        leaves.append(
+            pltpu.make_async_copy(held_ref.at[:, chunk], out_ref.at[:, chunk], sems.at[at])
+        )
+        leaves[-1].start()
+    for leave in leaves:
+        leave.wait()
+
+
+def subtract(eigen, pieces):
     return call(
         subtract_kernel,
         jax.ShapeDtypeStruct(eigen.shape, F32),
-        [SM] + [VM] * 6,
-        (place, eigen, *pieces),
+        [VM] * 6,
+        (eigen, *pieces),
+        [pltpu.VMEM(eigen.shape, F32), pltpu.SemaphoreType.DMA((X_SIZE,))],
         flops=eigen.size,
         size=10 * eigen.size,
-        vmem=10,
+        vmem=12,
+        outs=ANY,
     )
 
 
@@ -461,12 +478,8 @@
     rows = eigvecs.shape[0]
     order = count * own * X_SIZE * Z_SIZE
     cut = -(-columns // (LANE * X_SIZE)) * LANE
-    place = jnp.stack(
-        [lax.axis_index("row"), lax.axis_size("row"), lax.axis_index("x"), lax.axis_index("z")]
-    ).astype(jnp.int32)
-
-    packed = pack(place, panels, cut)
-    swept = sweep_all(place, eigvecs, span_vectors, span_offsets, cut)
+    *packed, down, up = front(eigvecs, span_vectors, span_offsets, panels, cut)
+    swept = sweep_all(eigvecs, span_vectors, span_offsets, down, up, cut)
     eigen, pieces = swept[0], swept[1:]
     one, two, far = traded(packed)
     found, spots = [], []
@@ -476,12 +489,12 @@
             found.append(block)
             spots.append([(back, back_x, panel) for back_x, panel in unit])
     others = [pieces[0], *traded(pieces)]
-    ordered, sums = products(place, found, others, spots, own, order, rows)
+    ordered, sums = products(found, others, spots, own, order, rows)
 
     parts = exchange(sums.reshape(peers, -1, LANE), ("row", "x"))
     sums = exchange(total_for_all(parts), ("row", "x"))
-    corrections = correction(place, sums.reshape(-1, LANE), ordered, rows)
-    return subtract(place, eigen, [corrections[0], *traded(corrections)])
+    corrections = correction(sums.reshape(-1, LANE), ordered, rows)
+    return subtract(eigen, [corrections[0], *traded(corrections)])
 
 
 def solution(mesh):

time: 118 us -> 113 us (0.958)
  local copies, waits for them, and re-layouts: 3.91 us -> 0.95 us
  Pallas kernels: 15.9 us -> 14.6 us
  waiting for transfers between devices: 18.4 us -> 17.2 us
    unnamed x16 -> x8, local copies, waits for them, and re-layouts: 3.88 us -> 0.92 us
    pallas_call x7 -> x6, Pallas kernels: 15.9 us -> 14.6 us  [call(): pl.pallas_call(kernel, out_shape=out_shape, in_specs=in_specs, out_specs=...]
  transfers between devices with their start and end apart: 26 -> 26, of which waited for: 9 -> 9; matrix products, arithmetic and copies ran while one was open for 0% -> 1% of each run, Pallas kernels for 3% -> 3%
where the time goes in v3:
time: 113 us; the launch traced here: 112 us
  starting transfers between devices  43.7 us (39%)
  blocking collectives  35.3 us (31%)
  waiting for transfers between devices  17.2 us (15%)
  Pallas kernels  14.6 us (13%)
    ppermute x24, starting transfers between devices, shifted(): lax.ppermute(value, axis, [(at, (at + steps) % count) for at in range(cou...  37.2 us
    all_to_all x2, blocking collectives, exchange(): return lax.all_to_all(pieces, axes, 0, 0, tiled=True)  35.3 us
    ppermute x24, waiting for transfers between devices, shifted(): lax.ppermute(value, axis, [(at, (at + steps) % count) for at in range(cou...  17.2 us
    pallas_call x6, Pallas kernels, call(): pl.pallas_call(kernel, out_shape=out_shape, in_specs=in_specs, out_specs=...  14.6 us
    ppermute x2, starting transfers between devices, from_behind(): lax.ppermute(value, axis, [(source, source + steps) for source in range(f...  6.51 us
  transfers between devices with their start and end apart: 26, of which 9 were waited for; matrix products, arithmetic and copies ran while one was open for 1% of the time, Pallas kernels for 3%

profile of v3, /device:TPU:1, one launch (start us, length us, event | category | flops | bytes accessed | tf_op | source)
XLA Modules:
  0.0 112.1 jit_solution(16034063838844045927)
XLA Ops:
  0.0 3.0 %shard_map.46 = (bf16[16,3200]{1,0:T(8,128)(2,1)}, bf16[16,3200]{1,0:T(8,128)(2,1)}, bf16[16,3200]{1,0:T(8,128)(2,1)}, bf16[16,3200]{1,0:T(8,128)(2,1)}, f32[32,2432]{1,0:T(8,128)}, /*index=5*/f32[32,1408]{1,0:T(8,128)}) custom-call(s32[2,8]{1,0:T(2,128)} %offsets_ref.3, f32[2,8,4,128]{3,2,1,0:T(4,128)} %vectors_ref.3, bf16[2,8,12544]{2,1,0:T(8,128)(2,1)} %panels_ref.1, ...), custom_call_target="tpu_custom_call" | custom-call | flops 200704 | bytes 802816 | tf_op jit(solution)/shard_map/pallas_call | solution.py:28
  3.1 2.1 %collective-permute-start.2 = (bf16[16,3200]{1,0:T(8,128)(2,1)}, bf16[16,3200]{1,0:T(8,128)(2,1)S(1)}, u32[]{:S(2)}, u32[]{:S(2)}) collective-permute-start(bf16[16,3200]{1,0:T(8,128)(2,1)} %get-tuple-element.27), channel_id=1, source_target_pairs={{0,8},{8,16},{16,24},{24,0},{1,9},{9,17},{17,25},{25,1},{2,10},{10... | collective-permute-start | bytes 307208 | tf_op jit(solution)/shard_map/ppermute | solution.py:41
  5.2 1.4 %collective-permute-start.10 = (bf16[16,3200]{1,0:T(8,128)(2,1)}, bf16[16,3200]{1,0:T(8,128)(2,1)S(1)}, u32[]{:S(2)}, u32[]{:S(2)}) collective-permute-start(bf16[16,3200]{1,0:T(8,128)(2,1)} %get-tuple-element.28), channel_id=1, source_target_pairs={{0,24},{8,0},{16,8},{24,16},{1,25},{9,1},{17,9},{25,17},{2,26},{10... | collective-permute-start | bytes 307208 | tf_op jit(solution)/shard_map/ppermute | solution.py:41
  6.5 1.6 %collective-permute-start.11 = (bf16[16,3200]{1,0:T(8,128)(2,1)}, bf16[16,3200]{1,0:T(8,128)(2,1)S(1)}, u32[]{:S(2)}, u32[]{:S(2)}) collective-permute-start(bf16[16,3200]{1,0:T(8,128)(2,1)} %get-tuple-element.29), channel_id=1, source_target_pairs={{0,16},{8,24},{16,0},{24,8},{1,17},{9,25},{17,1},{25,9},{2,18},{10... | collective-permute-start | bytes 307208 | tf_op jit(solution)/shard_map/ppermute | solution.py:41
  8.2 3.4 %collective-permute-start.1 = (f32[32,1408]{1,0:T(8,128)}, f32[32,1408]{1,0:T(8,128)S(1)}, u32[]{:S(2)}, u32[]{:S(2)}) collective-permute-start(f32[32,1408]{1,0:T(8,128)} %get-tuple-element.24), channel_id=1, source_target_pairs={{32,0},{64,32},{96,64},{128,96},{160,128},{192,160},{224,192},{33,... | collective-permute-start | bytes 540680 | tf_op jit(solution)/shard_map/ppermute | solution.py:47
  11.6 3.1 %collective-permute-start = (f32[32,2432]{1,0:T(8,128)}, f32[32,2432]{1,0:T(8,128)S(1)}, u32[]{:S(2)}, u32[]{:S(2)}) collective-permute-start(f32[32,2432]{1,0:T(8,128)} %get-tuple-element.23), channel_id=1, source_target_pairs={{0,32},{32,64},{64,96},{96,128},{128,160},{160,192},{192,224},{1,3... | collective-permute-start | bytes 933896 | tf_op jit(solution)/shard_map/ppermute | solution.py:47
  14.7 0.9 constant_dynamic-update-slice_fusion.1
  15.6 5.7 %collective-permute-start.4 = (bf16[32,3200]{1,0:T(8,128)(2,1)S(1)}, bf16[32,3200]{1,0:T(8,128)(2,1)S(1)}, u32[]{:S(2)}, u32[]{:S(2)}) collective-permute-start(bf16[32,3200]{1,0:T(8,128)(2,1)S(1)} %constant_dynamic-update-slice_fusion.refs_0_), channel_id=1, source_target_pairs={{0,7},{1,0},{2,1},{3,2},{4,3},{5,4},{6,5},{7,6},{8,15},{9,8},{10,9... | collective-permute-start | bytes 614408 | tf_op jit(solution)/shard_map/ppermute | solution.py:41
  21.3 2.7 %collective-permute-start.13 = (bf16[32,3200]{1,0:T(8,128)(2,1)S(1)}, bf16[32,3200]{1,0:T(8,128)(2,1)S(1)}, u32[]{:S(2)}, u32[]{:S(2)}) collective-permute-start(bf16[32,3200]{1,0:T(8,128)(2,1)S(1)} %constant_dynamic-update-slice_fusion.2.refs_8_), channel_id=1, source_target_pairs={{0,7},{1,0},{2,1},{3,2},{4,3},{5,4},{6,5},{7,6},{8,15},{9,8},{10,9... | collective-permute-start | bytes 614408 | tf_op jit(solution)/shard_map/ppermute | solution.py:41
  24.1 2.1 %collective-permute-done.4.refs_2_ = bf16[32,3200]{1,0:T(8,128)(2,1)S(1)} collective-permute-done((bf16[32,3200]{1,0:T(8,128)(2,1)S(1)}, bf16[32,3200]{1,0:T(8,128)(2,1)S(1)}, u32[]{:S(2)}, u32[]{:S(2)}) %collective-permute-start.4) | collective-permute-done | bytes 204832 | tf_op jit(solution)/shard_map/ppermute | solution.py:41
  26.2 3.4 %collective-permute-start.6 = (bf16[32,3200]{1,0:T(8,128)(2,1)S(1)}, bf16[32,3200]{1,0:T(8,128)(2,1)S(1)}, u32[]{:S(2)}, u32[]{:S(2)}) collective-permute-start(bf16[32,3200]{1,0:T(8,128)(2,1)S(1)} %collective-permute-done.4.refs_2_), channel_id=1, source_target_pairs={{0,7},{1,0},{2,1},{3,2},{4,3},{5,4},{6,5},{7,6},{8,15},{9,8},{10,9... | collective-permute-start | bytes 614408 | tf_op jit(solution)/shard_map/ppermute | solution.py:41
  29.6 0.8 collective-permute-done.13.refs_10_
  30.3 3.2 %collective-permute-start.15 = (bf16[32,3200]{1,0:T(8,128)(2,1)S(1)}, bf16[32,3200]{1,0:T(8,128)(2,1)S(1)}, u32[]{:S(2)}, u32[]{:S(2)}) collective-permute-start(bf16[32,3200]{1,0:T(8,128)(2,1)S(1)} %collective-permute-done.13.refs_10_), channel_id=1, source_target_pairs={{0,7},{1,0},{2,1},{3,2},{4,3},{5,4},{6,5},{7,6},{8,15},{9,8},{10,9... | collective-permute-start | bytes 614408 | tf_op jit(solution)/shard_map/ppermute | solution.py:41
  33.9 3.6 %shard_map.47 = (f32[32,12544]{1,0:T(8,128)S(1)}, bf16[32,3200]{1,0:T(8,128)(2,1)S(1)}, bf16[32,3200]{1,0:T(8,128)(2,1)S(1)}, bf16[32,3200]{1,0:T(8,128)(2,1)S(1)}, bf16[32,3200]{1,0:T(8,128)(2,1)S(1)}) custom-call(s32[2,8]{1,0:T(2,128)S(1)} %copy-done.2, s32[2,8]{1,0:T(2,128)S(1)} %slice_convert_fusion.1.upper_offsets_ref, ...), custom_call_target="tpu_custom_call" | custom-call | flops 16056320 | bytes 4816896 | tf_op jit(solution)/shard_map/pallas_call | solution.py:28
  37.6 0.4 collective-permute-start.19
  38.0 2.4 %collective-permute-start.20 = (bf16[32,3200]{1,0:T(8,128)(2,1)S(1)}, bf16[32,3200]{1,0:T(8,128)(2,1)S(1)}, u32[]{:S(2)}, u32[]{:S(2)}) collective-permute-start(bf16[32,3200]{1,0:T(8,128)(2,1)S(1)} %get-tuple-element.32), channel_id=1, source_target_pairs={{0,24},{8,0},{16,8},{24,16},{1,25},{9,1},{17,9},{25,17},{2,26},{10... | collective-permute-start | bytes 614408 | tf_op jit(solution)/shard_map/ppermute | solution.py:41
  40.4 2.7 %collective-permute-start.17 = (bf16[32,3200]{1,0:T(8,128)(2,1)S(1)}, bf16[32,3200]{1,0:T(8,128)(2,1)S(1)}, u32[]{:S(2)}, u32[]{:S(2)}) collective-permute-start(bf16[32,3200]{1,0:T(8,128)(2,1)S(1)} %collective-permute-done.15.refs_12_), channel_id=1, source_target_pairs={{0,7},{1,0},{2,1},{3,2},{4,3},{5,4},{6,5},{7,6},{8,15},{9,8},{10,9... | collective-permute-start | bytes 614408 | tf_op jit(solution)/shard_map/ppermute | solution.py:41
  43.1 0.7 collective-permute-start.21
  43.8 1.4 %collective-permute-done.19.refs_17_ = bf16[32,3200]{1,0:T(8,128)(2,1)S(1)} collective-permute-done((bf16[32,3200]{1,0:T(8,128)(2,1)S(1)}, bf16[32,3200]{1,0:T(8,128)(2,1)S(1)}, u32[]{:S(2)}, u32[]{:S(2)}) %collective-permute-start.19) | collective-permute-done | bytes 204832 | tf_op jit(solution)/shard_map/ppermute | solution.py:41
  45.2 2.4 %collective-permute-start.8 = (bf16[32,3200]{1,0:T(8,128)(2,1)S(1)}, bf16[32,3200]{1,0:T(8,128)(2,1)S(1)}, u32[]{:S(2)}, u32[]{:S(2)}) collective-permute-start(bf16[32,3200]{1,0:T(8,128)(2,1)S(1)} %collective-permute-done.6.refs_4_), channel_id=1, source_target_pairs={{0,7},{1,0},{2,1},{3,2},{4,3},{5,4},{6,5},{7,6},{8,15},{9,8},{10,9... | collective-permute-start | bytes 614408 | tf_op jit(solution)/shard_map/ppermute | solution.py:41
  47.7 2.7 %collective-permute-start.18 = (bf16[32,3200]{1,0:T(8,128)(2,1)S(1)}, bf16[32,3200]{1,0:T(8,128)(2,1)S(1)}, u32[]{:S(2)}, u32[]{:S(2)}) collective-permute-start(bf16[32,3200]{1,0:T(8,128)(2,1)S(1)} %collective-permute-done.17.refs_14_), channel_id=1, source_target_pairs={{0,7},{1,0},{2,1},{3,2},{4,3},{5,4},{6,5},{7,6},{8,15},{9,8},{10,9... | collective-permute-start | bytes 614408 | tf_op jit(solution)/shard_map/ppermute | solution.py:41
  50.6 2.8 %collective-permute-done.16.refs_13_ = bf16[32,3200]{1,0:T(8,128)(2,1)S(1)} collective-permute-done((bf16[32,3200]{1,0:T(8,128)(2,1)S(1)}, bf16[32,3200]{1,0:T(8,128)(2,1)S(1)}, u32[]{:S(2)}, u32[]{:S(2)}) %collective-permute-start.16) | collective-permute-done | bytes 204832 | tf_op jit(solution)/shard_map/ppermute | solution.py:41
  53.4 3.9 %collective-permute-done.9.refs_7_ = bf16[32,3200]{1,0:T(8,128)(2,1)S(1)} collective-permute-done((bf16[32,3200]{1,0:T(8,128)(2,1)S(1)}, bf16[32,3200]{1,0:T(8,128)(2,1)S(1)}, u32[]{:S(2)}, u32[]{:S(2)}) %collective-permute-start.9) | collective-permute-done | bytes 204832 | tf_op jit(solution)/shard_map/ppermute | solution.py:41
  57.3 2.6 %shard_map.48 = (bf16[512,3200]{1,0:T(8,128)(2,1)S(1)}, bf16[1792,128]{1,0:T(8,128)(2,1)S(1)}) custom-call(bf16[32,3200]{1,0:T(8,128)(2,1)S(1)} %constant_dynamic-update-slice_fusion.refs_0_, bf16[32,3200]{1,0:T(8,128)(2,1)S(1)} %collective-permute-done.3.refs_1_, bf16[32,3200]{1,0:T(8,128)(2,1)S(1)} %collective-permute-done.4.refs_2_, ...), custom_call_target="tpu_custom_call" | custom-call | flops 2097152000 | bytes 9830400 | tf_op jit(solution)/shard_map/pallas_call | solution.py:28
  59.9 20.5 %all_to_all.10.parts_ref = bf16[32,56,128]{2,1,0:T(8,128)(2,1)S(1)} all-to-all(bf16[32,56,128]{2,1,0:T(8,128)(2,1)S(1)} %bitcast.3), channel_id=1, replica_groups=mesh['row'=8,'x'=4,'z'=8] {'row','x'}, dimensions={0} | all-to-all | bytes 917504 | tf_op jit(solution)/shard_map/all_to_all | solution.py:471
  80.5 14.8 %all_to_all.11 = bf16[32,56,128]{2,1,0:T(8,128)(2,1)S(1)} all-to-all(bf16[32,56,128]{2,1,0:T(8,128)(2,1)S(1)} %shard_map.49), channel_id=1, replica_groups=mesh['row'=8,'x'=4,'z'=8] {'row','x'}, dimensions={0} | all-to-all | bytes 917504 | tf_op jit(solution)/shard_map/all_to_all | solution.py:471
  95.3 4.0 %shard_map.50 = (bf16[32,3200]{1,0:T(8,128)(2,1)S(1)}, bf16[32,3200]{1,0:T(8,128)(2,1)S(1)}, bf16[32,3200]{1,0:T(8,128)(2,1)S(1)}, bf16[16,3200]{1,0:T(8,128)(2,1)S(1)}, bf16[16,3200]{1,0:T(8,128)(2,1)S(1)}) custom-call(bf16[1792,128]{1,0:T(8,128)(2,1)S(1)} %bitcast.2, bf16[512,3200]{1,0:T(8,128)(2,1)S(1)} %get-tuple-element.35.ordered_ref), custom_call_target="tpu_custom_call" | custom-call | flops 419430400 | bytes 6553600 | tf_op jit(solution)/shard_map/pallas_call | solution.py:28
  99.7 2.4 %collective-permute-start.23 = (bf16[32,3200]{1,0:T(8,128)(2,1)S(1)}, bf16[32,3200]{1,0:T(8,128)(2,1)S(1)}, u32[]{:S(2)}, u32[]{:S(2)}) collective-permute-start(bf16[32,3200]{1,0:T(8,128)(2,1)S(1)} %get-tuple-element.38), channel_id=1, source_target_pairs={{0,24},{8,0},{16,8},{24,16},{1,25},{9,1},{17,9},{25,17},{2,26},{10... | collective-permute-start | bytes 614408 | tf_op jit(solution)/shard_map/ppermute | solution.py:41
  102.1 3.0 %collective-permute-start.25 = (bf16[16,3200]{1,0:T(8,128)(2,1)S(1)}, bf16[16,3200]{1,0:T(8,128)(2,1)S(1)}, u32[]{:S(2)}, u32[]{:S(2)}) collective-permute-start(bf16[16,3200]{1,0:T(8,128)(2,1)S(1)} %get-tuple-element.40), channel_id=1, source_target_pairs={{0,16},{8,24},{16,0},{24,8},{1,17},{9,25},{17,1},{25,9},{2,18},{10... | collective-permute-start | bytes 307208 | tf_op jit(solution)/shard_map/ppermute | solution.py:41
  105.0 3.4 %collective-permute-done.24.half0 = bf16[16,3200]{1,0:T(8,128)(2,1)S(1)} collective-permute-done((bf16[16,3200]{1,0:T(8,128)(2,1)S(1)}, bf16[16,3200]{1,0:T(8,128)(2,1)S(1)}, u32[]{:S(2)}, u32[]{:S(2)}) %collective-permute-start.24) | collective-permute-done | bytes 102432 | tf_op jit(solution)/shard_map/ppermute | solution.py:41
  108.5 2.2 %collective-permute-done.25.half1 = bf16[16,3200]{1,0:T(8,128)(2,1)S(1)} collective-permute-done((bf16[16,3200]{1,0:T(8,128)(2,1)S(1)}, bf16[16,3200]{1,0:T(8,128)(2,1)S(1)}, u32[]{:S(2)}, u32[]{:S(2)}) %collective-permute-start.25) | collective-permute-done | bytes 102432 | tf_op jit(solution)/shard_map/ppermute | solution.py:41
  110.7 1.2 %shard_map.51 = f32[32,12544]{1,0:T(8,128)} custom-call(f32[32,12544]{1,0:T(8,128)S(1)} %get-tuple-element.25.eigen_ref, bf16[32,3200]{1,0:T(8,128)(2,1)S(1)} %get-tuple-element.36.mine, bf16[32,3200]{1,0:T(8,128)(2,1)S(1)} %collective-permute-done.22.one, bf16[32,3200]{1,0:T(8,128)(2,1)S(1)} %collective-permute-done.23.two, ...), custom_call_target="tpu_custom_call" | custom-call | flops 401408 | bytes 4014080 | tf_op jit(solution)/shard_map/pallas_call | solution.py:28
  (40 shorter events, 1.3 us)
Async XLA Ops:
  0.0 33.9 %copy-start.2 = (s32[2,8]{1,0:T(2,128)S(1)}, s32[2,8]{1,0:T(2,128)}, u32[]{:S(2)}) copy-start(s32[2,8]{1,0:T(2,128)} %offsets_ref.3) | copy-start | bytes 196
  0.0 33.9 %copy-start.1 = (f32[2,8,4,128]{3,2,1,0:T(4,128)S(1)}, f32[2,8,4,128]{3,2,1,0:T(4,128)}, u32[]{:S(2)}) copy-start(f32[2,8,4,128]{3,2,1,0:T(4,128)} %vectors_ref.3) | copy-start | bytes 98308
  0.0 33.9 %copy-start = (f32[32,12544]{1,0:T(8,128)S(1)}, f32[32,12544]{1,0:T(8,128)}, u32[]{:S(2)}) copy-start(f32[32,12544]{1,0:T(8,128)} %own_ref.1) | copy-start | bytes 4816900
  3.1 12.5 %collective-permute-start.2 = (bf16[16,3200]{1,0:T(8,128)(2,1)}, bf16[16,3200]{1,0:T(8,128)(2,1)S(1)}, u32[]{:S(2)}, u32[]{:S(2)}) collective-permute-start(bf16[16,3200]{1,0:T(8,128)(2,1)} %get-tuple-element.27), channel_id=1, source_target_pairs={{0,8},{8,16},{16,24},{24,0},{1,9},{9,17},{17,25},{25,1},{2,10},{10... | collective-permute-start | bytes 307208 | tf_op jit(solution)/shard_map/ppermute | solution.py:41
  5.2 16.1 %collective-permute-start.10 = (bf16[16,3200]{1,0:T(8,128)(2,1)}, bf16[16,3200]{1,0:T(8,128)(2,1)S(1)}, u32[]{:S(2)}, u32[]{:S(2)}) collective-permute-start(bf16[16,3200]{1,0:T(8,128)(2,1)} %get-tuple-element.28), channel_id=1, source_target_pairs={{0,24},{8,0},{16,8},{24,16},{1,25},{9,1},{17,9},{25,17},{2,26},{10... | collective-permute-start | bytes 307208 | tf_op jit(solution)/shard_map/ppermute | solution.py:41
  6.5 14.8 %collective-permute-start.11 = (bf16[16,3200]{1,0:T(8,128)(2,1)}, bf16[16,3200]{1,0:T(8,128)(2,1)S(1)}, u32[]{:S(2)}, u32[]{:S(2)}) collective-permute-start(bf16[16,3200]{1,0:T(8,128)(2,1)} %get-tuple-element.29), channel_id=1, source_target_pairs={{0,16},{8,24},{16,0},{24,8},{1,17},{9,25},{17,1},{25,9},{2,18},{10... | collective-permute-start | bytes 307208 | tf_op jit(solution)/shard_map/ppermute | solution.py:41
  8.2 15.9 %collective-permute-start.1 = (f32[32,1408]{1,0:T(8,128)}, f32[32,1408]{1,0:T(8,128)S(1)}, u32[]{:S(2)}, u32[]{:S(2)}) collective-permute-start(f32[32,1408]{1,0:T(8,128)} %get-tuple-element.24), channel_id=1, source_target_pairs={{32,0},{64,32},{96,64},{128,96},{160,128},{192,160},{224,192},{33,... | collective-permute-start | bytes 540680 | tf_op jit(solution)/shard_map/ppermute | solution.py:47
  11.6 22.3 %collective-permute-start = (f32[32,2432]{1,0:T(8,128)}, f32[32,2432]{1,0:T(8,128)S(1)}, u32[]{:S(2)}, u32[]{:S(2)}) collective-permute-start(f32[32,2432]{1,0:T(8,128)} %get-tuple-element.23), channel_id=1, source_target_pairs={{0,32},{32,64},{64,96},{96,128},{128,160},{160,192},{192,224},{1,3... | collective-permute-start | bytes 933896 | tf_op jit(solution)/shard_map/ppermute | solution.py:47
  15.6 10.5 %collective-permute-start.4 = (bf16[32,3200]{1,0:T(8,128)(2,1)S(1)}, bf16[32,3200]{1,0:T(8,128)(2,1)S(1)}, u32[]{:S(2)}, u32[]{:S(2)}) collective-permute-start(bf16[32,3200]{1,0:T(8,128)(2,1)S(1)} %constant_dynamic-update-slice_fusion.refs_0_), channel_id=1, source_target_pairs={{0,7},{1,0},{2,1},{3,2},{4,3},{5,4},{6,5},{7,6},{8,15},{9,8},{10,9... | collective-permute-start | bytes 614408 | tf_op jit(solution)/shard_map/ppermute | solution.py:41
  21.3 8.3 %collective-permute-start.3 = (bf16[32,3200]{1,0:T(8,128)(2,1)S(1)}, bf16[32,3200]{1,0:T(8,128)(2,1)S(1)}, u32[]{:S(2)}, u32[]{:S(2)}) collective-permute-start(bf16[32,3200]{1,0:T(8,128)(2,1)S(1)} %constant_dynamic-update-slice_fusion.refs_0_), channel_id=1, source_target_pairs={{0,1},{1,2},{2,3},{3,4},{4,5},{5,6},{6,7},{7,0},{8,9},{9,10},{10,1... | collective-permute-start | bytes 614408 | tf_op jit(solution)/shard_map/ppermute | solution.py:41
  21.3 9.0 %collective-permute-start.13 = (bf16[32,3200]{1,0:T(8,128)(2,1)S(1)}, bf16[32,3200]{1,0:T(8,128)(2,1)S(1)}, u32[]{:S(2)}, u32[]{:S(2)}) collective-permute-start(bf16[32,3200]{1,0:T(8,128)(2,1)S(1)} %constant_dynamic-update-slice_fusion.2.refs_8_), channel_id=1, source_target_pairs={{0,7},{1,0},{2,1},{3,2},{4,3},{5,4},{6,5},{7,6},{8,15},{9,8},{10,9... | collective-permute-start | bytes 614408 | tf_op jit(solution)/shard_map/ppermute | solution.py:41
  24.1 9.8 %collective-permute-start.12 = (bf16[32,3200]{1,0:T(8,128)(2,1)S(1)}, bf16[32,3200]{1,0:T(8,128)(2,1)S(1)}, u32[]{:S(2)}, u32[]{:S(2)}) collective-permute-start(bf16[32,3200]{1,0:T(8,128)(2,1)S(1)} %constant_dynamic-update-slice_fusion.2.refs_8_), channel_id=1, source_target_pairs={{0,1},{1,2},{2,3},{3,4},{4,5},{5,6},{6,7},{7,0},{8,9},{9,10},{10,1... | collective-permute-start | bytes 614408 | tf_op jit(solution)/shard_map/ppermute | solution.py:41
  26.2 11.8 %collective-permute-start.6 = (bf16[32,3200]{1,0:T(8,128)(2,1)S(1)}, bf16[32,3200]{1,0:T(8,128)(2,1)S(1)}, u32[]{:S(2)}, u32[]{:S(2)}) collective-permute-start(bf16[32,3200]{1,0:T(8,128)(2,1)S(1)} %collective-permute-done.4.refs_2_), channel_id=1, source_target_pairs={{0,7},{1,0},{2,1},{3,2},{4,3},{5,4},{6,5},{7,6},{8,15},{9,8},{10,9... | collective-permute-start | bytes 614408 | tf_op jit(solution)/shard_map/ppermute | solution.py:41
  29.6 10.8 %collective-permute-start.5 = (bf16[32,3200]{1,0:T(8,128)(2,1)S(1)}, bf16[32,3200]{1,0:T(8,128)(2,1)S(1)}, u32[]{:S(2)}, u32[]{:S(2)}) collective-permute-start(bf16[32,3200]{1,0:T(8,128)(2,1)S(1)} %collective-permute-done.3.refs_1_), channel_id=1, source_target_pairs={{0,1},{1,2},{2,3},{3,4},{4,5},{5,6},{6,7},{7,0},{8,9},{9,10},{10,1... | collective-permute-start | bytes 614408 | tf_op jit(solution)/shard_map/ppermute | solution.py:41
  30.3 10.0 %collective-permute-start.15 = (bf16[32,3200]{1,0:T(8,128)(2,1)S(1)}, bf16[32,3200]{1,0:T(8,128)(2,1)S(1)}, u32[]{:S(2)}, u32[]{:S(2)}) collective-permute-start(bf16[32,3200]{1,0:T(8,128)(2,1)S(1)} %collective-permute-done.13.refs_10_), channel_id=1, source_target_pairs={{0,7},{1,0},{2,1},{3,2},{4,3},{5,4},{6,5},{7,6},{8,15},{9,8},{10,9... | collective-permute-start | bytes 614408 | tf_op jit(solution)/shard_map/ppermute | solution.py:41
  33.9 9.2 %collective-permute-start.14 = (bf16[32,3200]{1,0:T(8,128)(2,1)S(1)}, bf16[32,3200]{1,0:T(8,128)(2,1)S(1)}, u32[]{:S(2)}, u32[]{:S(2)}) collective-permute-start(bf16[32,3200]{1,0:T(8,128)(2,1)S(1)} %collective-permute-done.12.refs_9_), channel_id=1, source_target_pairs={{0,1},{1,2},{2,3},{3,4},{4,5},{5,6},{6,7},{7,0},{8,9},{9,10},{10,1... | collective-permute-start | bytes 614408 | tf_op jit(solution)/shard_map/ppermute | solution.py:41
  37.6 7.6 %collective-permute-start.19 = (bf16[32,3200]{1,0:T(8,128)(2,1)S(1)}, bf16[32,3200]{1,0:T(8,128)(2,1)S(1)}, u32[]{:S(2)}, u32[]{:S(2)}) collective-permute-start(bf16[32,3200]{1,0:T(8,128)(2,1)S(1)} %get-tuple-element.31), channel_id=1, source_target_pairs={{0,8},{8,16},{16,24},{24,0},{1,9},{9,17},{17,25},{25,1},{2,10},{10... | collective-permute-start | bytes 614408 | tf_op jit(solution)/shard_map/ppermute | solution.py:41
  38.0 9.6 %collective-permute-start.20 = (bf16[32,3200]{1,0:T(8,128)(2,1)S(1)}, bf16[32,3200]{1,0:T(8,128)(2,1)S(1)}, u32[]{:S(2)}, u32[]{:S(2)}) collective-permute-start(bf16[32,3200]{1,0:T(8,128)(2,1)S(1)} %get-tuple-element.32), channel_id=1, source_target_pairs={{0,24},{8,0},{16,8},{24,16},{1,25},{9,1},{17,9},{25,17},{2,26},{10... | collective-permute-start | bytes 614408 | tf_op jit(solution)/shard_map/ppermute | solution.py:41
  40.4 7.2 %collective-permute-start.7 = (bf16[32,3200]{1,0:T(8,128)(2,1)S(1)}, bf16[32,3200]{1,0:T(8,128)(2,1)S(1)}, u32[]{:S(2)}, u32[]{:S(2)}) collective-permute-start(bf16[32,3200]{1,0:T(8,128)(2,1)S(1)} %collective-permute-done.5.refs_3_), channel_id=1, source_target_pairs={{0,1},{1,2},{2,3},{3,4},{4,5},{5,6},{6,7},{7,0},{8,9},{9,10},{10,1... | collective-permute-start | bytes 614408 | tf_op jit(solution)/shard_map/ppermute | solution.py:41
  40.4 7.3 %collective-permute-start.17 = (bf16[32,3200]{1,0:T(8,128)(2,1)S(1)}, bf16[32,3200]{1,0:T(8,128)(2,1)S(1)}, u32[]{:S(2)}, u32[]{:S(2)}) collective-permute-start(bf16[32,3200]{1,0:T(8,128)(2,1)S(1)} %collective-permute-done.15.refs_12_), channel_id=1, source_target_pairs={{0,7},{1,0},{2,1},{3,2},{4,3},{5,4},{6,5},{7,6},{8,15},{9,8},{10,9... | collective-permute-start | bytes 614408 | tf_op jit(solution)/shard_map/ppermute | solution.py:41
  43.1 7.2 %collective-permute-start.21 = (bf16[32,3200]{1,0:T(8,128)(2,1)S(1)}, bf16[32,3200]{1,0:T(8,128)(2,1)S(1)}, u32[]{:S(2)}, u32[]{:S(2)}) collective-permute-start(bf16[32,3200]{1,0:T(8,128)(2,1)S(1)} %get-tuple-element.33), channel_id=1, source_target_pairs={{0,16},{8,24},{16,0},{24,8},{1,17},{9,25},{17,1},{25,9},{2,18},{10... | collective-permute-start | bytes 614408 | tf_op jit(solution)/shard_map/ppermute | solution.py:41
  45.2 5.4 %collective-permute-start.8 = (bf16[32,3200]{1,0:T(8,128)(2,1)S(1)}, bf16[32,3200]{1,0:T(8,128)(2,1)S(1)}, u32[]{:S(2)}, u32[]{:S(2)}) collective-permute-start(bf16[32,3200]{1,0:T(8,128)(2,1)S(1)} %collective-permute-done.6.refs_4_), channel_id=1, source_target_pairs={{0,7},{1,0},{2,1},{3,2},{4,3},{5,4},{6,5},{7,6},{8,15},{9,8},{10,9... | collective-permute-start | bytes 614408 | tf_op jit(solution)/shard_map/ppermute | solution.py:41
  47.5 5.8 %collective-permute-start.16 = (bf16[32,3200]{1,0:T(8,128)(2,1)S(1)}, bf16[32,3200]{1,0:T(8,128)(2,1)S(1)}, u32[]{:S(2)}, u32[]{:S(2)}) collective-permute-start(bf16[32,3200]{1,0:T(8,128)(2,1)S(1)} %collective-permute-done.14.refs_11_), channel_id=1, source_target_pairs={{0,1},{1,2},{2,3},{3,4},{4,5},{5,6},{6,7},{7,0},{8,9},{9,10},{10,1... | collective-permute-start | bytes 614408 | tf_op jit(solution)/shard_map/ppermute | solution.py:41
  47.6 9.7 %collective-permute-start.9 = (bf16[32,3200]{1,0:T(8,128)(2,1)S(1)}, bf16[32,3200]{1,0:T(8,128)(2,1)S(1)}, u32[]{:S(2)}, u32[]{:S(2)}) collective-permute-start(bf16[32,3200]{1,0:T(8,128)(2,1)S(1)} %collective-permute-done.7.refs_5_), channel_id=1, source_target_pairs={{0,1},{1,2},{2,3},{3,4},{4,5},{5,6},{6,7},{7,0},{8,9},{9,10},{10,1... | collective-permute-start | bytes 614408 | tf_op jit(solution)/shard_map/ppermute | solution.py:41
  47.7 9.6 %collective-permute-start.18 = (bf16[32,3200]{1,0:T(8,128)(2,1)S(1)}, bf16[32,3200]{1,0:T(8,128)(2,1)S(1)}, u32[]{:S(2)}, u32[]{:S(2)}) collective-permute-start(bf16[32,3200]{1,0:T(8,128)(2,1)S(1)} %collective-permute-done.17.refs_14_), channel_id=1, source_target_pairs={{0,7},{1,0},{2,1},{3,2},{4,3},{5,4},{6,5},{7,6},{8,15},{9,8},{10,9... | collective-permute-start | bytes 614408 | tf_op jit(solution)/shard_map/ppermute | solution.py:41
  99.3 11.4 %collective-permute-start.22 = (bf16[32,3200]{1,0:T(8,128)(2,1)S(1)}, bf16[32,3200]{1,0:T(8,128)(2,1)S(1)}, u32[]{:S(2)}, u32[]{:S(2)}) collective-permute-start(bf16[32,3200]{1,0:T(8,128)(2,1)S(1)} %get-tuple-element.37), channel_id=1, source_target_pairs={{0,8},{8,16},{16,24},{24,0},{1,9},{9,17},{17,25},{25,1},{2,10},{10... | collective-permute-start | bytes 614408 | tf_op jit(solution)/shard_map/ppermute | solution.py:41
  99.7 11.0 %collective-permute-start.23 = (bf16[32,3200]{1,0:T(8,128)(2,1)S(1)}, bf16[32,3200]{1,0:T(8,128)(2,1)S(1)}, u32[]{:S(2)}, u32[]{:S(2)}) collective-permute-start(bf16[32,3200]{1,0:T(8,128)(2,1)S(1)} %get-tuple-element.38), channel_id=1, source_target_pairs={{0,24},{8,0},{16,8},{24,16},{1,25},{9,1},{17,9},{25,17},{2,26},{10... | collective-permute-start | bytes 614408 | tf_op jit(solution)/shard_map/ppermute | solution.py:41
  102.1 6.4 %collective-permute-start.24 = (bf16[16,3200]{1,0:T(8,128)(2,1)S(1)}, bf16[16,3200]{1,0:T(8,128)(2,1)S(1)}, u32[]{:S(2)}, u32[]{:S(2)}) collective-permute-start(bf16[16,3200]{1,0:T(8,128)(2,1)S(1)} %get-tuple-element.39), channel_id=1, source_target_pairs={{0,16},{8,24},{16,0},{24,8},{1,17},{9,25},{17,1},{25,9},{2,18},{10... | collective-permute-start | bytes 307208 | tf_op jit(solution)/shard_map/ppermute | solution.py:41
  102.1 8.6 %collective-permute-start.25 = (bf16[16,3200]{1,0:T(8,128)(2,1)S(1)}, bf16[16,3200]{1,0:T(8,128)(2,1)S(1)}, u32[]{:S(2)}, u32[]{:S(2)}) collective-permute-start(bf16[16,3200]{1,0:T(8,128)(2,1)S(1)} %get-tuple-element.40), channel_id=1, source_target_pairs={{0,16},{8,24},{16,0},{24,8},{1,17},{9,25},{17,1},{25,9},{2,18},{10... | collective-permute-start | bytes 307208 | tf_op jit(solution)/shard_map/ppermute | solution.py:41

commit v4 on v3

--- a/solution.py
+++ b/solution.py
@@ -12,6 +12,7 @@
 COL = ("x", "z")
 X_SIZE, Z_SIZE = 4, 8
 LANE = 128
+GROUP = 4
 FRONT_MB = 60
 UNIT = 8
 F32 = jnp.float32
@@ -68,22 +69,56 @@
         pairs_ref[:, refl + i, band:] = jnp.zeros((spans, band), F32)
 
 
+def window_of(begin, width):
+    return pl.ds(pl.multiple_of(begin // LANE * LANE, LANE), width)
+
+
+def apply_spans(begins, pairs, state_ref):
+    refl, width = pairs[0].shape[0] // 2, pairs[0].shape[1]
+    moved = [pltpu.roll(pair, begin % LANE, 1) for begin, pair in zip(begins, pairs)]
+    windows = [state_ref[:, window_of(begin, width)] for begin in begins]
+    inner = [
+        [jnp.sum(window * pair[i : i + 1, :], axis=1, keepdims=True) for i in range(refl)]
+        for window, pair in zip(windows, moved)
+    ]
+    for begin, window, pair, sums in zip(begins, windows, moved, inner):
+        for i in range(refl):
+            window = window - sums[i] * pair[refl + i : refl + i + 1, :]
+        state_ref[:, window_of(begin, width)] = window
+
+
 def apply_span(begin, pair, state_ref):
-    refl = pair.shape[0] // 2
-    base = pl.multiple_of(begin // LANE * LANE, LANE)
-    moved = pltpu.roll(pair, begin - base, 1)
-    window = state_ref[:, pl.ds(base, pair.shape[1])]
-    update = window
-    for i in range(refl):
-        inner = jnp.sum(window * moved[i : i + 1, :], axis=1, keepdims=True)
-        update = update - inner * moved[refl + i : refl + i + 1, :]
-    state_ref[:, pl.ds(base, pair.shape[1])] = update
+    apply_spans([begin], [pair], state_ref)
+
+
+def apply_in_order(begins, pairs_ref, spots, state_ref):
+    if len(begins) == 1:
+        apply_span(begins[0], pairs_ref[spots[0]], state_ref)
+        return
+    tiles = [begin // LANE for begin in begins]
+    apart = [
+        jnp.abs(one - other) >= pairs_ref.shape[-1] // LANE
+        for at, one in enumerate(tiles)
+        for other in tiles[:at]
+    ]
+    clear = functools.reduce(jnp.logical_and, apart)
+
+    @pl.when(clear)
+    def _():
+        apply_spans(begins, [pairs_ref[spot] for spot in spots], state_ref)
+
+    @pl.when(jnp.logical_not(clear))
+    def _():
+        half = len(begins) // 2
+        apply_in_order(begins[:half], pairs_ref, spots[:half], state_ref)
+        apply_in_order(begins[half:], pairs_ref, spots[half:], state_ref)
 
 
 def front_kernel(
     offsets_ref, vectors_ref, panels_ref, eigen_ref, *refs
 ):
-    down_ref, up_ref, wide_ref, sems = refs[-4:]
+    *piece_refs, down_out, up_out = refs[:6]
+    down_ref, up_ref, wide_ref, sems = refs[6:]
     sweeps, spans, refl, band = vectors_ref.shape
     rows, columns = eigen_ref.shape
     panels, own, _ = panels_ref.shape
@@ -116,11 +151,20 @@
         ref[0:sweeps, width + count * band : width + count * band + spans] = offsets_ref[...].astype(F32)
     for move in moves[:panels]:
         move.wait()
-    for step, ref in zip((0, *PEERS), refs):
+    leaves = []
+
+    def leave(source, target):
+        leaves.append(pltpu.make_async_copy(source, target, sems.at[len(moves) + len(leaves)]))
+        leaves[-1].start()
+
+    for step, ref in zip((0, *PEERS), piece_refs):
         cut = ref.shape[1]
         at = pl.multiple_of((lax.axis_index("x") + step) % X_SIZE * cut, LANE)
-        ref[...] = wide_ref[:, pl.ds(at, cut)]
-    for move in moves[panels:]:
+        leave(wide_ref.at[:, pl.ds(at, cut)], ref)
+    for move, source, target in zip(moves[panels:], (down_ref, up_ref), (down_out, up_out)):
+        move.wait()
+        leave(source, target)
+    for move in leaves:
         move.wait()
 
 
@@ -141,17 +185,23 @@
         + [wide(left + sweeps * band + LANE), wide(right + (sweeps - 1) * band + LANE)],
         [VM, VM, ANY, ANY],
         (offsets, vectors, panels, eigen),
-        [pltpu.VMEM((high, X_SIZE * cut), BF16), pltpu.SemaphoreType.DMA((panels.shape[0] + 2,))],
+        [
+            pltpu.VMEM((rows, left + sweeps * band + LANE), F32),
+            pltpu.VMEM((rows, right + (sweeps - 1) * band + LANE), F32),
+            pltpu.VMEM((high, X_SIZE * cut), BF16),
+            pltpu.SemaphoreType.DMA((panels.shape[0] + 8,)),
+        ],
         flops=panels.size,
         size=4 * panels.size,
         vmem=FRONT_MB,
+        outs=[ANY] * 6,
     )
 
 
 def sweep_kernel(
     offsets_ref, upper_offsets_ref, lower_offsets_ref,
     vectors_ref, own_ref, upper_ref, lower_ref,
-    out_ref, mine_ref, next_ref, last_ref, far_ref,
+    out_ref, mine_ref, next_ref, last_ref, one_ref, two_ref,
     state_ref, pairs_ref, rounded_ref,
 ):
     sweeps, spans, refl, band = vectors_ref.shape
@@ -193,8 +243,14 @@
             return carry
 
         lax.fori_loop(0, spans, from_upper, 0)
-        for at in range(spans):
-            apply_span(left + offsets_ref[sweep, at], pairs_ref[sweep * 3 + 1, at], state_ref)
+        for at in range(0, spans, GROUP):
+            group = range(at, at + GROUP)
+            apply_in_order(
+                [left + offsets_ref[sweep, k] for k in group],
+                pairs_ref,
+                [(sweep * 3 + 1, k) for k in group],
+                state_ref,
+            )
         if sweep < sweeps - 1:
             lax.fori_loop(0, spans, from_lower, 0)
     out_ref[...] = state_ref[:, left : left + columns]
@@ -202,9 +258,14 @@
     rounded_ref[:, 0:columns] = state_ref[:, left : left + columns].astype(BF16)
     rounded_ref[:, columns:] = jnp.zeros((rows, padded - columns), BF16)
     cut = mine_ref.shape[1]
-    for step, ref in ((0, mine_ref), (PEERS[0], next_ref), (PEERS[1], last_ref), (PEERS[2], far_ref)):
+    half = rows // 2
+    targets = (
+        (0, 0, mine_ref), (PEERS[0], 0, next_ref), (PEERS[1], 0, last_ref),
+        (PEERS[2], 0, one_ref), (PEERS[2], half, two_ref),
+    )
+    for step, row, ref in targets:
         at = pl.multiple_of((lax.axis_index("x") + step) % X_SIZE * cut, LANE)
-        ref[...] = rounded_ref[:, pl.ds(at, cut)]
+        ref[...] = rounded_ref[row : row + ref.shape[0], pl.ds(at, cut)]
 
 
 def sweep_all(eigen, vectors, offsets, down, up, cut):
@@ -219,7 +280,7 @@
     return call(
         sweep_kernel,
         [jax.ShapeDtypeStruct(eigen.shape, F32)]
-        + [jax.ShapeDtypeStruct((rows, cut), BF16)] * 4,
+        + piece_shapes(rows, cut),
         [SM] * 3 + [VM] * 4,
         (offsets, upper_offsets, lower_offsets, vectors, eigen, upper, lower),
         [
@@ -258,8 +319,8 @@
 
 
 def products_kernel(*refs, spots, own, rows):
-    blocks, (mine, one, two, far) = refs[: len(spots)], refs[len(spots) : len(spots) + 4]
-    ordered_ref, sums_ref, eigen_ref = refs[len(spots) + 4 :]
+    blocks, (mine, one, two, half0, half1) = refs[: len(spots)], refs[len(spots) : len(spots) + 5]
+    ordered_ref, sums_ref, eigen_ref = refs[len(spots) + 5 :]
     order = ordered_ref.shape[0]
     x, z = lax.axis_index("x"), lax.axis_index("z")
     for ref, units in zip(blocks, spots):
@@ -267,8 +328,9 @@
             source = (x + X_SIZE - back_x) % X_SIZE * Z_SIZE + (z + Z_SIZE - back_z) % Z_SIZE
             to = pl.multiple_of(panel * (order // 2) + source * own, UNIT)
             ordered_ref[pl.ds(to, own), :] = ref[at * own : (at + 1) * own, :]
-    for back, ref in ((0, mine), (1, one), (3, two), (2, far)):
-        to = pl.multiple_of((x + X_SIZE - back) % X_SIZE * rows, UNIT)
+    sources = ((0, 0, mine), (1, 0, one), (3, 0, two), (2, 0, half0), (2, rows // 2, half1))
+    for back, row, ref in sources:
+        to = pl.multiple_of((x + X_SIZE - back) % X_SIZE * rows + row, UNIT)
         eigen_ref[pl.ds(to, ref.shape[0]), :] = ref[...]
 
     def put(value, at):

time: 113 us -> 116 us (1.027)
  waiting for transfers between devices: 17.2 us -> 25.4 us
  starting transfers between devices: 43.7 us -> 40.3 us
    ppermute x24 -> x25, waiting for transfers between devices: 17.2 us -> 25.3 us  [shifted(): lax.ppermute(value, axis, [(at, (at + steps) % count) for at in range(cou...]
    ppermute x24 -> x25, starting transfers between devices: 37.2 us -> 33.8 us  [shifted(): lax.ppermute(value, axis, [(at, (at + steps) % count) for at in range(cou...]
  transfers between devices with their start and end apart: 26 -> 27, of which waited for: 9 -> 10; matrix products, arithmetic and copies ran while one was open for 1% -> 1% of each run, Pallas kernels for 3% -> 3%
where the time goes in v4:
time: 116 us
  starting transfers between devices  40.3 us (35%)
  blocking collectives  35 us (30%)
  waiting for transfers between devices  25.4 us (22%)
  Pallas kernels  13.8 us (12%)
    all_to_all x2, blocking collectives, exchange(): return lax.all_to_all(pieces, axes, 0, 0, tiled=True)  35 us
    ppermute x25, starting transfers between devices, shifted(): lax.ppermute(value, axis, [(at, (at + steps) % count) for at in range(cou...  33.8 us
    ppermute x25, waiting for transfers between devices, shifted(): lax.ppermute(value, axis, [(at, (at + steps) % count) for at in range(cou...  25.3 us
    pallas_call x6, Pallas kernels, call(): pl.pallas_call(kernel, out_shape=out_shape, in_specs=in_specs, out_specs=...  13.8 us
    ppermute x2, starting transfers between devices, from_behind(): lax.ppermute(value, axis, [(source, source + steps) for source in range(f...  6.51 us
  transfers between devices with their start and end apart: 27, of which 10 were waited for; matrix products, arithmetic and copies ran while one was open for 1% of the time, Pallas kernels for 3%

profile of v4, /device:TPU:1, one launch (start us, length us, event | category | flops | bytes accessed | tf_op | source)
XLA Modules:
  0.0 115.6 jit_solution(9389754083303369621)
XLA Ops:
  0.0 2.9 %shard_map.46 = (bf16[16,3200]{1,0:T(8,128)(2,1)}, bf16[16,3200]{1,0:T(8,128)(2,1)}, bf16[16,3200]{1,0:T(8,128)(2,1)}, bf16[16,3200]{1,0:T(8,128)(2,1)}, f32[32,2432]{1,0:T(8,128)}, /*index=5*/f32[32,1408]{1,0:T(8,128)}) custom-call(s32[2,8]{1,0:T(2,128)} %offsets_ref.3, f32[2,8,4,128]{3,2,1,0:T(4,128)} %vectors_ref.3, bf16[2,8,12544]{2,1,0:T(8,128)(2,1)} %panels_ref.1, ...), custom_call_target="tpu_custom_call" | custom-call | flops 200704 | bytes 802816 | tf_op jit(solution)/shard_map/pallas_call | solution.py:29
  2.9 2.1 %collective-permute-start.2 = (bf16[16,3200]{1,0:T(8,128)(2,1)}, bf16[16,3200]{1,0:T(8,128)(2,1)S(1)}, u32[]{:S(2)}, u32[]{:S(2)}) collective-permute-start(bf16[16,3200]{1,0:T(8,128)(2,1)} %get-tuple-element.28), channel_id=1, source_target_pairs={{0,8},{8,16},{16,24},{24,0},{1,9},{9,17},{17,25},{25,1},{2,10},{10... | collective-permute-start | bytes 307208 | tf_op jit(solution)/shard_map/ppermute | solution.py:42
  5.0 1.4 %collective-permute-start.10 = (bf16[16,3200]{1,0:T(8,128)(2,1)}, bf16[16,3200]{1,0:T(8,128)(2,1)S(1)}, u32[]{:S(2)}, u32[]{:S(2)}) collective-permute-start(bf16[16,3200]{1,0:T(8,128)(2,1)} %get-tuple-element.29), channel_id=1, source_target_pairs={{0,24},{8,0},{16,8},{24,16},{1,25},{9,1},{17,9},{25,17},{2,26},{10... | collective-permute-start | bytes 307208 | tf_op jit(solution)/shard_map/ppermute | solution.py:42
  6.4 1.6 %collective-permute-start.11 = (bf16[16,3200]{1,0:T(8,128)(2,1)}, bf16[16,3200]{1,0:T(8,128)(2,1)S(1)}, u32[]{:S(2)}, u32[]{:S(2)}) collective-permute-start(bf16[16,3200]{1,0:T(8,128)(2,1)} %get-tuple-element.30), channel_id=1, source_target_pairs={{0,16},{8,24},{16,0},{24,8},{1,17},{9,25},{17,1},{25,9},{2,18},{10... | collective-permute-start | bytes 307208 | tf_op jit(solution)/shard_map/ppermute | solution.py:42
  8.0 3.4 %collective-permute-start.1 = (f32[32,1408]{1,0:T(8,128)}, f32[32,1408]{1,0:T(8,128)S(1)}, u32[]{:S(2)}, u32[]{:S(2)}) collective-permute-start(f32[32,1408]{1,0:T(8,128)} %get-tuple-element.25), channel_id=1, source_target_pairs={{32,0},{64,32},{96,64},{128,96},{160,128},{192,160},{224,192},{33,... | collective-permute-start | bytes 540680 | tf_op jit(solution)/shard_map/ppermute | solution.py:48
  11.5 3.1 %collective-permute-start = (f32[32,2432]{1,0:T(8,128)}, f32[32,2432]{1,0:T(8,128)S(1)}, u32[]{:S(2)}, u32[]{:S(2)}) collective-permute-start(f32[32,2432]{1,0:T(8,128)} %get-tuple-element.24), channel_id=1, source_target_pairs={{0,32},{32,64},{64,96},{96,128},{128,160},{160,192},{192,224},{1,3... | collective-permute-start | bytes 933896 | tf_op jit(solution)/shard_map/ppermute | solution.py:48
  14.6 0.9 constant_dynamic-update-slice_fusion.1
  15.5 5.7 %collective-permute-start.4 = (bf16[32,3200]{1,0:T(8,128)(2,1)S(1)}, bf16[32,3200]{1,0:T(8,128)(2,1)S(1)}, u32[]{:S(2)}, u32[]{:S(2)}) collective-permute-start(bf16[32,3200]{1,0:T(8,128)(2,1)S(1)} %constant_dynamic-update-slice_fusion.refs_0_), channel_id=1, source_target_pairs={{0,7},{1,0},{2,1},{3,2},{4,3},{5,4},{6,5},{7,6},{8,15},{9,8},{10,9... | collective-permute-start | bytes 614408 | tf_op jit(solution)/shard_map/ppermute | solution.py:42
  21.2 2.7 %collective-permute-start.13 = (bf16[32,3200]{1,0:T(8,128)(2,1)S(1)}, bf16[32,3200]{1,0:T(8,128)(2,1)S(1)}, u32[]{:S(2)}, u32[]{:S(2)}) collective-permute-start(bf16[32,3200]{1,0:T(8,128)(2,1)S(1)} %constant_dynamic-update-slice_fusion.2.refs_8_), channel_id=1, source_target_pairs={{0,7},{1,0},{2,1},{3,2},{4,3},{5,4},{6,5},{7,6},{8,15},{9,8},{10,9... | collective-permute-start | bytes 614408 | tf_op jit(solution)/shard_map/ppermute | solution.py:42
  24.0 5.4 %collective-permute-done.3.refs_1_ = bf16[32,3200]{1,0:T(8,128)(2,1)S(1)} collective-permute-done((bf16[32,3200]{1,0:T(8,128)(2,1)S(1)}, bf16[32,3200]{1,0:T(8,128)(2,1)S(1)}, u32[]{:S(2)}, u32[]{:S(2)}) %collective-permute-start.3) | collective-permute-done | bytes 204832 | tf_op jit(solution)/shard_map/ppermute | solution.py:42
  30.2 3.2 %collective-permute-start.15 = (bf16[32,3200]{1,0:T(8,128)(2,1)S(1)}, bf16[32,3200]{1,0:T(8,128)(2,1)S(1)}, u32[]{:S(2)}, u32[]{:S(2)}) collective-permute-start(bf16[32,3200]{1,0:T(8,128)(2,1)S(1)} %collective-permute-done.13.refs_10_), channel_id=1, source_target_pairs={{0,7},{1,0},{2,1},{3,2},{4,3},{5,4},{6,5},{7,6},{8,15},{9,8},{10,9... | collective-permute-start | bytes 614408 | tf_op jit(solution)/shard_map/ppermute | solution.py:42
  33.5 2.9 %shard_map.47 = (f32[32,12544]{1,0:T(8,128)S(1)}, bf16[32,3200]{1,0:T(8,128)(2,1)S(1)}, bf16[32,3200]{1,0:T(8,128)(2,1)S(1)}, bf16[32,3200]{1,0:T(8,128)(2,1)S(1...) custom-call(s32[2,8]{1,0:T(2,128)S(1)} %copy-done.2, s32[2,8]{1,0:T(2,128)S(1)} %slice_convert_fusion.1.upper_offsets_ref, ...), custom_call_target="tpu_custom_call" | custom-call | flops 16056320 | bytes 4816896 | tf_op jit(solution)/shard_map/pallas_call | solution.py:29
  36.4 1.5 %collective-permute-start.21 = (bf16[16,3200]{1,0:T(8,128)(2,1)S(1)}, bf16[16,3200]{1,0:T(8,128)(2,1)S(1)}, u32[]{:S(2)}, u32[]{:S(2)}) collective-permute-start(bf16[16,3200]{1,0:T(8,128)(2,1)S(1)} %get-tuple-element.34), channel_id=1, source_target_pairs={{0,16},{8,24},{16,0},{24,8},{1,17},{9,25},{17,1},{25,9},{2,18},{10... | collective-permute-start | bytes 307208 | tf_op jit(solution)/shard_map/ppermute | solution.py:42
  37.9 1.5 %collective-permute-start.22 = (bf16[16,3200]{1,0:T(8,128)(2,1)S(1)}, bf16[16,3200]{1,0:T(8,128)(2,1)S(1)}, u32[]{:S(2)}, u32[]{:S(2)}) collective-permute-start(bf16[16,3200]{1,0:T(8,128)(2,1)S(1)} %get-tuple-element.35), channel_id=1, source_target_pairs={{0,16},{8,24},{16,0},{24,8},{1,17},{9,25},{17,1},{25,9},{2,18},{10... | collective-permute-start | bytes 307208 | tf_op jit(solution)/shard_map/ppermute | solution.py:42
  39.5 2.5 %collective-permute-done.21.refs_19_ = bf16[16,3200]{1,0:T(8,128)(2,1)S(1)} collective-permute-done((bf16[16,3200]{1,0:T(8,128)(2,1)S(1)}, bf16[16,3200]{1,0:T(8,128)(2,1)S(1)}, u32[]{:S(2)}, u32[]{:S(2)}) %collective-permute-start.21) | collective-permute-done | bytes 102432 | tf_op jit(solution)/shard_map/ppermute | solution.py:42
  41.9 2.4 %collective-permute-done.22.refs_20_ = bf16[16,3200]{1,0:T(8,128)(2,1)S(1)} collective-permute-done((bf16[16,3200]{1,0:T(8,128)(2,1)S(1)}, bf16[16,3200]{1,0:T(8,128)(2,1)S(1)}, u32[]{:S(2)}, u32[]{:S(2)}) %collective-permute-start.22) | collective-permute-done | bytes 102432 | tf_op jit(solution)/shard_map/ppermute | solution.py:42
  44.4 2.7 %collective-permute-start.17 = (bf16[32,3200]{1,0:T(8,128)(2,1)S(1)}, bf16[32,3200]{1,0:T(8,128)(2,1)S(1)}, u32[]{:S(2)}, u32[]{:S(2)}) collective-permute-start(bf16[32,3200]{1,0:T(8,128)(2,1)S(1)} %collective-permute-done.15.refs_12_), channel_id=1, source_target_pairs={{0,7},{1,0},{2,1},{3,2},{4,3},{5,4},{6,5},{7,6},{8,15},{9,8},{10,9... | collective-permute-start | bytes 614408 | tf_op jit(solution)/shard_map/ppermute | solution.py:42
  47.1 2.6 %collective-permute-start.20 = (bf16[32,3200]{1,0:T(8,128)(2,1)S(1)}, bf16[32,3200]{1,0:T(8,128)(2,1)S(1)}, u32[]{:S(2)}, u32[]{:S(2)}) collective-permute-start(bf16[32,3200]{1,0:T(8,128)(2,1)S(1)} %get-tuple-element.33), channel_id=1, source_target_pairs={{0,24},{8,0},{16,8},{24,16},{1,25},{9,1},{17,9},{25,17},{2,26},{10... | collective-permute-start | bytes 614408 | tf_op jit(solution)/shard_map/ppermute | solution.py:42
  49.8 1.2 %collective-permute-done.19.refs_17_ = bf16[32,3200]{1,0:T(8,128)(2,1)S(1)} collective-permute-done((bf16[32,3200]{1,0:T(8,128)(2,1)S(1)}, bf16[32,3200]{1,0:T(8,128)(2,1)S(1)}, u32[]{:S(2)}, u32[]{:S(2)}) %collective-permute-start.19) | collective-permute-done | bytes 204832 | tf_op jit(solution)/shard_map/ppermute | solution.py:42
  51.2 1.5 %collective-permute-done.7.refs_5_ = bf16[32,3200]{1,0:T(8,128)(2,1)S(1)} collective-permute-done((bf16[32,3200]{1,0:T(8,128)(2,1)S(1)}, bf16[32,3200]{1,0:T(8,128)(2,1)S(1)}, u32[]{:S(2)}, u32[]{:S(2)}) %collective-permute-start.7) | collective-permute-done | bytes 204832 | tf_op jit(solution)/shard_map/ppermute | solution.py:42
  52.7 2.7 %collective-permute-start.18 = (bf16[32,3200]{1,0:T(8,128)(2,1)S(1)}, bf16[32,3200]{1,0:T(8,128)(2,1)S(1)}, u32[]{:S(2)}, u32[]{:S(2)}) collective-permute-start(bf16[32,3200]{1,0:T(8,128)(2,1)S(1)} %collective-permute-done.17.refs_14_), channel_id=1, source_target_pairs={{0,7},{1,0},{2,1},{3,2},{4,3},{5,4},{6,5},{7,6},{8,15},{9,8},{10,9... | collective-permute-start | bytes 614408 | tf_op jit(solution)/shard_map/ppermute | solution.py:42
  55.4 1.5 %collective-permute-done.16.refs_13_ = bf16[32,3200]{1,0:T(8,128)(2,1)S(1)} collective-permute-done((bf16[32,3200]{1,0:T(8,128)(2,1)S(1)}, bf16[32,3200]{1,0:T(8,128)(2,1)S(1)}, u32[]{:S(2)}, u32[]{:S(2)}) %collective-permute-start.16) | collective-permute-done | bytes 204832 | tf_op jit(solution)/shard_map/ppermute | solution.py:42
  56.8 4.3 %collective-permute-done.9.refs_7_ = bf16[32,3200]{1,0:T(8,128)(2,1)S(1)} collective-permute-done((bf16[32,3200]{1,0:T(8,128)(2,1)S(1)}, bf16[32,3200]{1,0:T(8,128)(2,1)S(1)}, u32[]{:S(2)}, u32[]{:S(2)}) %collective-permute-start.9) | collective-permute-done | bytes 204832 | tf_op jit(solution)/shard_map/ppermute | solution.py:42
  61.1 2.6 %shard_map.48 = (bf16[512,3200]{1,0:T(8,128)(2,1)S(1)}, bf16[1792,128]{1,0:T(8,128)(2,1)S(1)}) custom-call(bf16[32,3200]{1,0:T(8,128)(2,1)S(1)} %constant_dynamic-update-slice_fusion.refs_0_, bf16[32,3200]{1,0:T(8,128)(2,1)S(1)} %collective-permute-done.3.refs_1_, bf16[32,3200]{1,0:T(8,128)(2,1)S(1)} %collective-permute-done.4.refs_2_, ...), custom_call_target="tpu_custom_call" | custom-call | flops 2097152000 | bytes 9830400 | tf_op jit(solution)/shard_map/pallas_call | solution.py:29
  63.8 20.1 %all_to_all.10.parts_ref = bf16[32,56,128]{2,1,0:T(8,128)(2,1)S(1)} all-to-all(bf16[32,56,128]{2,1,0:T(8,128)(2,1)S(1)} %bitcast.3), channel_id=1, replica_groups=mesh['row'=8,'x'=4,'z'=8] {'row','x'}, dimensions={0} | all-to-all | bytes 917504 | tf_op jit(solution)/shard_map/all_to_all | solution.py:533
  84.0 14.8 %all_to_all.11 = bf16[32,56,128]{2,1,0:T(8,128)(2,1)S(1)} all-to-all(bf16[32,56,128]{2,1,0:T(8,128)(2,1)S(1)} %shard_map.49), channel_id=1, replica_groups=mesh['row'=8,'x'=4,'z'=8] {'row','x'}, dimensions={0} | all-to-all | bytes 917504 | tf_op jit(solution)/shard_map/all_to_all | solution.py:533
  98.8 4.0 %shard_map.50 = (bf16[32,3200]{1,0:T(8,128)(2,1)S(1)}, bf16[32,3200]{1,0:T(8,128)(2,1)S(1)}, bf16[32,3200]{1,0:T(8,128)(2,1)S(1)}, bf16[16,3200]{1,0:T(8,128)(2,1)S(1)}, bf16[16,3200]{1,0:T(8,128)(2,1)S(1)}) custom-call(bf16[1792,128]{1,0:T(8,128)(2,1)S(1)} %bitcast.2, bf16[512,3200]{1,0:T(8,128)(2,1)S(1)} %get-tuple-element.37.ordered_ref), custom_call_target="tpu_custom_call" | custom-call | flops 419430400 | bytes 6553600 | tf_op jit(solution)/shard_map/pallas_call | solution.py:29
  103.2 2.4 %collective-permute-start.24 = (bf16[32,3200]{1,0:T(8,128)(2,1)S(1)}, bf16[32,3200]{1,0:T(8,128)(2,1)S(1)}, u32[]{:S(2)}, u32[]{:S(2)}) collective-permute-start(bf16[32,3200]{1,0:T(8,128)(2,1)S(1)} %get-tuple-element.40), channel_id=1, source_target_pairs={{0,24},{8,0},{16,8},{24,16},{1,25},{9,1},{17,9},{25,17},{2,26},{10... | collective-permute-start | bytes 614408 | tf_op jit(solution)/shard_map/ppermute | solution.py:42
  105.6 3.0 %collective-permute-start.26 = (bf16[16,3200]{1,0:T(8,128)(2,1)S(1)}, bf16[16,3200]{1,0:T(8,128)(2,1)S(1)}, u32[]{:S(2)}, u32[]{:S(2)}) collective-permute-start(bf16[16,3200]{1,0:T(8,128)(2,1)S(1)} %get-tuple-element.42), channel_id=1, source_target_pairs={{0,16},{8,24},{16,0},{24,8},{1,17},{9,25},{17,1},{25,9},{2,18},{10... | collective-permute-start | bytes 307208 | tf_op jit(solution)/shard_map/ppermute | solution.py:42
  108.5 3.4 %collective-permute-done.25.half0 = bf16[16,3200]{1,0:T(8,128)(2,1)S(1)} collective-permute-done((bf16[16,3200]{1,0:T(8,128)(2,1)S(1)}, bf16[16,3200]{1,0:T(8,128)(2,1)S(1)}, u32[]{:S(2)}, u32[]{:S(2)}) %collective-permute-start.25) | collective-permute-done | bytes 102432 | tf_op jit(solution)/shard_map/ppermute | solution.py:42
  112.0 2.2 %collective-permute-done.26.half1 = bf16[16,3200]{1,0:T(8,128)(2,1)S(1)} collective-permute-done((bf16[16,3200]{1,0:T(8,128)(2,1)S(1)}, bf16[16,3200]{1,0:T(8,128)(2,1)S(1)}, u32[]{:S(2)}, u32[]{:S(2)}) %collective-permute-start.26) | collective-permute-done | bytes 102432 | tf_op jit(solution)/shard_map/ppermute | solution.py:42
  114.2 1.2 %shard_map.51 = f32[32,12544]{1,0:T(8,128)} custom-call(f32[32,12544]{1,0:T(8,128)S(1)} %get-tuple-element.26.eigen_ref, bf16[32,3200]{1,0:T(8,128)(2,1)S(1)} %get-tuple-element.38.mine, bf16[32,3200]{1,0:T(8,128)(2,1)S(1)} %collective-permute-done.23.one, bf16[32,3200]{1,0:T(8,128)(2,1)S(1)} %collective-permute-done.24.two, ...), custom_call_target="tpu_custom_call" | custom-call | flops 401408 | bytes 4014080 | tf_op jit(solution)/shard_map/pallas_call | solution.py:29
  (42 shorter events, 1.7 us)
Async XLA Ops:
  0.0 33.4 %copy-start.2 = (s32[2,8]{1,0:T(2,128)S(1)}, s32[2,8]{1,0:T(2,128)}, u32[]{:S(2)}) copy-start(s32[2,8]{1,0:T(2,128)} %offsets_ref.3) | copy-start | bytes 196
  0.0 33.4 %copy-start.1 = (f32[2,8,4,128]{3,2,1,0:T(4,128)S(1)}, f32[2,8,4,128]{3,2,1,0:T(4,128)}, u32[]{:S(2)}) copy-start(f32[2,8,4,128]{3,2,1,0:T(4,128)} %vectors_ref.3) | copy-start | bytes 98308
  0.0 33.4 %copy-start = (f32[32,12544]{1,0:T(8,128)S(1)}, f32[32,12544]{1,0:T(8,128)}, u32[]{:S(2)}) copy-start(f32[32,12544]{1,0:T(8,128)} %own_ref.1) | copy-start | bytes 4816900
  2.9 12.5 %collective-permute-start.2 = (bf16[16,3200]{1,0:T(8,128)(2,1)}, bf16[16,3200]{1,0:T(8,128)(2,1)S(1)}, u32[]{:S(2)}, u32[]{:S(2)}) collective-permute-start(bf16[16,3200]{1,0:T(8,128)(2,1)} %get-tuple-element.28), channel_id=1, source_target_pairs={{0,8},{8,16},{16,24},{24,0},{1,9},{9,17},{17,25},{25,1},{2,10},{10... | collective-permute-start | bytes 307208 | tf_op jit(solution)/shard_map/ppermute | solution.py:42
  5.0 16.1 %collective-permute-start.10 = (bf16[16,3200]{1,0:T(8,128)(2,1)}, bf16[16,3200]{1,0:T(8,128)(2,1)S(1)}, u32[]{:S(2)}, u32[]{:S(2)}) collective-permute-start(bf16[16,3200]{1,0:T(8,128)(2,1)} %get-tuple-element.29), channel_id=1, source_target_pairs={{0,24},{8,0},{16,8},{24,16},{1,25},{9,1},{17,9},{25,17},{2,26},{10... | collective-permute-start | bytes 307208 | tf_op jit(solution)/shard_map/ppermute | solution.py:42
  6.4 14.8 %collective-permute-start.11 = (bf16[16,3200]{1,0:T(8,128)(2,1)}, bf16[16,3200]{1,0:T(8,128)(2,1)S(1)}, u32[]{:S(2)}, u32[]{:S(2)}) collective-permute-start(bf16[16,3200]{1,0:T(8,128)(2,1)} %get-tuple-element.30), channel_id=1, source_target_pairs={{0,16},{8,24},{16,0},{24,8},{1,17},{9,25},{17,1},{25,9},{2,18},{10... | collective-permute-start | bytes 307208 | tf_op jit(solution)/shard_map/ppermute | solution.py:42
  8.0 15.9 %collective-permute-start.1 = (f32[32,1408]{1,0:T(8,128)}, f32[32,1408]{1,0:T(8,128)S(1)}, u32[]{:S(2)}, u32[]{:S(2)}) collective-permute-start(f32[32,1408]{1,0:T(8,128)} %get-tuple-element.25), channel_id=1, source_target_pairs={{32,0},{64,32},{96,64},{128,96},{160,128},{192,160},{224,192},{33,... | collective-permute-start | bytes 540680 | tf_op jit(solution)/shard_map/ppermute | solution.py:48
  11.5 22.0 %collective-permute-start = (f32[32,2432]{1,0:T(8,128)}, f32[32,2432]{1,0:T(8,128)S(1)}, u32[]{:S(2)}, u32[]{:S(2)}) collective-permute-start(f32[32,2432]{1,0:T(8,128)} %get-tuple-element.24), channel_id=1, source_target_pairs={{0,32},{32,64},{64,96},{96,128},{128,160},{160,192},{192,224},{1,3... | collective-permute-start | bytes 933896 | tf_op jit(solution)/shard_map/ppermute | solution.py:48
  15.5 22.4 %collective-permute-start.4 = (bf16[32,3200]{1,0:T(8,128)(2,1)S(1)}, bf16[32,3200]{1,0:T(8,128)(2,1)S(1)}, u32[]{:S(2)}, u32[]{:S(2)}) collective-permute-start(bf16[32,3200]{1,0:T(8,128)(2,1)S(1)} %constant_dynamic-update-slice_fusion.refs_0_), channel_id=1, source_target_pairs={{0,7},{1,0},{2,1},{3,2},{4,3},{5,4},{6,5},{7,6},{8,15},{9,8},{10,9... | collective-permute-start | bytes 614408 | tf_op jit(solution)/shard_map/ppermute | solution.py:42
  21.2 8.2 %collective-permute-start.3 = (bf16[32,3200]{1,0:T(8,128)(2,1)S(1)}, bf16[32,3200]{1,0:T(8,128)(2,1)S(1)}, u32[]{:S(2)}, u32[]{:S(2)}) collective-permute-start(bf16[32,3200]{1,0:T(8,128)(2,1)S(1)} %constant_dynamic-update-slice_fusion.refs_0_), channel_id=1, source_target_pairs={{0,1},{1,2},{2,3},{3,4},{4,5},{5,6},{6,7},{7,0},{8,9},{9,10},{10,1... | collective-permute-start | bytes 614408 | tf_op jit(solution)/shard_map/ppermute | solution.py:42
  21.2 9.0 %collective-permute-start.13 = (bf16[32,3200]{1,0:T(8,128)(2,1)S(1)}, bf16[32,3200]{1,0:T(8,128)(2,1)S(1)}, u32[]{:S(2)}, u32[]{:S(2)}) collective-permute-start(bf16[32,3200]{1,0:T(8,128)(2,1)S(1)} %constant_dynamic-update-slice_fusion.2.refs_8_), channel_id=1, source_target_pairs={{0,7},{1,0},{2,1},{3,2},{4,3},{5,4},{6,5},{7,6},{8,15},{9,8},{10,9... | collective-permute-start | bytes 614408 | tf_op jit(solution)/shard_map/ppermute | solution.py:42
  23.9 15.5 %collective-permute-start.12 = (bf16[32,3200]{1,0:T(8,128)(2,1)S(1)}, bf16[32,3200]{1,0:T(8,128)(2,1)S(1)}, u32[]{:S(2)}, u32[]{:S(2)}) collective-permute-start(bf16[32,3200]{1,0:T(8,128)(2,1)S(1)} %constant_dynamic-update-slice_fusion.2.refs_8_), channel_id=1, source_target_pairs={{0,1},{1,2},{2,3},{3,4},{4,5},{5,6},{6,7},{7,0},{8,9},{9,10},{10,1... | collective-permute-start | bytes 614408 | tf_op jit(solution)/shard_map/ppermute | solution.py:42
  29.4 15.0 %collective-permute-start.5 = (bf16[32,3200]{1,0:T(8,128)(2,1)S(1)}, bf16[32,3200]{1,0:T(8,128)(2,1)S(1)}, u32[]{:S(2)}, u32[]{:S(2)}) collective-permute-start(bf16[32,3200]{1,0:T(8,128)(2,1)S(1)} %collective-permute-done.3.refs_1_), channel_id=1, source_target_pairs={{0,1},{1,2},{2,3},{3,4},{4,5},{5,6},{6,7},{7,0},{8,9},{9,10},{10,1... | collective-permute-start | bytes 614408 | tf_op jit(solution)/shard_map/ppermute | solution.py:42
  30.2 14.2 %collective-permute-start.15 = (bf16[32,3200]{1,0:T(8,128)(2,1)S(1)}, bf16[32,3200]{1,0:T(8,128)(2,1)S(1)}, u32[]{:S(2)}, u32[]{:S(2)}) collective-permute-start(bf16[32,3200]{1,0:T(8,128)(2,1)S(1)} %collective-permute-done.13.refs_10_), channel_id=1, source_target_pairs={{0,7},{1,0},{2,1},{3,2},{4,3},{5,4},{6,5},{7,6},{8,15},{9,8},{10,9... | collective-permute-start | bytes 614408 | tf_op jit(solution)/shard_map/ppermute | solution.py:42
  36.4 5.5 %collective-permute-start.21 = (bf16[16,3200]{1,0:T(8,128)(2,1)S(1)}, bf16[16,3200]{1,0:T(8,128)(2,1)S(1)}, u32[]{:S(2)}, u32[]{:S(2)}) collective-permute-start(bf16[16,3200]{1,0:T(8,128)(2,1)S(1)} %get-tuple-element.34), channel_id=1, source_target_pairs={{0,16},{8,24},{16,0},{24,8},{1,17},{9,25},{17,1},{25,9},{2,18},{10... | collective-permute-start | bytes 307208 | tf_op jit(solution)/shard_map/ppermute | solution.py:42
  37.9 6.4 %collective-permute-start.22 = (bf16[16,3200]{1,0:T(8,128)(2,1)S(1)}, bf16[16,3200]{1,0:T(8,128)(2,1)S(1)}, u32[]{:S(2)}, u32[]{:S(2)}) collective-permute-start(bf16[16,3200]{1,0:T(8,128)(2,1)S(1)} %get-tuple-element.35), channel_id=1, source_target_pairs={{0,16},{8,24},{16,0},{24,8},{1,17},{9,25},{17,1},{25,9},{2,18},{10... | collective-permute-start | bytes 307208 | tf_op jit(solution)/shard_map/ppermute | solution.py:42
  39.5 7.7 %collective-permute-start.6 = (bf16[32,3200]{1,0:T(8,128)(2,1)S(1)}, bf16[32,3200]{1,0:T(8,128)(2,1)S(1)}, u32[]{:S(2)}, u32[]{:S(2)}) collective-permute-start(bf16[32,3200]{1,0:T(8,128)(2,1)S(1)} %collective-permute-done.4.refs_2_), channel_id=1, source_target_pairs={{0,7},{1,0},{2,1},{3,2},{4,3},{5,4},{6,5},{7,6},{8,15},{9,8},{10,9... | collective-permute-start | bytes 614408 | tf_op jit(solution)/shard_map/ppermute | solution.py:42
  41.9 7.8 %collective-permute-start.14 = (bf16[32,3200]{1,0:T(8,128)(2,1)S(1)}, bf16[32,3200]{1,0:T(8,128)(2,1)S(1)}, u32[]{:S(2)}, u32[]{:S(2)}) collective-permute-start(bf16[32,3200]{1,0:T(8,128)(2,1)S(1)} %collective-permute-done.12.refs_9_), channel_id=1, source_target_pairs={{0,1},{1,2},{2,3},{3,4},{4,5},{5,6},{6,7},{7,0},{8,9},{9,10},{10,1... | collective-permute-start | bytes 614408 | tf_op jit(solution)/shard_map/ppermute | solution.py:42
  44.3 6.7 %collective-permute-start.19 = (bf16[32,3200]{1,0:T(8,128)(2,1)S(1)}, bf16[32,3200]{1,0:T(8,128)(2,1)S(1)}, u32[]{:S(2)}, u32[]{:S(2)}) collective-permute-start(bf16[32,3200]{1,0:T(8,128)(2,1)S(1)} %get-tuple-element.32), channel_id=1, source_target_pairs={{0,8},{8,16},{16,24},{24,0},{1,9},{9,17},{17,25},{25,1},{2,10},{10... | collective-permute-start | bytes 614408 | tf_op jit(solution)/shard_map/ppermute | solution.py:42
  44.4 8.2 %collective-permute-start.7 = (bf16[32,3200]{1,0:T(8,128)(2,1)S(1)}, bf16[32,3200]{1,0:T(8,128)(2,1)S(1)}, u32[]{:S(2)}, u32[]{:S(2)}) collective-permute-start(bf16[32,3200]{1,0:T(8,128)(2,1)S(1)} %collective-permute-done.5.refs_3_), channel_id=1, source_target_pairs={{0,1},{1,2},{2,3},{3,4},{4,5},{5,6},{6,7},{7,0},{8,9},{9,10},{10,1... | collective-permute-start | bytes 614408 | tf_op jit(solution)/shard_map/ppermute | solution.py:42
  44.4 8.2 %collective-permute-start.17 = (bf16[32,3200]{1,0:T(8,128)(2,1)S(1)}, bf16[32,3200]{1,0:T(8,128)(2,1)S(1)}, u32[]{:S(2)}, u32[]{:S(2)}) collective-permute-start(bf16[32,3200]{1,0:T(8,128)(2,1)S(1)} %collective-permute-done.15.refs_12_), channel_id=1, source_target_pairs={{0,7},{1,0},{2,1},{3,2},{4,3},{5,4},{6,5},{7,6},{8,15},{9,8},{10,9... | collective-permute-start | bytes 614408 | tf_op jit(solution)/shard_map/ppermute | solution.py:42
  47.1 8.2 %collective-permute-start.20 = (bf16[32,3200]{1,0:T(8,128)(2,1)S(1)}, bf16[32,3200]{1,0:T(8,128)(2,1)S(1)}, u32[]{:S(2)}, u32[]{:S(2)}) collective-permute-start(bf16[32,3200]{1,0:T(8,128)(2,1)S(1)} %get-tuple-element.33), channel_id=1, source_target_pairs={{0,24},{8,0},{16,8},{24,16},{1,25},{9,1},{17,9},{25,17},{2,26},{10... | collective-permute-start | bytes 614408 | tf_op jit(solution)/shard_map/ppermute | solution.py:42
  49.7 5.7 %collective-permute-start.8 = (bf16[32,3200]{1,0:T(8,128)(2,1)S(1)}, bf16[32,3200]{1,0:T(8,128)(2,1)S(1)}, u32[]{:S(2)}, u32[]{:S(2)}) collective-permute-start(bf16[32,3200]{1,0:T(8,128)(2,1)S(1)} %collective-permute-done.6.refs_4_), channel_id=1, source_target_pairs={{0,7},{1,0},{2,1},{3,2},{4,3},{5,4},{6,5},{7,6},{8,15},{9,8},{10,9... | collective-permute-start | bytes 614408 | tf_op jit(solution)/shard_map/ppermute | solution.py:42
  51.0 5.8 %collective-permute-start.16 = (bf16[32,3200]{1,0:T(8,128)(2,1)S(1)}, bf16[32,3200]{1,0:T(8,128)(2,1)S(1)}, u32[]{:S(2)}, u32[]{:S(2)}) collective-permute-start(bf16[32,3200]{1,0:T(8,128)(2,1)S(1)} %collective-permute-done.14.refs_11_), channel_id=1, source_target_pairs={{0,1},{1,2},{2,3},{3,4},{4,5},{5,6},{6,7},{7,0},{8,9},{9,10},{10,1... | collective-permute-start | bytes 614408 | tf_op jit(solution)/shard_map/ppermute | solution.py:42
  52.7 8.5 %collective-permute-start.9 = (bf16[32,3200]{1,0:T(8,128)(2,1)S(1)}, bf16[32,3200]{1,0:T(8,128)(2,1)S(1)}, u32[]{:S(2)}, u32[]{:S(2)}) collective-permute-start(bf16[32,3200]{1,0:T(8,128)(2,1)S(1)} %collective-permute-done.7.refs_5_), channel_id=1, source_target_pairs={{0,1},{1,2},{2,3},{3,4},{4,5},{5,6},{6,7},{7,0},{8,9},{9,10},{10,1... | collective-permute-start | bytes 614408 | tf_op jit(solution)/shard_map/ppermute | solution.py:42
  52.7 8.5 %collective-permute-start.18 = (bf16[32,3200]{1,0:T(8,128)(2,1)S(1)}, bf16[32,3200]{1,0:T(8,128)(2,1)S(1)}, u32[]{:S(2)}, u32[]{:S(2)}) collective-permute-start(bf16[32,3200]{1,0:T(8,128)(2,1)S(1)} %collective-permute-done.17.refs_14_), channel_id=1, source_target_pairs={{0,7},{1,0},{2,1},{3,2},{4,3},{5,4},{6,5},{7,6},{8,15},{9,8},{10,9... | collective-permute-start | bytes 614408 | tf_op jit(solution)/shard_map/ppermute | solution.py:42
  102.8 11.4 %collective-permute-start.23 = (bf16[32,3200]{1,0:T(8,128)(2,1)S(1)}, bf16[32,3200]{1,0:T(8,128)(2,1)S(1)}, u32[]{:S(2)}, u32[]{:S(2)}) collective-permute-start(bf16[32,3200]{1,0:T(8,128)(2,1)S(1)} %get-tuple-element.39), channel_id=1, source_target_pairs={{0,8},{8,16},{16,24},{24,0},{1,9},{9,17},{17,25},{25,1},{2,10},{10... | collective-permute-start | bytes 614408 | tf_op jit(solution)/shard_map/ppermute | solution.py:42
  103.2 11.0 %collective-permute-start.24 = (bf16[32,3200]{1,0:T(8,128)(2,1)S(1)}, bf16[32,3200]{1,0:T(8,128)(2,1)S(1)}, u32[]{:S(2)}, u32[]{:S(2)}) collective-permute-start(bf16[32,3200]{1,0:T(8,128)(2,1)S(1)} %get-tuple-element.40), channel_id=1, source_target_pairs={{0,24},{8,0},{16,8},{24,16},{1,25},{9,1},{17,9},{25,17},{2,26},{10... | collective-permute-start | bytes 614408 | tf_op jit(solution)/shard_map/ppermute | solution.py:42
  105.6 6.4 %collective-permute-start.25 = (bf16[16,3200]{1,0:T(8,128)(2,1)S(1)}, bf16[16,3200]{1,0:T(8,128)(2,1)S(1)}, u32[]{:S(2)}, u32[]{:S(2)}) collective-permute-start(bf16[16,3200]{1,0:T(8,128)(2,1)S(1)} %get-tuple-element.41), channel_id=1, source_target_pairs={{0,16},{8,24},{16,0},{24,8},{1,17},{9,25},{17,1},{25,9},{2,18},{10... | collective-permute-start | bytes 307208 | tf_op jit(solution)/shard_map/ppermute | solution.py:42
  105.6 8.6 %collective-permute-start.26 = (bf16[16,3200]{1,0:T(8,128)(2,1)S(1)}, bf16[16,3200]{1,0:T(8,128)(2,1)S(1)}, u32[]{:S(2)}, u32[]{:S(2)}) collective-permute-start(bf16[16,3200]{1,0:T(8,128)(2,1)S(1)} %get-tuple-element.42), channel_id=1, source_target_pairs={{0,16},{8,24},{16,0},{24,8},{1,17},{9,25},{17,1},{25,9},{2,18},{10... | collective-permute-start | bytes 307208 | tf_op jit(solution)/shard_map/ppermute | solution.py:42

commit v5 on v4

--- a/solution.py
+++ b/solution.py
@@ -118,7 +118,7 @@
     offsets_ref, vectors_ref, panels_ref, eigen_ref, *refs
 ):
     *piece_refs, down_out, up_out = refs[:6]
-    down_ref, up_ref, wide_ref, sems = refs[6:]
+    down_ref, up_ref, wide_ref, held_vectors_ref, held_offsets_ref, sems = refs[6:]
     sweeps, spans, refl, band = vectors_ref.shape
     rows, columns = eigen_ref.shape
     panels, own, _ = panels_ref.shape
@@ -137,30 +137,37 @@
                 eigen_ref.at[:, begin : begin + width], ref.at[:, 0:width], sems.at[len(moves)]
             )
         )
-    for move in moves:
+    small = [
+        pltpu.make_async_copy(vectors_ref, held_vectors_ref, sems.at[len(moves)]),
+        pltpu.make_async_copy(offsets_ref, held_offsets_ref, sems.at[len(moves) + 1]),
+    ]
+    for move in moves + small:
         move.start()
     wide_ref[:, columns:] = jnp.zeros((panels * own, wide_ref.shape[1] - columns), BF16)
+    leaves = []
+
+    def leave(source, target):
+        leaves.append(pltpu.make_async_copy(source, target, sems.at[len(moves) + 2 + len(leaves)]))
+        leaves[-1].start()
+
+    for move in moves[:panels]:
+        move.wait()
+    for step, ref in zip((*PEERS, 0), (*piece_refs[1:], piece_refs[0])):
+        cut = ref.shape[1]
+        at = pl.multiple_of((lax.axis_index("x") + step) % X_SIZE * cut, LANE)
+        leave(wide_ref.at[:, pl.ds(at, cut)], ref)
+    for move in small:
+        move.wait()
     for ref, _, count in halos:
         width = ref.shape[1] - count * band - LANE
         for sweep in range(count):
             for i in range(refl):
                 ref[i * spans : (i + 1) * spans, width + sweep * band : width + (sweep + 1) * band] = (
-                    vectors_ref[sweep, :, i, :]
+                    held_vectors_ref[sweep, :, i, :]
                 )
         ref[:, width + count * band :] = jnp.zeros((rows, LANE), F32)
-        ref[0:sweeps, width + count * band : width + count * band + spans] = offsets_ref[...].astype(F32)
-    for move in moves[:panels]:
-        move.wait()
-    leaves = []
-
-    def leave(source, target):
-        leaves.append(pltpu.make_async_copy(source, target, sems.at[len(moves) + len(leaves)]))
-        leaves[-1].start()
-
-    for step, ref in zip((0, *PEERS), piece_refs):
-        cut = ref.shape[1]
-        at = pl.multiple_of((lax.axis_index("x") + step) % X_SIZE * cut, LANE)
-        leave(wide_ref.at[:, pl.ds(at, cut)], ref)
+        starts = held_offsets_ref[...].astype(F32)
+        ref[0:sweeps, width + count * band : width + count * band + spans] = starts
     for move, source, target in zip(moves[panels:], (down_ref, up_ref), (down_out, up_out)):
         move.wait()
         leave(source, target)
@@ -183,13 +190,15 @@
         front_kernel,
         [jax.ShapeDtypeStruct((high, cut), BF16)] * 4
         + [wide(left + sweeps * band + LANE), wide(right + (sweeps - 1) * band + LANE)],
-        [VM, VM, ANY, ANY],
+        [ANY] * 4,
         (offsets, vectors, panels, eigen),
         [
             pltpu.VMEM((rows, left + sweeps * band + LANE), F32),
             pltpu.VMEM((rows, right + (sweeps - 1) * band + LANE), F32),
             pltpu.VMEM((high, X_SIZE * cut), BF16),
-            pltpu.SemaphoreType.DMA((panels.shape[0] + 8,)),
+            pltpu.VMEM(vectors.shape, F32),
+            pltpu.VMEM(offsets.shape, jnp.int32),
+            pltpu.SemaphoreType.DMA((panels.shape[0] + 10,)),
         ],
         flops=panels.size,
         size=4 * panels.size,
@@ -428,16 +437,28 @@
     tile = lambda at: sums_ref[at * LANE : (at + 1) * LANE, :]
     gram = lambda i, j: tile(TILES[i, j])
     inverses = [split(f) for f in small_inverses([gram(i, i) for i in range(4)])]
-    solved = {}
-    for i in (1, 0, 3, 2):
-        value = tile(i).astype(F32)
-        for j in solved:
-            if j // 2 < i // 2:
-                known = (solved[j].astype(BF16), None)
-            else:
-                known = solved[j]
-            value = value - fine_dot((gram(i, j), None), known)
-        solved[i] = fine_dot(inverses[i], value)
+    above = [
+        split(fine_dot(inverses[at], fine_dot((gram(at, at + 1), None), inverses[at + 1])))
+        for at in (0, 2)
+    ]
+
+    def solve(panel, first, second):
+        at = 2 * panel
+        return [
+            fine_dot(inverses[at], first) - fine_dot(above[panel], second),
+            fine_dot(inverses[at + 1], second),
+        ]
+
+    solved = solve(0, (tile(0), None), (tile(1), None))
+    known = [value.astype(BF16) for value in solved]
+    rest = [
+        tile(i).astype(F32)
+        - jnp.dot(gram(i, 0), known[0], preferred_element_type=F32)
+        - jnp.dot(gram(i, 1), known[1], preferred_element_type=F32)
+        for i in (2, 3)
+    ]
+    solved += solve(1, *map(split, rest))
+    for i in range(4):
         turned = solved[i].T.astype(BF16)
         for x in range(X_SIZE):
             to = pl.multiple_of((x + X_SIZE - lax.axis_index("x")) % X_SIZE * rows, UNIT)

time: 116 us -> 115 us (level)
  no operation moved by 1% of the time
where the time goes in v5:
time: 115 us
  starting transfers between devices  40.3 us (35%)
  blocking collectives  35 us (30%)
  waiting for transfers between devices  25.4 us (22%)
  Pallas kernels  12.8 us (11%)
    all_to_all x2, blocking collectives, exchange(): return lax.all_to_all(pieces, axes, 0, 0, tiled=True)  35 us
    ppermute x25, starting transfers between devices, shifted(): lax.ppermute(value, axis, [(at, (at + steps) % count) for at in range(cou...  33.8 us
    ppermute x25, waiting for transfers between devices, shifted(): lax.ppermute(value, axis, [(at, (at + steps) % count) for at in range(cou...  25.4 us
    pallas_call x6, Pallas kernels, call(): pl.pallas_call(kernel, out_shape=out_shape, in_specs=in_specs, out_specs=...  12.8 us
    ppermute x2, starting transfers between devices, from_behind(): lax.ppermute(value, axis, [(source, source + steps) for source in range(f...  6.51 us
  transfers between devices with their start and end apart: 27, of which 10 were waited for; matrix products, arithmetic and copies ran while one was open for 1% of the time, Pallas kernels for 3%

profile of v5, /device:TPU:1, one launch (start us, length us, event | category | flops | bytes accessed | tf_op | source)
XLA Modules:
  0.0 114.6 jit_solution(3842112586598442762)
XLA Ops:
  0.0 2.2 %shard_map.46 = (bf16[16,3200]{1,0:T(8,128)(2,1)}, bf16[16,3200]{1,0:T(8,128)(2,1)}, bf16[16,3200]{1,0:T(8,128)(2,1)}, bf16[16,3200]{1,0:T(8,128)(2,1)}, f32[32,2432]{1,0:T(8,128)}, /*index=5*/f32[32,1408]{1,0:T(8,128)}) custom-call(s32[2,8]{1,0:T(2,128)} %offsets_ref.3, f32[2,8,4,128]{3,2,1,0:T(4,128)} %vectors_ref.3, bf16[2,8,12544]{2,1,0:T(8,128)(2,1)} %panels_ref.1, ...), custom_call_target="tpu_custom_call" | custom-call | flops 200704 | bytes 802816 | tf_op jit(solution)/shard_map/pallas_call | solution.py:29
  2.2 2.1 %collective-permute-start.2 = (bf16[16,3200]{1,0:T(8,128)(2,1)}, bf16[16,3200]{1,0:T(8,128)(2,1)S(1)}, u32[]{:S(2)}, u32[]{:S(2)}) collective-permute-start(bf16[16,3200]{1,0:T(8,128)(2,1)} %get-tuple-element.28), channel_id=1, source_target_pairs={{0,8},{8,16},{16,24},{24,0},{1,9},{9,17},{17,25},{25,1},{2,10},{10... | collective-permute-start | bytes 307208 | tf_op jit(solution)/shard_map/ppermute | solution.py:42
  4.3 1.4 %collective-permute-start.10 = (bf16[16,3200]{1,0:T(8,128)(2,1)}, bf16[16,3200]{1,0:T(8,128)(2,1)S(1)}, u32[]{:S(2)}, u32[]{:S(2)}) collective-permute-start(bf16[16,3200]{1,0:T(8,128)(2,1)} %get-tuple-element.29), channel_id=1, source_target_pairs={{0,24},{8,0},{16,8},{24,16},{1,25},{9,1},{17,9},{25,17},{2,26},{10... | collective-permute-start | bytes 307208 | tf_op jit(solution)/shard_map/ppermute | solution.py:42
  5.6 1.6 %collective-permute-start.11 = (bf16[16,3200]{1,0:T(8,128)(2,1)}, bf16[16,3200]{1,0:T(8,128)(2,1)S(1)}, u32[]{:S(2)}, u32[]{:S(2)}) collective-permute-start(bf16[16,3200]{1,0:T(8,128)(2,1)} %get-tuple-element.30), channel_id=1, source_target_pairs={{0,16},{8,24},{16,0},{24,8},{1,17},{9,25},{17,1},{25,9},{2,18},{10... | collective-permute-start | bytes 307208 | tf_op jit(solution)/shard_map/ppermute | solution.py:42
  7.3 3.4 %collective-permute-start.1 = (f32[32,1408]{1,0:T(8,128)}, f32[32,1408]{1,0:T(8,128)S(1)}, u32[]{:S(2)}, u32[]{:S(2)}) collective-permute-start(f32[32,1408]{1,0:T(8,128)} %get-tuple-element.25), channel_id=1, source_target_pairs={{32,0},{64,32},{96,64},{128,96},{160,128},{192,160},{224,192},{33,... | collective-permute-start | bytes 540680 | tf_op jit(solution)/shard_map/ppermute | solution.py:48
  10.7 3.1 %collective-permute-start = (f32[32,2432]{1,0:T(8,128)}, f32[32,2432]{1,0:T(8,128)S(1)}, u32[]{:S(2)}, u32[]{:S(2)}) collective-permute-start(f32[32,2432]{1,0:T(8,128)} %get-tuple-element.24), channel_id=1, source_target_pairs={{0,32},{32,64},{64,96},{96,128},{128,160},{160,192},{192,224},{1,3... | collective-permute-start | bytes 933896 | tf_op jit(solution)/shard_map/ppermute | solution.py:48
  13.8 0.9 constant_dynamic-update-slice_fusion.1
  14.7 5.7 %collective-permute-start.4 = (bf16[32,3200]{1,0:T(8,128)(2,1)S(1)}, bf16[32,3200]{1,0:T(8,128)(2,1)S(1)}, u32[]{:S(2)}, u32[]{:S(2)}) collective-permute-start(bf16[32,3200]{1,0:T(8,128)(2,1)S(1)} %constant_dynamic-update-slice_fusion.refs_0_), channel_id=1, source_target_pairs={{0,7},{1,0},{2,1},{3,2},{4,3},{5,4},{6,5},{7,6},{8,15},{9,8},{10,9... | collective-permute-start | bytes 614408 | tf_op jit(solution)/shard_map/ppermute | solution.py:42
  20.4 2.7 %collective-permute-start.13 = (bf16[32,3200]{1,0:T(8,128)(2,1)S(1)}, bf16[32,3200]{1,0:T(8,128)(2,1)S(1)}, u32[]{:S(2)}, u32[]{:S(2)}) collective-permute-start(bf16[32,3200]{1,0:T(8,128)(2,1)S(1)} %constant_dynamic-update-slice_fusion.2.refs_8_), channel_id=1, source_target_pairs={{0,7},{1,0},{2,1},{3,2},{4,3},{5,4},{6,5},{7,6},{8,15},{9,8},{10,9... | collective-permute-start | bytes 614408 | tf_op jit(solution)/shard_map/ppermute | solution.py:42
  23.2 5.4 %collective-permute-done.3.refs_1_ = bf16[32,3200]{1,0:T(8,128)(2,1)S(1)} collective-permute-done((bf16[32,3200]{1,0:T(8,128)(2,1)S(1)}, bf16[32,3200]{1,0:T(8,128)(2,1)S(1)}, u32[]{:S(2)}, u32[]{:S(2)}) %collective-permute-start.3) | collective-permute-done | bytes 204832 | tf_op jit(solution)/shard_map/ppermute | solution.py:42
  29.5 3.2 %collective-permute-start.15 = (bf16[32,3200]{1,0:T(8,128)(2,1)S(1)}, bf16[32,3200]{1,0:T(8,128)(2,1)S(1)}, u32[]{:S(2)}, u32[]{:S(2)}) collective-permute-start(bf16[32,3200]{1,0:T(8,128)(2,1)S(1)} %collective-permute-done.13.refs_10_), channel_id=1, source_target_pairs={{0,7},{1,0},{2,1},{3,2},{4,3},{5,4},{6,5},{7,6},{8,15},{9,8},{10,9... | collective-permute-start | bytes 614408 | tf_op jit(solution)/shard_map/ppermute | solution.py:42
  32.7 2.9 %shard_map.47 = (f32[32,12544]{1,0:T(8,128)S(1)}, bf16[32,3200]{1,0:T(8,128)(2,1)S(1)}, bf16[32,3200]{1,0:T(8,128)(2,1)S(1)}, bf16[32,3200]{1,0:T(8,128)(2,1)S(1...) custom-call(s32[2,8]{1,0:T(2,128)S(1)} %copy-done.2, s32[2,8]{1,0:T(2,128)S(1)} %slice_convert_fusion.1.upper_offsets_ref, ...), custom_call_target="tpu_custom_call" | custom-call | flops 16056320 | bytes 4816896 | tf_op jit(solution)/shard_map/pallas_call | solution.py:29
  35.6 1.5 %collective-permute-start.21 = (bf16[16,3200]{1,0:T(8,128)(2,1)S(1)}, bf16[16,3200]{1,0:T(8,128)(2,1)S(1)}, u32[]{:S(2)}, u32[]{:S(2)}) collective-permute-start(bf16[16,3200]{1,0:T(8,128)(2,1)S(1)} %get-tuple-element.34), channel_id=1, source_target_pairs={{0,16},{8,24},{16,0},{24,8},{1,17},{9,25},{17,1},{25,9},{2,18},{10... | collective-permute-start | bytes 307208 | tf_op jit(solution)/shard_map/ppermute | solution.py:42
  37.2 1.5 %collective-permute-start.22 = (bf16[16,3200]{1,0:T(8,128)(2,1)S(1)}, bf16[16,3200]{1,0:T(8,128)(2,1)S(1)}, u32[]{:S(2)}, u32[]{:S(2)}) collective-permute-start(bf16[16,3200]{1,0:T(8,128)(2,1)S(1)} %get-tuple-element.35), channel_id=1, source_target_pairs={{0,16},{8,24},{16,0},{24,8},{1,17},{9,25},{17,1},{25,9},{2,18},{10... | collective-permute-start | bytes 307208 | tf_op jit(solution)/shard_map/ppermute | solution.py:42
  38.7 2.5 %collective-permute-done.21.refs_19_ = bf16[16,3200]{1,0:T(8,128)(2,1)S(1)} collective-permute-done((bf16[16,3200]{1,0:T(8,128)(2,1)S(1)}, bf16[16,3200]{1,0:T(8,128)(2,1)S(1)}, u32[]{:S(2)}, u32[]{:S(2)}) %collective-permute-start.21) | collective-permute-done | bytes 102432 | tf_op jit(solution)/shard_map/ppermute | solution.py:42
  41.2 2.4 %collective-permute-done.22.refs_20_ = bf16[16,3200]{1,0:T(8,128)(2,1)S(1)} collective-permute-done((bf16[16,3200]{1,0:T(8,128)(2,1)S(1)}, bf16[16,3200]{1,0:T(8,128)(2,1)S(1)}, u32[]{:S(2)}, u32[]{:S(2)}) %collective-permute-start.22) | collective-permute-done | bytes 102432 | tf_op jit(solution)/shard_map/ppermute | solution.py:42
  43.7 2.7 %collective-permute-start.17 = (bf16[32,3200]{1,0:T(8,128)(2,1)S(1)}, bf16[32,3200]{1,0:T(8,128)(2,1)S(1)}, u32[]{:S(2)}, u32[]{:S(2)}) collective-permute-start(bf16[32,3200]{1,0:T(8,128)(2,1)S(1)} %collective-permute-done.15.refs_12_), channel_id=1, source_target_pairs={{0,7},{1,0},{2,1},{3,2},{4,3},{5,4},{6,5},{7,6},{8,15},{9,8},{10,9... | collective-permute-start | bytes 614408 | tf_op jit(solution)/shard_map/ppermute | solution.py:42
  46.4 2.6 %collective-permute-start.20 = (bf16[32,3200]{1,0:T(8,128)(2,1)S(1)}, bf16[32,3200]{1,0:T(8,128)(2,1)S(1)}, u32[]{:S(2)}, u32[]{:S(2)}) collective-permute-start(bf16[32,3200]{1,0:T(8,128)(2,1)S(1)} %get-tuple-element.33), channel_id=1, source_target_pairs={{0,24},{8,0},{16,8},{24,16},{1,25},{9,1},{17,9},{25,17},{2,26},{10... | collective-permute-start | bytes 614408 | tf_op jit(solution)/shard_map/ppermute | solution.py:42
  49.0 1.2 %collective-permute-done.19.refs_17_ = bf16[32,3200]{1,0:T(8,128)(2,1)S(1)} collective-permute-done((bf16[32,3200]{1,0:T(8,128)(2,1)S(1)}, bf16[32,3200]{1,0:T(8,128)(2,1)S(1)}, u32[]{:S(2)}, u32[]{:S(2)}) %collective-permute-start.19) | collective-permute-done | bytes 204832 | tf_op jit(solution)/shard_map/ppermute | solution.py:42
  50.4 1.5 %collective-permute-done.7.refs_5_ = bf16[32,3200]{1,0:T(8,128)(2,1)S(1)} collective-permute-done((bf16[32,3200]{1,0:T(8,128)(2,1)S(1)}, bf16[32,3200]{1,0:T(8,128)(2,1)S(1)}, u32[]{:S(2)}, u32[]{:S(2)}) %collective-permute-start.7) | collective-permute-done | bytes 204832 | tf_op jit(solution)/shard_map/ppermute | solution.py:42
  51.9 2.7 %collective-permute-start.18 = (bf16[32,3200]{1,0:T(8,128)(2,1)S(1)}, bf16[32,3200]{1,0:T(8,128)(2,1)S(1)}, u32[]{:S(2)}, u32[]{:S(2)}) collective-permute-start(bf16[32,3200]{1,0:T(8,128)(2,1)S(1)} %collective-permute-done.17.refs_14_), channel_id=1, source_target_pairs={{0,7},{1,0},{2,1},{3,2},{4,3},{5,4},{6,5},{7,6},{8,15},{9,8},{10,9... | collective-permute-start | bytes 614408 | tf_op jit(solution)/shard_map/ppermute | solution.py:42
  54.6 1.5 %collective-permute-done.16.refs_13_ = bf16[32,3200]{1,0:T(8,128)(2,1)S(1)} collective-permute-done((bf16[32,3200]{1,0:T(8,128)(2,1)S(1)}, bf16[32,3200]{1,0:T(8,128)(2,1)S(1)}, u32[]{:S(2)}, u32[]{:S(2)}) %collective-permute-start.16) | collective-permute-done | bytes 204832 | tf_op jit(solution)/shard_map/ppermute | solution.py:42
  56.1 4.3 %collective-permute-done.9.refs_7_ = bf16[32,3200]{1,0:T(8,128)(2,1)S(1)} collective-permute-done((bf16[32,3200]{1,0:T(8,128)(2,1)S(1)}, bf16[32,3200]{1,0:T(8,128)(2,1)S(1)}, u32[]{:S(2)}, u32[]{:S(2)}) %collective-permute-start.9) | collective-permute-done | bytes 204832 | tf_op jit(solution)/shard_map/ppermute | solution.py:42
  60.4 2.6 %shard_map.48 = (bf16[512,3200]{1,0:T(8,128)(2,1)S(1)}, bf16[1792,128]{1,0:T(8,128)(2,1)S(1)}) custom-call(bf16[32,3200]{1,0:T(8,128)(2,1)S(1)} %constant_dynamic-update-slice_fusion.refs_0_, bf16[32,3200]{1,0:T(8,128)(2,1)S(1)} %collective-permute-done.3.refs_1_, bf16[32,3200]{1,0:T(8,128)(2,1)S(1)} %collective-permute-done.4.refs_2_, ...), custom_call_target="tpu_custom_call" | custom-call | flops 2097152000 | bytes 9830400 | tf_op jit(solution)/shard_map/pallas_call | solution.py:29
  63.0 20.1 %all_to_all.10.parts_ref = bf16[32,56,128]{2,1,0:T(8,128)(2,1)S(1)} all-to-all(bf16[32,56,128]{2,1,0:T(8,128)(2,1)S(1)} %bitcast.3), channel_id=1, replica_groups=mesh['row'=8,'x'=4,'z'=8] {'row','x'}, dimensions={0} | all-to-all | bytes 917504 | tf_op jit(solution)/shard_map/all_to_all | solution.py:554
  83.2 14.8 %all_to_all.11 = bf16[32,56,128]{2,1,0:T(8,128)(2,1)S(1)} all-to-all(bf16[32,56,128]{2,1,0:T(8,128)(2,1)S(1)} %shard_map.49), channel_id=1, replica_groups=mesh['row'=8,'x'=4,'z'=8] {'row','x'}, dimensions={0} | all-to-all | bytes 917504 | tf_op jit(solution)/shard_map/all_to_all | solution.py:554
  98.1 3.7 %shard_map.50 = (bf16[32,3200]{1,0:T(8,128)(2,1)S(1)}, bf16[32,3200]{1,0:T(8,128)(2,1)S(1)}, bf16[32,3200]{1,0:T(8,128)(2,1)S(1)}, bf16[16,3200]{1,0:T(8,128)(2,1)S(1)}, bf16[16,3200]{1,0:T(8,128)(2,1)S(1)}) custom-call(bf16[1792,128]{1,0:T(8,128)(2,1)S(1)} %bitcast.2, bf16[512,3200]{1,0:T(8,128)(2,1)S(1)} %get-tuple-element.37.ordered_ref), custom_call_target="tpu_custom_call" | custom-call | flops 419430400 | bytes 6553600 | tf_op jit(solution)/shard_map/pallas_call | solution.py:29
  102.2 2.4 %collective-permute-start.24 = (bf16[32,3200]{1,0:T(8,128)(2,1)S(1)}, bf16[32,3200]{1,0:T(8,128)(2,1)S(1)}, u32[]{:S(2)}, u32[]{:S(2)}) collective-permute-start(bf16[32,3200]{1,0:T(8,128)(2,1)S(1)} %get-tuple-element.40), channel_id=1, source_target_pairs={{0,24},{8,0},{16,8},{24,16},{1,25},{9,1},{17,9},{25,17},{2,26},{10... | collective-permute-start | bytes 614408 | tf_op jit(solution)/shard_map/ppermute | solution.py:42
  104.6 3.0 %collective-permute-start.26 = (bf16[16,3200]{1,0:T(8,128)(2,1)S(1)}, bf16[16,3200]{1,0:T(8,128)(2,1)S(1)}, u32[]{:S(2)}, u32[]{:S(2)}) collective-permute-start(bf16[16,3200]{1,0:T(8,128)(2,1)S(1)} %get-tuple-element.42), channel_id=1, source_target_pairs={{0,16},{8,24},{16,0},{24,8},{1,17},{9,25},{17,1},{25,9},{2,18},{10... | collective-permute-start | bytes 307208 | tf_op jit(solution)/shard_map/ppermute | solution.py:42
  107.5 3.4 %collective-permute-done.25.half0 = bf16[16,3200]{1,0:T(8,128)(2,1)S(1)} collective-permute-done((bf16[16,3200]{1,0:T(8,128)(2,1)S(1)}, bf16[16,3200]{1,0:T(8,128)(2,1)S(1)}, u32[]{:S(2)}, u32[]{:S(2)}) %collective-permute-start.25) | collective-permute-done | bytes 102432 | tf_op jit(solution)/shard_map/ppermute | solution.py:42
  111.0 2.2 %collective-permute-done.26.half1 = bf16[16,3200]{1,0:T(8,128)(2,1)S(1)} collective-permute-done((bf16[16,3200]{1,0:T(8,128)(2,1)S(1)}, bf16[16,3200]{1,0:T(8,128)(2,1)S(1)}, u32[]{:S(2)}, u32[]{:S(2)}) %collective-permute-start.26) | collective-permute-done | bytes 102432 | tf_op jit(solution)/shard_map/ppermute | solution.py:42
  113.2 1.2 %shard_map.51 = f32[32,12544]{1,0:T(8,128)} custom-call(f32[32,12544]{1,0:T(8,128)S(1)} %get-tuple-element.26.eigen_ref, bf16[32,3200]{1,0:T(8,128)(2,1)S(1)} %get-tuple-element.38.mine, bf16[32,3200]{1,0:T(8,128)(2,1)S(1)} %collective-permute-done.23.one, bf16[32,3200]{1,0:T(8,128)(2,1)S(1)} %collective-permute-done.24.two, ...), custom_call_target="tpu_custom_call" | custom-call | flops 401408 | bytes 4014080 | tf_op jit(solution)/shard_map/pallas_call | solution.py:29
  (42 shorter events, 1.7 us)
Async XLA Ops:
  0.0 32.7 %copy-start.2 = (s32[2,8]{1,0:T(2,128)S(1)}, s32[2,8]{1,0:T(2,128)}, u32[]{:S(2)}) copy-start(s32[2,8]{1,0:T(2,128)} %offsets_ref.3) | copy-start | bytes 196
  0.0 32.7 %copy-start.1 = (f32[2,8,4,128]{3,2,1,0:T(4,128)S(1)}, f32[2,8,4,128]{3,2,1,0:T(4,128)}, u32[]{:S(2)}) copy-start(f32[2,8,4,128]{3,2,1,0:T(4,128)} %vectors_ref.3) | copy-start | bytes 98308
  0.0 32.7 %copy-start = (f32[32,12544]{1,0:T(8,128)S(1)}, f32[32,12544]{1,0:T(8,128)}, u32[]{:S(2)}) copy-start(f32[32,12544]{1,0:T(8,128)} %own_ref.1) | copy-start | bytes 4816900
  2.2 12.5 %collective-permute-start.2 = (bf16[16,3200]{1,0:T(8,128)(2,1)}, bf16[16,3200]{1,0:T(8,128)(2,1)S(1)}, u32[]{:S(2)}, u32[]{:S(2)}) collective-permute-start(bf16[16,3200]{1,0:T(8,128)(2,1)} %get-tuple-element.28), channel_id=1, source_target_pairs={{0,8},{8,16},{16,24},{24,0},{1,9},{9,17},{17,25},{25,1},{2,10},{10... | collective-permute-start | bytes 307208 | tf_op jit(solution)/shard_map/ppermute | solution.py:42
  4.3 16.1 %collective-permute-start.10 = (bf16[16,3200]{1,0:T(8,128)(2,1)}, bf16[16,3200]{1,0:T(8,128)(2,1)S(1)}, u32[]{:S(2)}, u32[]{:S(2)}) collective-permute-start(bf16[16,3200]{1,0:T(8,128)(2,1)} %get-tuple-element.29), channel_id=1, source_target_pairs={{0,24},{8,0},{16,8},{24,16},{1,25},{9,1},{17,9},{25,17},{2,26},{10... | collective-permute-start | bytes 307208 | tf_op jit(solution)/shard_map/ppermute | solution.py:42
  5.6 14.8 %collective-permute-start.11 = (bf16[16,3200]{1,0:T(8,128)(2,1)}, bf16[16,3200]{1,0:T(8,128)(2,1)S(1)}, u32[]{:S(2)}, u32[]{:S(2)}) collective-permute-start(bf16[16,3200]{1,0:T(8,128)(2,1)} %get-tuple-element.30), channel_id=1, source_target_pairs={{0,16},{8,24},{16,0},{24,8},{1,17},{9,25},{17,1},{25,9},{2,18},{10... | collective-permute-start | bytes 307208 | tf_op jit(solution)/shard_map/ppermute | solution.py:42
  7.3 15.9 %collective-permute-start.1 = (f32[32,1408]{1,0:T(8,128)}, f32[32,1408]{1,0:T(8,128)S(1)}, u32[]{:S(2)}, u32[]{:S(2)}) collective-permute-start(f32[32,1408]{1,0:T(8,128)} %get-tuple-element.25), channel_id=1, source_target_pairs={{32,0},{64,32},{96,64},{128,96},{160,128},{192,160},{224,192},{33,... | collective-permute-start | bytes 540680 | tf_op jit(solution)/shard_map/ppermute | solution.py:48
  10.7 22.0 %collective-permute-start = (f32[32,2432]{1,0:T(8,128)}, f32[32,2432]{1,0:T(8,128)S(1)}, u32[]{:S(2)}, u32[]{:S(2)}) collective-permute-start(f32[32,2432]{1,0:T(8,128)} %get-tuple-element.24), channel_id=1, source_target_pairs={{0,32},{32,64},{64,96},{96,128},{128,160},{160,192},{192,224},{1,3... | collective-permute-start | bytes 933896 | tf_op jit(solution)/shard_map/ppermute | solution.py:48
  14.7 22.4 %collective-permute-start.4 = (bf16[32,3200]{1,0:T(8,128)(2,1)S(1)}, bf16[32,3200]{1,0:T(8,128)(2,1)S(1)}, u32[]{:S(2)}, u32[]{:S(2)}) collective-permute-start(bf16[32,3200]{1,0:T(8,128)(2,1)S(1)} %constant_dynamic-update-slice_fusion.refs_0_), channel_id=1, source_target_pairs={{0,7},{1,0},{2,1},{3,2},{4,3},{5,4},{6,5},{7,6},{8,15},{9,8},{10,9... | collective-permute-start | bytes 614408 | tf_op jit(solution)/shard_map/ppermute | solution.py:42
  20.4 8.2 %collective-permute-start.3 = (bf16[32,3200]{1,0:T(8,128)(2,1)S(1)}, bf16[32,3200]{1,0:T(8,128)(2,1)S(1)}, u32[]{:S(2)}, u32[]{:S(2)}) collective-permute-start(bf16[32,3200]{1,0:T(8,128)(2,1)S(1)} %constant_dynamic-update-slice_fusion.refs_0_), channel_id=1, source_target_pairs={{0,1},{1,2},{2,3},{3,4},{4,5},{5,6},{6,7},{7,0},{8,9},{9,10},{10,1... | collective-permute-start | bytes 614408 | tf_op jit(solution)/shard_map/ppermute | solution.py:42
  20.4 9.0 %collective-permute-start.13 = (bf16[32,3200]{1,0:T(8,128)(2,1)S(1)}, bf16[32,3200]{1,0:T(8,128)(2,1)S(1)}, u32[]{:S(2)}, u32[]{:S(2)}) collective-permute-start(bf16[32,3200]{1,0:T(8,128)(2,1)S(1)} %constant_dynamic-update-slice_fusion.2.refs_8_), channel_id=1, source_target_pairs={{0,7},{1,0},{2,1},{3,2},{4,3},{5,4},{6,5},{7,6},{8,15},{9,8},{10,9... | collective-permute-start | bytes 614408 | tf_op jit(solution)/shard_map/ppermute | solution.py:42
  23.2 15.5 %collective-permute-start.12 = (bf16[32,3200]{1,0:T(8,128)(2,1)S(1)}, bf16[32,3200]{1,0:T(8,128)(2,1)S(1)}, u32[]{:S(2)}, u32[]{:S(2)}) collective-permute-start(bf16[32,3200]{1,0:T(8,128)(2,1)S(1)} %constant_dynamic-update-slice_fusion.2.refs_8_), channel_id=1, source_target_pairs={{0,1},{1,2},{2,3},{3,4},{4,5},{5,6},{6,7},{7,0},{8,9},{9,10},{10,1... | collective-permute-start | bytes 614408 | tf_op jit(solution)/shard_map/ppermute | solution.py:42
  28.6 15.0 %collective-permute-start.5 = (bf16[32,3200]{1,0:T(8,128)(2,1)S(1)}, bf16[32,3200]{1,0:T(8,128)(2,1)S(1)}, u32[]{:S(2)}, u32[]{:S(2)}) collective-permute-start(bf16[32,3200]{1,0:T(8,128)(2,1)S(1)} %collective-permute-done.3.refs_1_), channel_id=1, source_target_pairs={{0,1},{1,2},{2,3},{3,4},{4,5},{5,6},{6,7},{7,0},{8,9},{9,10},{10,1... | collective-permute-start | bytes 614408 | tf_op jit(solution)/shard_map/ppermute | solution.py:42
  29.5 14.2 %collective-permute-start.15 = (bf16[32,3200]{1,0:T(8,128)(2,1)S(1)}, bf16[32,3200]{1,0:T(8,128)(2,1)S(1)}, u32[]{:S(2)}, u32[]{:S(2)}) collective-permute-start(bf16[32,3200]{1,0:T(8,128)(2,1)S(1)} %collective-permute-done.13.refs_10_), channel_id=1, source_target_pairs={{0,7},{1,0},{2,1},{3,2},{4,3},{5,4},{6,5},{7,6},{8,15},{9,8},{10,9... | collective-permute-start | bytes 614408 | tf_op jit(solution)/shard_map/ppermute | solution.py:42
  35.6 5.5 %collective-permute-start.21 = (bf16[16,3200]{1,0:T(8,128)(2,1)S(1)}, bf16[16,3200]{1,0:T(8,128)(2,1)S(1)}, u32[]{:S(2)}, u32[]{:S(2)}) collective-permute-start(bf16[16,3200]{1,0:T(8,128)(2,1)S(1)} %get-tuple-element.34), channel_id=1, source_target_pairs={{0,16},{8,24},{16,0},{24,8},{1,17},{9,25},{17,1},{25,9},{2,18},{10... | collective-permute-start | bytes 307208 | tf_op jit(solution)/shard_map/ppermute | solution.py:42
  37.2 6.4 %collective-permute-start.22 = (bf16[16,3200]{1,0:T(8,128)(2,1)S(1)}, bf16[16,3200]{1,0:T(8,128)(2,1)S(1)}, u32[]{:S(2)}, u32[]{:S(2)}) collective-permute-start(bf16[16,3200]{1,0:T(8,128)(2,1)S(1)} %get-tuple-element.35), channel_id=1, source_target_pairs={{0,16},{8,24},{16,0},{24,8},{1,17},{9,25},{17,1},{25,9},{2,18},{10... | collective-permute-start | bytes 307208 | tf_op jit(solution)/shard_map/ppermute | solution.py:42
  38.7 7.7 %collective-permute-start.6 = (bf16[32,3200]{1,0:T(8,128)(2,1)S(1)}, bf16[32,3200]{1,0:T(8,128)(2,1)S(1)}, u32[]{:S(2)}, u32[]{:S(2)}) collective-permute-start(bf16[32,3200]{1,0:T(8,128)(2,1)S(1)} %collective-permute-done.4.refs_2_), channel_id=1, source_target_pairs={{0,7},{1,0},{2,1},{3,2},{4,3},{5,4},{6,5},{7,6},{8,15},{9,8},{10,9... | collective-permute-start | bytes 614408 | tf_op jit(solution)/shard_map/ppermute | solution.py:42
  41.2 7.8 %collective-permute-start.14 = (bf16[32,3200]{1,0:T(8,128)(2,1)S(1)}, bf16[32,3200]{1,0:T(8,128)(2,1)S(1)}, u32[]{:S(2)}, u32[]{:S(2)}) collective-permute-start(bf16[32,3200]{1,0:T(8,128)(2,1)S(1)} %collective-permute-done.12.refs_9_), channel_id=1, source_target_pairs={{0,1},{1,2},{2,3},{3,4},{4,5},{5,6},{6,7},{7,0},{8,9},{9,10},{10,1... | collective-permute-start | bytes 614408 | tf_op jit(solution)/shard_map/ppermute | solution.py:42
  43.6 6.7 %collective-permute-start.19 = (bf16[32,3200]{1,0:T(8,128)(2,1)S(1)}, bf16[32,3200]{1,0:T(8,128)(2,1)S(1)}, u32[]{:S(2)}, u32[]{:S(2)}) collective-permute-start(bf16[32,3200]{1,0:T(8,128)(2,1)S(1)} %get-tuple-element.32), channel_id=1, source_target_pairs={{0,8},{8,16},{16,24},{24,0},{1,9},{9,17},{17,25},{25,1},{2,10},{10... | collective-permute-start | bytes 614408 | tf_op jit(solution)/shard_map/ppermute | solution.py:42
  43.7 8.2 %collective-permute-start.7 = (bf16[32,3200]{1,0:T(8,128)(2,1)S(1)}, bf16[32,3200]{1,0:T(8,128)(2,1)S(1)}, u32[]{:S(2)}, u32[]{:S(2)}) collective-permute-start(bf16[32,3200]{1,0:T(8,128)(2,1)S(1)} %collective-permute-done.5.refs_3_), channel_id=1, source_target_pairs={{0,1},{1,2},{2,3},{3,4},{4,5},{5,6},{6,7},{7,0},{8,9},{9,10},{10,1... | collective-permute-start | bytes 614408 | tf_op jit(solution)/shard_map/ppermute | solution.py:42
  43.7 8.2 %collective-permute-start.17 = (bf16[32,3200]{1,0:T(8,128)(2,1)S(1)}, bf16[32,3200]{1,0:T(8,128)(2,1)S(1)}, u32[]{:S(2)}, u32[]{:S(2)}) collective-permute-start(bf16[32,3200]{1,0:T(8,128)(2,1)S(1)} %collective-permute-done.15.refs_12_), channel_id=1, source_target_pairs={{0,7},{1,0},{2,1},{3,2},{4,3},{5,4},{6,5},{7,6},{8,15},{9,8},{10,9... | collective-permute-start | bytes 614408 | tf_op jit(solution)/shard_map/ppermute | solution.py:42
  46.4 8.2 %collective-permute-start.20 = (bf16[32,3200]{1,0:T(8,128)(2,1)S(1)}, bf16[32,3200]{1,0:T(8,128)(2,1)S(1)}, u32[]{:S(2)}, u32[]{:S(2)}) collective-permute-start(bf16[32,3200]{1,0:T(8,128)(2,1)S(1)} %get-tuple-element.33), channel_id=1, source_target_pairs={{0,24},{8,0},{16,8},{24,16},{1,25},{9,1},{17,9},{25,17},{2,26},{10... | collective-permute-start | bytes 614408 | tf_op jit(solution)/shard_map/ppermute | solution.py:42
  48.9 5.7 %collective-permute-start.8 = (bf16[32,3200]{1,0:T(8,128)(2,1)S(1)}, bf16[32,3200]{1,0:T(8,128)(2,1)S(1)}, u32[]{:S(2)}, u32[]{:S(2)}) collective-permute-start(bf16[32,3200]{1,0:T(8,128)(2,1)S(1)} %collective-permute-done.6.refs_4_), channel_id=1, source_target_pairs={{0,7},{1,0},{2,1},{3,2},{4,3},{5,4},{6,5},{7,6},{8,15},{9,8},{10,9... | collective-permute-start | bytes 614408 | tf_op jit(solution)/shard_map/ppermute | solution.py:42
  50.3 5.8 %collective-permute-start.16 = (bf16[32,3200]{1,0:T(8,128)(2,1)S(1)}, bf16[32,3200]{1,0:T(8,128)(2,1)S(1)}, u32[]{:S(2)}, u32[]{:S(2)}) collective-permute-start(bf16[32,3200]{1,0:T(8,128)(2,1)S(1)} %collective-permute-done.14.refs_11_), channel_id=1, source_target_pairs={{0,1},{1,2},{2,3},{3,4},{4,5},{5,6},{6,7},{7,0},{8,9},{9,10},{10,1... | collective-permute-start | bytes 614408 | tf_op jit(solution)/shard_map/ppermute | solution.py:42
  51.9 8.5 %collective-permute-start.9 = (bf16[32,3200]{1,0:T(8,128)(2,1)S(1)}, bf16[32,3200]{1,0:T(8,128)(2,1)S(1)}, u32[]{:S(2)}, u32[]{:S(2)}) collective-permute-start(bf16[32,3200]{1,0:T(8,128)(2,1)S(1)} %collective-permute-done.7.refs_5_), channel_id=1, source_target_pairs={{0,1},{1,2},{2,3},{3,4},{4,5},{5,6},{6,7},{7,0},{8,9},{9,10},{10,1... | collective-permute-start | bytes 614408 | tf_op jit(solution)/shard_map/ppermute | solution.py:42
  51.9 8.5 %collective-permute-start.18 = (bf16[32,3200]{1,0:T(8,128)(2,1)S(1)}, bf16[32,3200]{1,0:T(8,128)(2,1)S(1)}, u32[]{:S(2)}, u32[]{:S(2)}) collective-permute-start(bf16[32,3200]{1,0:T(8,128)(2,1)S(1)} %collective-permute-done.17.refs_14_), channel_id=1, source_target_pairs={{0,7},{1,0},{2,1},{3,2},{4,3},{5,4},{6,5},{7,6},{8,15},{9,8},{10,9... | collective-permute-start | bytes 614408 | tf_op jit(solution)/shard_map/ppermute | solution.py:42
  101.8 11.4 %collective-permute-start.23 = (bf16[32,3200]{1,0:T(8,128)(2,1)S(1)}, bf16[32,3200]{1,0:T(8,128)(2,1)S(1)}, u32[]{:S(2)}, u32[]{:S(2)}) collective-permute-start(bf16[32,3200]{1,0:T(8,128)(2,1)S(1)} %get-tuple-element.39), channel_id=1, source_target_pairs={{0,8},{8,16},{16,24},{24,0},{1,9},{9,17},{17,25},{25,1},{2,10},{10... | collective-permute-start | bytes 614408 | tf_op jit(solution)/shard_map/ppermute | solution.py:42
  102.2 11.0 %collective-permute-start.24 = (bf16[32,3200]{1,0:T(8,128)(2,1)S(1)}, bf16[32,3200]{1,0:T(8,128)(2,1)S(1)}, u32[]{:S(2)}, u32[]{:S(2)}) collective-permute-start(bf16[32,3200]{1,0:T(8,128)(2,1)S(1)} %get-tuple-element.40), channel_id=1, source_target_pairs={{0,24},{8,0},{16,8},{24,16},{1,25},{9,1},{17,9},{25,17},{2,26},{10... | collective-permute-start | bytes 614408 | tf_op jit(solution)/shard_map/ppermute | solution.py:42
  104.6 6.4 %collective-permute-start.25 = (bf16[16,3200]{1,0:T(8,128)(2,1)S(1)}, bf16[16,3200]{1,0:T(8,128)(2,1)S(1)}, u32[]{:S(2)}, u32[]{:S(2)}) collective-permute-start(bf16[16,3200]{1,0:T(8,128)(2,1)S(1)} %get-tuple-element.41), channel_id=1, source_target_pairs={{0,16},{8,24},{16,0},{24,8},{1,17},{9,25},{17,1},{25,9},{2,18},{10... | collective-permute-start | bytes 307208 | tf_op jit(solution)/shard_map/ppermute | solution.py:42
  104.6 8.6 %collective-permute-start.26 = (bf16[16,3200]{1,0:T(8,128)(2,1)S(1)}, bf16[16,3200]{1,0:T(8,128)(2,1)S(1)}, u32[]{:S(2)}, u32[]{:S(2)}) collective-permute-start(bf16[16,3200]{1,0:T(8,128)(2,1)S(1)} %get-tuple-element.42), channel_id=1, source_target_pairs={{0,16},{8,24},{16,0},{24,8},{1,17},{9,25},{17,1},{25,9},{2,18},{10... | collective-permute-start | bytes 307208 | tf_op jit(solution)/shard_map/ppermute | solution.py:42

commit v6 on v5

--- a/solution.py
+++ b/solution.py
@@ -10,6 +10,8 @@
 
 
 COL = ("x", "z")
+ROW = ("y", "core")
+SUM_AXES = ("core", "x", "y")
 X_SIZE, Z_SIZE = 4, 8
 LANE = 128
 GROUP = 4
@@ -220,8 +222,8 @@
     state_ref[:, 0:left] = upper_ref[:, 0:left]
     state_ref[:, left : left + columns] = own_ref[...]
     state_ref[:, left + columns :] = lower_ref[:, 0:right]
-    first = lax.axis_index("row") == 0
-    final = lax.axis_index("row") == lax.axis_size("row") - 1
+    first = lax.axis_index(ROW) == 0
+    final = lax.axis_index(ROW) == lax.axis_size(ROW) - 1
 
     def beside(ref, width, sweep, i):
         return ref[i * spans : (i + 1) * spans, width + sweep * band : width + (sweep + 1) * band]
@@ -282,8 +284,8 @@
     rows, columns = eigen.shape
     left, right = halo_sizes(vectors)
     assert left + right + band < columns and spans * refl == rows
-    upper = from_behind(down, "row", 1)
-    lower = from_behind(up, "row", -1)
+    upper = from_behind(down, ROW, 1)
+    lower = from_behind(up, ROW, -1)
     upper_offsets = upper[0:sweeps, -LANE : spans - LANE].astype(jnp.int32)
     lower_offsets = lower[0:sweeps, -LANE : spans - LANE].astype(jnp.int32)
     return call(
@@ -556,7 +558,7 @@
 
 def inner(eigvecs, span_vectors, span_offsets, panels):
     assert (lax.axis_size("x"), lax.axis_size("z")) == (X_SIZE, Z_SIZE)
-    peers = lax.axis_size("row") * X_SIZE
+    peers = lax.axis_size(ROW) * X_SIZE
     count, own, columns = panels.shape
     rows = eigvecs.shape[0]
     order = count * own * X_SIZE * Z_SIZE
@@ -574,17 +576,15 @@
     others = [pieces[0], *traded(pieces)]
     ordered, sums = products(found, others, spots, own, order, rows)
 
-    parts = exchange(sums.reshape(peers, -1, LANE), ("row", "x"))
-    sums = exchange(total_for_all(parts), ("row", "x"))
+    parts = exchange(sums.reshape(peers, -1, LANE), SUM_AXES)
+    sums = exchange(total_for_all(parts), SUM_AXES)
     corrections = correction(sums.reshape(-1, LANE), ordered, rows)
     return subtract(eigen, [corrections[0], *traded(corrections)])
 
 
 def solution(mesh):
     finer = Mesh(
-        mesh.devices.reshape(mesh.shape["row"], X_SIZE, Z_SIZE), ("row", "x", "z")
-    )
-    placed = (P(COL, "row"), P(None, "row", None, None), P(None, "row"), P(None, COL, "row"))
-    return jax.shard_map(
-        inner, mesh=finer, in_specs=placed, out_specs=P(COL, "row"), check_vma=False
-    )
+        mesh.devices.reshape(mesh.shape["row"] // 2, 2, X_SIZE, Z_SIZE), (*ROW, *COL)
+    )
+    placed = (P(COL, ROW), P(None, ROW, None, None), P(None, ROW), P(None, COL, ROW))
+    return jax.shard_map(inner, mesh=finer, in_specs=placed, out_specs=P(COL, ROW), check_vma=False)

time: 115 us -> 115 us (level)
  no operation moved by 1% of the time
where the time goes in v6:
time: 115 us; the launch traced here: 114 us
  starting transfers between devices  40.3 us (35%)
  blocking collectives  34 us (30%)
  waiting for transfers between devices  26 us (23%)
  Pallas kernels  12.8 us (11%)
    all_to_all x2, blocking collectives, exchange(): return lax.all_to_all(pieces, axes, 0, 0, tiled=True)  34 us
    ppermute x25, starting transfers between devices, shifted(): lax.ppermute(value, axis, [(at, (at + steps) % count) for at in range(cou...  33.8 us
    ppermute x25, waiting for transfers between devices, shifted(): lax.ppermute(value, axis, [(at, (at + steps) % count) for at in range(cou...  26 us
    pallas_call x6, Pallas kernels, call(): pl.pallas_call(kernel, out_shape=out_shape, in_specs=in_specs, out_specs=...  12.8 us
    ppermute x2, starting transfers between devices, from_behind(): lax.ppermute(value, axis, [(source, source + steps) for source in range(f...  6.51 us
  transfers between devices with their start and end apart: 27, of which 10 were waited for; matrix products, arithmetic and copies ran while one was open for 1% of the time, Pallas kernels for 3%

profile of v6, /device:TPU:1, one launch (start us, length us, event | category | flops | bytes accessed | tf_op | source)
XLA Modules:
  0.0 114.3 jit_solution(7533728932615168940)
XLA Ops:
  0.0 2.2 %shard_map.46 = (bf16[16,3200]{1,0:T(8,128)(2,1)}, bf16[16,3200]{1,0:T(8,128)(2,1)}, bf16[16,3200]{1,0:T(8,128)(2,1)}, bf16[16,3200]{1,0:T(8,128)(2,1)}, f32[32,2432]{1,0:T(8,128)}, /*index=5*/f32[32,1408]{1,0:T(8,128)}) custom-call(s32[2,8]{1,0:T(2,128)} %offsets_ref.3, f32[2,8,4,128]{3,2,1,0:T(4,128)} %vectors_ref.3, bf16[2,8,12544]{2,1,0:T(8,128)(2,1)} %panels_ref.1, ...), custom_call_target="tpu_custom_call" | custom-call | flops 200704 | bytes 802816 | tf_op jit(solution)/shard_map/pallas_call | solution.py:31
  2.2 2.1 %collective-permute-start.2 = (bf16[16,3200]{1,0:T(8,128)(2,1)}, bf16[16,3200]{1,0:T(8,128)(2,1)S(1)}, u32[]{:S(2)}, u32[]{:S(2)}) collective-permute-start(bf16[16,3200]{1,0:T(8,128)(2,1)} %get-tuple-element.28), channel_id=1, source_target_pairs={{0,8},{8,16},{16,24},{24,0},{1,9},{9,17},{17,25},{25,1},{2,10},{10... | collective-permute-start | bytes 307208 | tf_op jit(solution)/shard_map/ppermute | solution.py:44
  4.3 1.4 %collective-permute-start.10 = (bf16[16,3200]{1,0:T(8,128)(2,1)}, bf16[16,3200]{1,0:T(8,128)(2,1)S(1)}, u32[]{:S(2)}, u32[]{:S(2)}) collective-permute-start(bf16[16,3200]{1,0:T(8,128)(2,1)} %get-tuple-element.29), channel_id=1, source_target_pairs={{0,24},{8,0},{16,8},{24,16},{1,25},{9,1},{17,9},{25,17},{2,26},{10... | collective-permute-start | bytes 307208 | tf_op jit(solution)/shard_map/ppermute | solution.py:44
  5.6 1.6 %collective-permute-start.11 = (bf16[16,3200]{1,0:T(8,128)(2,1)}, bf16[16,3200]{1,0:T(8,128)(2,1)S(1)}, u32[]{:S(2)}, u32[]{:S(2)}) collective-permute-start(bf16[16,3200]{1,0:T(8,128)(2,1)} %get-tuple-element.30), channel_id=1, source_target_pairs={{0,16},{8,24},{16,0},{24,8},{1,17},{9,25},{17,1},{25,9},{2,18},{10... | collective-permute-start | bytes 307208 | tf_op jit(solution)/shard_map/ppermute | solution.py:44
  7.3 3.4 %collective-permute-start.1 = (f32[32,1408]{1,0:T(8,128)}, f32[32,1408]{1,0:T(8,128)S(1)}, u32[]{:S(2)}, u32[]{:S(2)}) collective-permute-start(f32[32,1408]{1,0:T(8,128)} %get-tuple-element.25), channel_id=1, source_target_pairs={{32,0},{64,32},{96,64},{128,96},{160,128},{192,160},{224,192},{33,... | collective-permute-start | bytes 540680 | tf_op jit(solution)/shard_map/ppermute | solution.py:50
  10.7 3.1 %collective-permute-start = (f32[32,2432]{1,0:T(8,128)}, f32[32,2432]{1,0:T(8,128)S(1)}, u32[]{:S(2)}, u32[]{:S(2)}) collective-permute-start(f32[32,2432]{1,0:T(8,128)} %get-tuple-element.24), channel_id=1, source_target_pairs={{0,32},{32,64},{64,96},{96,128},{128,160},{160,192},{192,224},{1,3... | collective-permute-start | bytes 933896 | tf_op jit(solution)/shard_map/ppermute | solution.py:50
  13.8 0.9 constant_dynamic-update-slice_fusion.1
  14.7 5.7 %collective-permute-start.4 = (bf16[32,3200]{1,0:T(8,128)(2,1)S(1)}, bf16[32,3200]{1,0:T(8,128)(2,1)S(1)}, u32[]{:S(2)}, u32[]{:S(2)}) collective-permute-start(bf16[32,3200]{1,0:T(8,128)(2,1)S(1)} %constant_dynamic-update-slice_fusion.refs_0_), channel_id=1, source_target_pairs={{0,7},{1,0},{2,1},{3,2},{4,3},{5,4},{6,5},{7,6},{8,15},{9,8},{10,9... | collective-permute-start | bytes 614408 | tf_op jit(solution)/shard_map/ppermute | solution.py:44
  20.4 2.7 %collective-permute-start.13 = (bf16[32,3200]{1,0:T(8,128)(2,1)S(1)}, bf16[32,3200]{1,0:T(8,128)(2,1)S(1)}, u32[]{:S(2)}, u32[]{:S(2)}) collective-permute-start(bf16[32,3200]{1,0:T(8,128)(2,1)S(1)} %constant_dynamic-update-slice_fusion.2.refs_8_), channel_id=1, source_target_pairs={{0,7},{1,0},{2,1},{3,2},{4,3},{5,4},{6,5},{7,6},{8,15},{9,8},{10,9... | collective-permute-start | bytes 614408 | tf_op jit(solution)/shard_map/ppermute | solution.py:44
  23.2 5.4 %collective-permute-done.3.refs_1_ = bf16[32,3200]{1,0:T(8,128)(2,1)S(1)} collective-permute-done((bf16[32,3200]{1,0:T(8,128)(2,1)S(1)}, bf16[32,3200]{1,0:T(8,128)(2,1)S(1)}, u32[]{:S(2)}, u32[]{:S(2)}) %collective-permute-start.3) | collective-permute-done | bytes 204832 | tf_op jit(solution)/shard_map/ppermute | solution.py:44
  29.5 3.2 %collective-permute-start.15 = (bf16[32,3200]{1,0:T(8,128)(2,1)S(1)}, bf16[32,3200]{1,0:T(8,128)(2,1)S(1)}, u32[]{:S(2)}, u32[]{:S(2)}) collective-permute-start(bf16[32,3200]{1,0:T(8,128)(2,1)S(1)} %collective-permute-done.13.refs_10_), channel_id=1, source_target_pairs={{0,7},{1,0},{2,1},{3,2},{4,3},{5,4},{6,5},{7,6},{8,15},{9,8},{10,9... | collective-permute-start | bytes 614408 | tf_op jit(solution)/shard_map/ppermute | solution.py:44
  32.7 2.9 %shard_map.47 = (f32[32,12544]{1,0:T(8,128)S(1)}, bf16[32,3200]{1,0:T(8,128)(2,1)S(1)}, bf16[32,3200]{1,0:T(8,128)(2,1)S(1)}, bf16[32,3200]{1,0:T(8,128)(2,1)S(1...) custom-call(s32[2,8]{1,0:T(2,128)S(1)} %copy-done.2, s32[2,8]{1,0:T(2,128)S(1)} %slice_convert_fusion.1.upper_offsets_ref, ...), custom_call_target="tpu_custom_call" | custom-call | flops 16056320 | bytes 4816896 | tf_op jit(solution)/shard_map/pallas_call | solution.py:31
  35.6 1.5 %collective-permute-start.21 = (bf16[16,3200]{1,0:T(8,128)(2,1)S(1)}, bf16[16,3200]{1,0:T(8,128)(2,1)S(1)}, u32[]{:S(2)}, u32[]{:S(2)}) collective-permute-start(bf16[16,3200]{1,0:T(8,128)(2,1)S(1)} %get-tuple-element.34), channel_id=1, source_target_pairs={{0,16},{8,24},{16,0},{24,8},{1,17},{9,25},{17,1},{25,9},{2,18},{10... | collective-permute-start | bytes 307208 | tf_op jit(solution)/shard_map/ppermute | solution.py:44
  37.2 1.5 %collective-permute-start.22 = (bf16[16,3200]{1,0:T(8,128)(2,1)S(1)}, bf16[16,3200]{1,0:T(8,128)(2,1)S(1)}, u32[]{:S(2)}, u32[]{:S(2)}) collective-permute-start(bf16[16,3200]{1,0:T(8,128)(2,1)S(1)} %get-tuple-element.35), channel_id=1, source_target_pairs={{0,16},{8,24},{16,0},{24,8},{1,17},{9,25},{17,1},{25,9},{2,18},{10... | collective-permute-start | bytes 307208 | tf_op jit(solution)/shard_map/ppermute | solution.py:44
  38.7 2.5 %collective-permute-done.21.refs_19_ = bf16[16,3200]{1,0:T(8,128)(2,1)S(1)} collective-permute-done((bf16[16,3200]{1,0:T(8,128)(2,1)S(1)}, bf16[16,3200]{1,0:T(8,128)(2,1)S(1)}, u32[]{:S(2)}, u32[]{:S(2)}) %collective-permute-start.21) | collective-permute-done | bytes 102432 | tf_op jit(solution)/shard_map/ppermute | solution.py:44
  41.2 2.4 %collective-permute-done.22.refs_20_ = bf16[16,3200]{1,0:T(8,128)(2,1)S(1)} collective-permute-done((bf16[16,3200]{1,0:T(8,128)(2,1)S(1)}, bf16[16,3200]{1,0:T(8,128)(2,1)S(1)}, u32[]{:S(2)}, u32[]{:S(2)}) %collective-permute-start.22) | collective-permute-done | bytes 102432 | tf_op jit(solution)/shard_map/ppermute | solution.py:44
  43.7 2.7 %collective-permute-start.17 = (bf16[32,3200]{1,0:T(8,128)(2,1)S(1)}, bf16[32,3200]{1,0:T(8,128)(2,1)S(1)}, u32[]{:S(2)}, u32[]{:S(2)}) collective-permute-start(bf16[32,3200]{1,0:T(8,128)(2,1)S(1)} %collective-permute-done.15.refs_12_), channel_id=1, source_target_pairs={{0,7},{1,0},{2,1},{3,2},{4,3},{5,4},{6,5},{7,6},{8,15},{9,8},{10,9... | collective-permute-start | bytes 614408 | tf_op jit(solution)/shard_map/ppermute | solution.py:44
  46.4 2.6 %collective-permute-start.20 = (bf16[32,3200]{1,0:T(8,128)(2,1)S(1)}, bf16[32,3200]{1,0:T(8,128)(2,1)S(1)}, u32[]{:S(2)}, u32[]{:S(2)}) collective-permute-start(bf16[32,3200]{1,0:T(8,128)(2,1)S(1)} %get-tuple-element.33), channel_id=1, source_target_pairs={{0,24},{8,0},{16,8},{24,16},{1,25},{9,1},{17,9},{25,17},{2,26},{10... | collective-permute-start | bytes 614408 | tf_op jit(solution)/shard_map/ppermute | solution.py:44
  49.0 1.2 %collective-permute-done.19.refs_17_ = bf16[32,3200]{1,0:T(8,128)(2,1)S(1)} collective-permute-done((bf16[32,3200]{1,0:T(8,128)(2,1)S(1)}, bf16[32,3200]{1,0:T(8,128)(2,1)S(1)}, u32[]{:S(2)}, u32[]{:S(2)}) %collective-permute-start.19) | collective-permute-done | bytes 204832 | tf_op jit(solution)/shard_map/ppermute | solution.py:44
  50.4 1.5 %collective-permute-done.7.refs_5_ = bf16[32,3200]{1,0:T(8,128)(2,1)S(1)} collective-permute-done((bf16[32,3200]{1,0:T(8,128)(2,1)S(1)}, bf16[32,3200]{1,0:T(8,128)(2,1)S(1)}, u32[]{:S(2)}, u32[]{:S(2)}) %collective-permute-start.7) | collective-permute-done | bytes 204832 | tf_op jit(solution)/shard_map/ppermute | solution.py:44
  51.9 2.7 %collective-permute-start.18 = (bf16[32,3200]{1,0:T(8,128)(2,1)S(1)}, bf16[32,3200]{1,0:T(8,128)(2,1)S(1)}, u32[]{:S(2)}, u32[]{:S(2)}) collective-permute-start(bf16[32,3200]{1,0:T(8,128)(2,1)S(1)} %collective-permute-done.17.refs_14_), channel_id=1, source_target_pairs={{0,7},{1,0},{2,1},{3,2},{4,3},{5,4},{6,5},{7,6},{8,15},{9,8},{10,9... | collective-permute-start | bytes 614408 | tf_op jit(solution)/shard_map/ppermute | solution.py:44
  54.6 1.5 %collective-permute-done.16.refs_13_ = bf16[32,3200]{1,0:T(8,128)(2,1)S(1)} collective-permute-done((bf16[32,3200]{1,0:T(8,128)(2,1)S(1)}, bf16[32,3200]{1,0:T(8,128)(2,1)S(1)}, u32[]{:S(2)}, u32[]{:S(2)}) %collective-permute-start.16) | collective-permute-done | bytes 204832 | tf_op jit(solution)/shard_map/ppermute | solution.py:44
  56.1 4.3 %collective-permute-done.9.refs_7_ = bf16[32,3200]{1,0:T(8,128)(2,1)S(1)} collective-permute-done((bf16[32,3200]{1,0:T(8,128)(2,1)S(1)}, bf16[32,3200]{1,0:T(8,128)(2,1)S(1)}, u32[]{:S(2)}, u32[]{:S(2)}) %collective-permute-start.9) | collective-permute-done | bytes 204832 | tf_op jit(solution)/shard_map/ppermute | solution.py:44
  60.4 2.6 %shard_map.48 = (bf16[512,3200]{1,0:T(8,128)(2,1)S(1)}, bf16[1792,128]{1,0:T(8,128)(2,1)S(1)}) custom-call(bf16[32,3200]{1,0:T(8,128)(2,1)S(1)} %constant_dynamic-update-slice_fusion.refs_0_, bf16[32,3200]{1,0:T(8,128)(2,1)S(1)} %collective-permute-done.3.refs_1_, bf16[32,3200]{1,0:T(8,128)(2,1)S(1)} %collective-permute-done.4.refs_2_, ...), custom_call_target="tpu_custom_call" | custom-call | flops 2097152000 | bytes 9830400 | tf_op jit(solution)/shard_map/pallas_call | solution.py:31
  63.0 19.6 %all_to_all.10.parts_ref = bf16[32,56,128]{2,1,0:T(8,128)(2,1)S(1)} all-to-all(bf16[32,56,128]{2,1,0:T(8,128)(2,1)S(1)} %bitcast.3), channel_id=1, replica_groups=mesh['y'=4,'core'=2,'x'=4,'z'=8] {'core','x','y'}, dimensions={0} | all-to-all | bytes 917504 | tf_op jit(solution)/shard_map/all_to_all | solution.py:556
  82.7 14.4 %all_to_all.11 = bf16[32,56,128]{2,1,0:T(8,128)(2,1)S(1)} all-to-all(bf16[32,56,128]{2,1,0:T(8,128)(2,1)S(1)} %shard_map.49), channel_id=1, replica_groups=mesh['y'=4,'core'=2,'x'=4,'z'=8] {'core','x','y'}, dimensions={0} | all-to-all | bytes 917504 | tf_op jit(solution)/shard_map/all_to_all | solution.py:556
  97.1 3.7 %shard_map.50 = (bf16[32,3200]{1,0:T(8,128)(2,1)S(1)}, bf16[32,3200]{1,0:T(8,128)(2,1)S(1)}, bf16[32,3200]{1,0:T(8,128)(2,1)S(1)}, bf16[16,3200]{1,0:T(8,128)(2,1)S(1)}, bf16[16,3200]{1,0:T(8,128)(2,1)S(1)}) custom-call(bf16[1792,128]{1,0:T(8,128)(2,1)S(1)} %bitcast.2, bf16[512,3200]{1,0:T(8,128)(2,1)S(1)} %get-tuple-element.37.ordered_ref), custom_call_target="tpu_custom_call" | custom-call | flops 419430400 | bytes 6553600 | tf_op jit(solution)/shard_map/pallas_call | solution.py:31
  101.6 2.0 %collective-permute-start.24 = (bf16[32,3200]{1,0:T(8,128)(2,1)S(1)}, bf16[32,3200]{1,0:T(8,128)(2,1)S(1)}, u32[]{:S(2)}, u32[]{:S(2)}) collective-permute-start(bf16[32,3200]{1,0:T(8,128)(2,1)S(1)} %get-tuple-element.40), channel_id=1, source_target_pairs={{0,24},{8,0},{16,8},{24,16},{1,25},{9,1},{17,9},{25,17},{2,26},{10... | collective-permute-start | bytes 614408 | tf_op jit(solution)/shard_map/ppermute | solution.py:44
  103.7 2.9 %collective-permute-start.26 = (bf16[16,3200]{1,0:T(8,128)(2,1)S(1)}, bf16[16,3200]{1,0:T(8,128)(2,1)S(1)}, u32[]{:S(2)}, u32[]{:S(2)}) collective-permute-start(bf16[16,3200]{1,0:T(8,128)(2,1)S(1)} %get-tuple-element.42), channel_id=1, source_target_pairs={{0,16},{8,24},{16,0},{24,8},{1,17},{9,25},{17,1},{25,9},{2,18},{10... | collective-permute-start | bytes 307208 | tf_op jit(solution)/shard_map/ppermute | solution.py:44
  106.6 4.1 %collective-permute-done.25.half0 = bf16[16,3200]{1,0:T(8,128)(2,1)S(1)} collective-permute-done((bf16[16,3200]{1,0:T(8,128)(2,1)S(1)}, bf16[16,3200]{1,0:T(8,128)(2,1)S(1)}, u32[]{:S(2)}, u32[]{:S(2)}) %collective-permute-start.25) | collective-permute-done | bytes 102432 | tf_op jit(solution)/shard_map/ppermute | solution.py:44
  110.7 2.2 %collective-permute-done.26.half1 = bf16[16,3200]{1,0:T(8,128)(2,1)S(1)} collective-permute-done((bf16[16,3200]{1,0:T(8,128)(2,1)S(1)}, bf16[16,3200]{1,0:T(8,128)(2,1)S(1)}, u32[]{:S(2)}, u32[]{:S(2)}) %collective-permute-start.26) | collective-permute-done | bytes 102432 | tf_op jit(solution)/shard_map/ppermute | solution.py:44
  112.9 1.2 %shard_map.51 = f32[32,12544]{1,0:T(8,128)} custom-call(f32[32,12544]{1,0:T(8,128)S(1)} %get-tuple-element.26.eigen_ref, bf16[32,3200]{1,0:T(8,128)(2,1)S(1)} %get-tuple-element.38.mine, bf16[32,3200]{1,0:T(8,128)(2,1)S(1)} %collective-permute-done.23.one, bf16[32,3200]{1,0:T(8,128)(2,1)S(1)} %collective-permute-done.24.two, ...), custom_call_target="tpu_custom_call" | custom-call | flops 401408 | bytes 4014080 | tf_op jit(solution)/shard_map/pallas_call | solution.py:31
  (42 shorter events, 2.3 us)
Async XLA Ops:
  0.0 32.7 %copy-start.2 = (s32[2,8]{1,0:T(2,128)S(1)}, s32[2,8]{1,0:T(2,128)}, u32[]{:S(2)}) copy-start(s32[2,8]{1,0:T(2,128)} %offsets_ref.3) | copy-start | bytes 196
  0.0 32.7 %copy-start.1 = (f32[2,8,4,128]{3,2,1,0:T(4,128)S(1)}, f32[2,8,4,128]{3,2,1,0:T(4,128)}, u32[]{:S(2)}) copy-start(f32[2,8,4,128]{3,2,1,0:T(4,128)} %vectors_ref.3) | copy-start | bytes 98308
  0.0 32.7 %copy-start = (f32[32,12544]{1,0:T(8,128)S(1)}, f32[32,12544]{1,0:T(8,128)}, u32[]{:S(2)}) copy-start(f32[32,12544]{1,0:T(8,128)} %own_ref.1) | copy-start | bytes 4816900
  2.2 12.5 %collective-permute-start.2 = (bf16[16,3200]{1,0:T(8,128)(2,1)}, bf16[16,3200]{1,0:T(8,128)(2,1)S(1)}, u32[]{:S(2)}, u32[]{:S(2)}) collective-permute-start(bf16[16,3200]{1,0:T(8,128)(2,1)} %get-tuple-element.28), channel_id=1, source_target_pairs={{0,8},{8,16},{16,24},{24,0},{1,9},{9,17},{17,25},{25,1},{2,10},{10... | collective-permute-start | bytes 307208 | tf_op jit(solution)/shard_map/ppermute | solution.py:44
  4.3 16.1 %collective-permute-start.10 = (bf16[16,3200]{1,0:T(8,128)(2,1)}, bf16[16,3200]{1,0:T(8,128)(2,1)S(1)}, u32[]{:S(2)}, u32[]{:S(2)}) collective-permute-start(bf16[16,3200]{1,0:T(8,128)(2,1)} %get-tuple-element.29), channel_id=1, source_target_pairs={{0,24},{8,0},{16,8},{24,16},{1,25},{9,1},{17,9},{25,17},{2,26},{10... | collective-permute-start | bytes 307208 | tf_op jit(solution)/shard_map/ppermute | solution.py:44
  5.6 14.8 %collective-permute-start.11 = (bf16[16,3200]{1,0:T(8,128)(2,1)}, bf16[16,3200]{1,0:T(8,128)(2,1)S(1)}, u32[]{:S(2)}, u32[]{:S(2)}) collective-permute-start(bf16[16,3200]{1,0:T(8,128)(2,1)} %get-tuple-element.30), channel_id=1, source_target_pairs={{0,16},{8,24},{16,0},{24,8},{1,17},{9,25},{17,1},{25,9},{2,18},{10... | collective-permute-start | bytes 307208 | tf_op jit(solution)/shard_map/ppermute | solution.py:44
  7.3 15.9 %collective-permute-start.1 = (f32[32,1408]{1,0:T(8,128)}, f32[32,1408]{1,0:T(8,128)S(1)}, u32[]{:S(2)}, u32[]{:S(2)}) collective-permute-start(f32[32,1408]{1,0:T(8,128)} %get-tuple-element.25), channel_id=1, source_target_pairs={{32,0},{64,32},{96,64},{128,96},{160,128},{192,160},{224,192},{33,... | collective-permute-start | bytes 540680 | tf_op jit(solution)/shard_map/ppermute | solution.py:50
  10.7 22.0 %collective-permute-start = (f32[32,2432]{1,0:T(8,128)}, f32[32,2432]{1,0:T(8,128)S(1)}, u32[]{:S(2)}, u32[]{:S(2)}) collective-permute-start(f32[32,2432]{1,0:T(8,128)} %get-tuple-element.24), channel_id=1, source_target_pairs={{0,32},{32,64},{64,96},{96,128},{128,160},{160,192},{192,224},{1,3... | collective-permute-start | bytes 933896 | tf_op jit(solution)/shard_map/ppermute | solution.py:50
  14.7 22.4 %collective-permute-start.4 = (bf16[32,3200]{1,0:T(8,128)(2,1)S(1)}, bf16[32,3200]{1,0:T(8,128)(2,1)S(1)}, u32[]{:S(2)}, u32[]{:S(2)}) collective-permute-start(bf16[32,3200]{1,0:T(8,128)(2,1)S(1)} %constant_dynamic-update-slice_fusion.refs_0_), channel_id=1, source_target_pairs={{0,7},{1,0},{2,1},{3,2},{4,3},{5,4},{6,5},{7,6},{8,15},{9,8},{10,9... | collective-permute-start | bytes 614408 | tf_op jit(solution)/shard_map/ppermute | solution.py:44
  20.4 8.2 %collective-permute-start.3 = (bf16[32,3200]{1,0:T(8,128)(2,1)S(1)}, bf16[32,3200]{1,0:T(8,128)(2,1)S(1)}, u32[]{:S(2)}, u32[]{:S(2)}) collective-permute-start(bf16[32,3200]{1,0:T(8,128)(2,1)S(1)} %constant_dynamic-update-slice_fusion.refs_0_), channel_id=1, source_target_pairs={{0,1},{1,2},{2,3},{3,4},{4,5},{5,6},{6,7},{7,0},{8,9},{9,10},{10,1... | collective-permute-start | bytes 614408 | tf_op jit(solution)/shard_map/ppermute | solution.py:44
  20.4 9.0 %collective-permute-start.13 = (bf16[32,3200]{1,0:T(8,128)(2,1)S(1)}, bf16[32,3200]{1,0:T(8,128)(2,1)S(1)}, u32[]{:S(2)}, u32[]{:S(2)}) collective-permute-start(bf16[32,3200]{1,0:T(8,128)(2,1)S(1)} %constant_dynamic-update-slice_fusion.2.refs_8_), channel_id=1, source_target_pairs={{0,7},{1,0},{2,1},{3,2},{4,3},{5,4},{6,5},{7,6},{8,15},{9,8},{10,9... | collective-permute-start | bytes 614408 | tf_op jit(solution)/shard_map/ppermute | solution.py:44
  23.2 15.5 %collective-permute-start.12 = (bf16[32,3200]{1,0:T(8,128)(2,1)S(1)}, bf16[32,3200]{1,0:T(8,128)(2,1)S(1)}, u32[]{:S(2)}, u32[]{:S(2)}) collective-permute-start(bf16[32,3200]{1,0:T(8,128)(2,1)S(1)} %constant_dynamic-update-slice_fusion.2.refs_8_), channel_id=1, source_target_pairs={{0,1},{1,2},{2,3},{3,4},{4,5},{5,6},{6,7},{7,0},{8,9},{9,10},{10,1... | collective-permute-start | bytes 614408 | tf_op jit(solution)/shard_map/ppermute | solution.py:44
  28.6 15.0 %collective-permute-start.5 = (bf16[32,3200]{1,0:T(8,128)(2,1)S(1)}, bf16[32,3200]{1,0:T(8,128)(2,1)S(1)}, u32[]{:S(2)}, u32[]{:S(2)}) collective-permute-start(bf16[32,3200]{1,0:T(8,128)(2,1)S(1)} %collective-permute-done.3.refs_1_), channel_id=1, source_target_pairs={{0,1},{1,2},{2,3},{3,4},{4,5},{5,6},{6,7},{7,0},{8,9},{9,10},{10,1... | collective-permute-start | bytes 614408 | tf_op jit(solution)/shard_map/ppermute | solution.py:44
  29.5 14.2 %collective-permute-start.15 = (bf16[32,3200]{1,0:T(8,128)(2,1)S(1)}, bf16[32,3200]{1,0:T(8,128)(2,1)S(1)}, u32[]{:S(2)}, u32[]{:S(2)}) collective-permute-start(bf16[32,3200]{1,0:T(8,128)(2,1)S(1)} %collective-permute-done.13.refs_10_), channel_id=1, source_target_pairs={{0,7},{1,0},{2,1},{3,2},{4,3},{5,4},{6,5},{7,6},{8,15},{9,8},{10,9... | collective-permute-start | bytes 614408 | tf_op jit(solution)/shard_map/ppermute | solution.py:44
  35.6 5.5 %collective-permute-start.21 = (bf16[16,3200]{1,0:T(8,128)(2,1)S(1)}, bf16[16,3200]{1,0:T(8,128)(2,1)S(1)}, u32[]{:S(2)}, u32[]{:S(2)}) collective-permute-start(bf16[16,3200]{1,0:T(8,128)(2,1)S(1)} %get-tuple-element.34), channel_id=1, source_target_pairs={{0,16},{8,24},{16,0},{24,8},{1,17},{9,25},{17,1},{25,9},{2,18},{10... | collective-permute-start | bytes 307208 | tf_op jit(solution)/shard_map/ppermute | solution.py:44
  37.2 6.4 %collective-permute-start.22 = (bf16[16,3200]{1,0:T(8,128)(2,1)S(1)}, bf16[16,3200]{1,0:T(8,128)(2,1)S(1)}, u32[]{:S(2)}, u32[]{:S(2)}) collective-permute-start(bf16[16,3200]{1,0:T(8,128)(2,1)S(1)} %get-tuple-element.35), channel_id=1, source_target_pairs={{0,16},{8,24},{16,0},{24,8},{1,17},{9,25},{17,1},{25,9},{2,18},{10... | collective-permute-start | bytes 307208 | tf_op jit(solution)/shard_map/ppermute | solution.py:44
  38.7 7.7 %collective-permute-start.6 = (bf16[32,3200]{1,0:T(8,128)(2,1)S(1)}, bf16[32,3200]{1,0:T(8,128)(2,1)S(1)}, u32[]{:S(2)}, u32[]{:S(2)}) collective-permute-start(bf16[32,3200]{1,0:T(8,128)(2,1)S(1)} %collective-permute-done.4.refs_2_), channel_id=1, source_target_pairs={{0,7},{1,0},{2,1},{3,2},{4,3},{5,4},{6,5},{7,6},{8,15},{9,8},{10,9... | collective-permute-start | bytes 614408 | tf_op jit(solution)/shard_map/ppermute | solution.py:44
  41.2 7.8 %collective-permute-start.14 = (bf16[32,3200]{1,0:T(8,128)(2,1)S(1)}, bf16[32,3200]{1,0:T(8,128)(2,1)S(1)}, u32[]{:S(2)}, u32[]{:S(2)}) collective-permute-start(bf16[32,3200]{1,0:T(8,128)(2,1)S(1)} %collective-permute-done.12.refs_9_), channel_id=1, source_target_pairs={{0,1},{1,2},{2,3},{3,4},{4,5},{5,6},{6,7},{7,0},{8,9},{9,10},{10,1... | collective-permute-start | bytes 614408 | tf_op jit(solution)/shard_map/ppermute | solution.py:44
  43.6 6.7 %collective-permute-start.19 = (bf16[32,3200]{1,0:T(8,128)(2,1)S(1)}, bf16[32,3200]{1,0:T(8,128)(2,1)S(1)}, u32[]{:S(2)}, u32[]{:S(2)}) collective-permute-start(bf16[32,3200]{1,0:T(8,128)(2,1)S(1)} %get-tuple-element.32), channel_id=1, source_target_pairs={{0,8},{8,16},{16,24},{24,0},{1,9},{9,17},{17,25},{25,1},{2,10},{10... | collective-permute-start | bytes 614408 | tf_op jit(solution)/shard_map/ppermute | solution.py:44
  43.7 8.2 %collective-permute-start.7 = (bf16[32,3200]{1,0:T(8,128)(2,1)S(1)}, bf16[32,3200]{1,0:T(8,128)(2,1)S(1)}, u32[]{:S(2)}, u32[]{:S(2)}) collective-permute-start(bf16[32,3200]{1,0:T(8,128)(2,1)S(1)} %collective-permute-done.5.refs_3_), channel_id=1, source_target_pairs={{0,1},{1,2},{2,3},{3,4},{4,5},{5,6},{6,7},{7,0},{8,9},{9,10},{10,1... | collective-permute-start | bytes 614408 | tf_op jit(solution)/shard_map/ppermute | solution.py:44
  43.7 8.2 %collective-permute-start.17 = (bf16[32,3200]{1,0:T(8,128)(2,1)S(1)}, bf16[32,3200]{1,0:T(8,128)(2,1)S(1)}, u32[]{:S(2)}, u32[]{:S(2)}) collective-permute-start(bf16[32,3200]{1,0:T(8,128)(2,1)S(1)} %collective-permute-done.15.refs_12_), channel_id=1, source_target_pairs={{0,7},{1,0},{2,1},{3,2},{4,3},{5,4},{6,5},{7,6},{8,15},{9,8},{10,9... | collective-permute-start | bytes 614408 | tf_op jit(solution)/shard_map/ppermute | solution.py:44
  46.4 8.2 %collective-permute-start.20 = (bf16[32,3200]{1,0:T(8,128)(2,1)S(1)}, bf16[32,3200]{1,0:T(8,128)(2,1)S(1)}, u32[]{:S(2)}, u32[]{:S(2)}) collective-permute-start(bf16[32,3200]{1,0:T(8,128)(2,1)S(1)} %get-tuple-element.33), channel_id=1, source_target_pairs={{0,24},{8,0},{16,8},{24,16},{1,25},{9,1},{17,9},{25,17},{2,26},{10... | collective-permute-start | bytes 614408 | tf_op jit(solution)/shard_map/ppermute | solution.py:44
  48.9 5.7 %collective-permute-start.8 = (bf16[32,3200]{1,0:T(8,128)(2,1)S(1)}, bf16[32,3200]{1,0:T(8,128)(2,1)S(1)}, u32[]{:S(2)}, u32[]{:S(2)}) collective-permute-start(bf16[32,3200]{1,0:T(8,128)(2,1)S(1)} %collective-permute-done.6.refs_4_), channel_id=1, source_target_pairs={{0,7},{1,0},{2,1},{3,2},{4,3},{5,4},{6,5},{7,6},{8,15},{9,8},{10,9... | collective-permute-start | bytes 614408 | tf_op jit(solution)/shard_map/ppermute | solution.py:44
  50.3 5.8 %collective-permute-start.16 = (bf16[32,3200]{1,0:T(8,128)(2,1)S(1)}, bf16[32,3200]{1,0:T(8,128)(2,1)S(1)}, u32[]{:S(2)}, u32[]{:S(2)}) collective-permute-start(bf16[32,3200]{1,0:T(8,128)(2,1)S(1)} %collective-permute-done.14.refs_11_), channel_id=1, source_target_pairs={{0,1},{1,2},{2,3},{3,4},{4,5},{5,6},{6,7},{7,0},{8,9},{9,10},{10,1... | collective-permute-start | bytes 614408 | tf_op jit(solution)/shard_map/ppermute | solution.py:44
  51.9 8.5 %collective-permute-start.9 = (bf16[32,3200]{1,0:T(8,128)(2,1)S(1)}, bf16[32,3200]{1,0:T(8,128)(2,1)S(1)}, u32[]{:S(2)}, u32[]{:S(2)}) collective-permute-start(bf16[32,3200]{1,0:T(8,128)(2,1)S(1)} %collective-permute-done.7.refs_5_), channel_id=1, source_target_pairs={{0,1},{1,2},{2,3},{3,4},{4,5},{5,6},{6,7},{7,0},{8,9},{9,10},{10,1... | collective-permute-start | bytes 614408 | tf_op jit(solution)/shard_map/ppermute | solution.py:44
  51.9 8.5 %collective-permute-start.18 = (bf16[32,3200]{1,0:T(8,128)(2,1)S(1)}, bf16[32,3200]{1,0:T(8,128)(2,1)S(1)}, u32[]{:S(2)}, u32[]{:S(2)}) collective-permute-start(bf16[32,3200]{1,0:T(8,128)(2,1)S(1)} %collective-permute-done.17.refs_14_), channel_id=1, source_target_pairs={{0,7},{1,0},{2,1},{3,2},{4,3},{5,4},{6,5},{7,6},{8,15},{9,8},{10,9... | collective-permute-start | bytes 614408 | tf_op jit(solution)/shard_map/ppermute | solution.py:44
  100.8 12.1 %collective-permute-start.23 = (bf16[32,3200]{1,0:T(8,128)(2,1)S(1)}, bf16[32,3200]{1,0:T(8,128)(2,1)S(1)}, u32[]{:S(2)}, u32[]{:S(2)}) collective-permute-start(bf16[32,3200]{1,0:T(8,128)(2,1)S(1)} %get-tuple-element.39), channel_id=1, source_target_pairs={{0,8},{8,16},{16,24},{24,0},{1,9},{9,17},{17,25},{25,1},{2,10},{10... | collective-permute-start | bytes 614408 | tf_op jit(solution)/shard_map/ppermute | solution.py:44
  101.6 11.3 %collective-permute-start.24 = (bf16[32,3200]{1,0:T(8,128)(2,1)S(1)}, bf16[32,3200]{1,0:T(8,128)(2,1)S(1)}, u32[]{:S(2)}, u32[]{:S(2)}) collective-permute-start(bf16[32,3200]{1,0:T(8,128)(2,1)S(1)} %get-tuple-element.40), channel_id=1, source_target_pairs={{0,24},{8,0},{16,8},{24,16},{1,25},{9,1},{17,9},{25,17},{2,26},{10... | collective-permute-start | bytes 614408 | tf_op jit(solution)/shard_map/ppermute | solution.py:44
  103.6 7.1 %collective-permute-start.25 = (bf16[16,3200]{1,0:T(8,128)(2,1)S(1)}, bf16[16,3200]{1,0:T(8,128)(2,1)S(1)}, u32[]{:S(2)}, u32[]{:S(2)}) collective-permute-start(bf16[16,3200]{1,0:T(8,128)(2,1)S(1)} %get-tuple-element.41), channel_id=1, source_target_pairs={{0,16},{8,24},{16,0},{24,8},{1,17},{9,25},{17,1},{25,9},{2,18},{10... | collective-permute-start | bytes 307208 | tf_op jit(solution)/shard_map/ppermute | solution.py:44
  103.7 9.2 %collective-permute-start.26 = (bf16[16,3200]{1,0:T(8,128)(2,1)S(1)}, bf16[16,3200]{1,0:T(8,128)(2,1)S(1)}, u32[]{:S(2)}, u32[]{:S(2)}) collective-permute-start(bf16[16,3200]{1,0:T(8,128)(2,1)S(1)} %get-tuple-element.42), channel_id=1, source_target_pairs={{0,16},{8,24},{16,0},{24,8},{1,17},{9,25},{17,1},{25,9},{2,18},{10... | collective-permute-start | bytes 307208 | tf_op jit(solution)/shard_map/ppermute | solution.py:44

commit v7 on v6

--- a/solution.py
+++ b/solution.py
@@ -11,7 +11,7 @@
 
 COL = ("x", "z")
 ROW = ("y", "core")
-SUM_AXES = ("core", "x", "y")
+SUM_AXES = ("y", "x", "core")
 X_SIZE, Z_SIZE = 4, 8
 LANE = 128
 GROUP = 4
@@ -212,7 +212,7 @@
 def sweep_kernel(
     offsets_ref, upper_offsets_ref, lower_offsets_ref,
     vectors_ref, own_ref, upper_ref, lower_ref,
-    out_ref, mine_ref, next_ref, last_ref, one_ref, two_ref,
+    out_ref, mine_ref, next_ref, last_ref, far_ref,
     state_ref, pairs_ref, rounded_ref,
 ):
     sweeps, spans, refl, band = vectors_ref.shape
@@ -269,10 +269,9 @@
     rounded_ref[:, 0:columns] = state_ref[:, left : left + columns].astype(BF16)
     rounded_ref[:, columns:] = jnp.zeros((rows, padded - columns), BF16)
     cut = mine_ref.shape[1]
-    half = rows // 2
     targets = (
         (0, 0, mine_ref), (PEERS[0], 0, next_ref), (PEERS[1], 0, last_ref),
-        (PEERS[2], 0, one_ref), (PEERS[2], half, two_ref),
+        (PEERS[2], 0, far_ref),
     )
     for step, row, ref in targets:
         at = pl.multiple_of((lax.axis_index("x") + step) % X_SIZE * cut, LANE)
@@ -291,7 +290,7 @@
     return call(
         sweep_kernel,
         [jax.ShapeDtypeStruct(eigen.shape, F32)]
-        + piece_shapes(rows, cut),
+        + [jax.ShapeDtypeStruct((rows, cut), BF16)] * 4,
         [SM] * 3 + [VM] * 4,
         (offsets, upper_offsets, lower_offsets, vectors, eigen, upper, lower),
         [
@@ -330,8 +329,8 @@
 
 
 def products_kernel(*refs, spots, own, rows):
-    blocks, (mine, one, two, half0, half1) = refs[: len(spots)], refs[len(spots) : len(spots) + 5]
-    ordered_ref, sums_ref, eigen_ref = refs[len(spots) + 5 :]
+    blocks, (mine, one, two, far) = refs[: len(spots)], refs[len(spots) : len(spots) + 4]
+    ordered_ref, sums_ref, eigen_ref = refs[len(spots) + 4 :]
     order = ordered_ref.shape[0]
     x, z = lax.axis_index("x"), lax.axis_index("z")
     for ref, units in zip(blocks, spots):
@@ -339,7 +338,7 @@
             source = (x + X_SIZE - back_x) % X_SIZE * Z_SIZE + (z + Z_SIZE - back_z) % Z_SIZE
             to = pl.multiple_of(panel * (order // 2) + source * own, UNIT)
             ordered_ref[pl.ds(to, own), :] = ref[at * own : (at + 1) * own, :]
-    sources = ((0, 0, mine), (1, 0, one), (3, 0, two), (2, 0, half0), (2, rows // 2, half1))
+    sources = ((0, 0, mine), (1, 0, one), (3, 0, two), (2, 0, far))
     for back, row, ref in sources:
         to = pl.multiple_of((x + X_SIZE - back) % X_SIZE * rows + row, UNIT)
         eigen_ref[pl.ds(to, ref.shape[0]), :] = ref[...]

time: 115 us -> 111 us (0.965)
  waiting for transfers between devices: 26 us -> 17.6 us
  starting transfers between devices: 40.3 us -> 44.4 us
    ppermute x25 -> x24, waiting for transfers between devices: 26 us -> 17.6 us  [shifted(): lax.ppermute(value, axis, [(at, (at + steps) % count) for at in range(cou...]
    ppermute x25 -> x24, starting transfers between devices: 33.8 us -> 37.9 us  [shifted(): lax.ppermute(value, axis, [(at, (at + steps) % count) for at in range(cou...]
  transfers between devices with their start and end apart: 27 -> 26, of which waited for: 10 -> 9; matrix products, arithmetic and copies ran while one was open for 1% -> 1% of each run, Pallas kernels for 3% -> 3%
where the time goes in v7:
time: 111 us
  starting transfers between devices  44.4 us (40%)
  blocking collectives  35.1 us (32%)
  waiting for transfers between devices  17.6 us (16%)
  Pallas kernels  12.8 us (12%)
    ppermute x24, starting transfers between devices, shifted(): lax.ppermute(value, axis, [(at, (at + steps) % count) for at in range(cou...  37.9 us
    all_to_all x2, blocking collectives, exchange(): return lax.all_to_all(pieces, axes, 0, 0, tiled=True)  35.1 us
    ppermute x24, waiting for transfers between devices, shifted(): lax.ppermute(value, axis, [(at, (at + steps) % count) for at in range(cou...  17.6 us
    pallas_call x6, Pallas kernels, call(): pl.pallas_call(kernel, out_shape=out_shape, in_specs=in_specs, out_specs=...  12.8 us
    ppermute x2, starting transfers between devices, from_behind(): lax.ppermute(value, axis, [(source, source + steps) for source in range(f...  6.51 us
  transfers between devices with their start and end apart: 26, of which 9 were waited for; matrix products, arithmetic and copies ran while one was open for 1% of the time, Pallas kernels for 3%

profile of v7, /device:TPU:1, one launch (start us, length us, event | category | flops | bytes accessed | tf_op | source)
XLA Modules:
  0.0 111.1 jit_solution(12671726901603120743)
XLA Ops:
  0.0 2.2 %shard_map.46 = (bf16[16,3200]{1,0:T(8,128)(2,1)}, bf16[16,3200]{1,0:T(8,128)(2,1)}, bf16[16,3200]{1,0:T(8,128)(2,1)}, bf16[16,3200]{1,0:T(8,128)(2,1)}, f32[32,2432]{1,0:T(8,128)}, /*index=5*/f32[32,1408]{1,0:T(8,128)}) custom-call(s32[2,8]{1,0:T(2,128)} %offsets_ref.3, f32[2,8,4,128]{3,2,1,0:T(4,128)} %vectors_ref.3, bf16[2,8,12544]{2,1,0:T(8,128)(2,1)} %panels_ref.1, ...), custom_call_target="tpu_custom_call" | custom-call | flops 200704 | bytes 802816 | tf_op jit(solution)/shard_map/pallas_call | solution.py:31
  2.2 2.1 %collective-permute-start.2 = (bf16[16,3200]{1,0:T(8,128)(2,1)}, bf16[16,3200]{1,0:T(8,128)(2,1)S(1)}, u32[]{:S(2)}, u32[]{:S(2)}) collective-permute-start(bf16[16,3200]{1,0:T(8,128)(2,1)} %get-tuple-element.27), channel_id=1, source_target_pairs={{0,8},{8,16},{16,24},{24,0},{1,9},{9,17},{17,25},{25,1},{2,10},{10... | collective-permute-start | bytes 307208 | tf_op jit(solution)/shard_map/ppermute | solution.py:44
  4.3 1.4 %collective-permute-start.10 = (bf16[16,3200]{1,0:T(8,128)(2,1)}, bf16[16,3200]{1,0:T(8,128)(2,1)S(1)}, u32[]{:S(2)}, u32[]{:S(2)}) collective-permute-start(bf16[16,3200]{1,0:T(8,128)(2,1)} %get-tuple-element.28), channel_id=1, source_target_pairs={{0,24},{8,0},{16,8},{24,16},{1,25},{9,1},{17,9},{25,17},{2,26},{10... | collective-permute-start | bytes 307208 | tf_op jit(solution)/shard_map/ppermute | solution.py:44
  5.6 1.6 %collective-permute-start.11 = (bf16[16,3200]{1,0:T(8,128)(2,1)}, bf16[16,3200]{1,0:T(8,128)(2,1)S(1)}, u32[]{:S(2)}, u32[]{:S(2)}) collective-permute-start(bf16[16,3200]{1,0:T(8,128)(2,1)} %get-tuple-element.29), channel_id=1, source_target_pairs={{0,16},{8,24},{16,0},{24,8},{1,17},{9,25},{17,1},{25,9},{2,18},{10... | collective-permute-start | bytes 307208 | tf_op jit(solution)/shard_map/ppermute | solution.py:44
  7.3 3.4 %collective-permute-start.1 = (f32[32,1408]{1,0:T(8,128)}, f32[32,1408]{1,0:T(8,128)S(1)}, u32[]{:S(2)}, u32[]{:S(2)}) collective-permute-start(f32[32,1408]{1,0:T(8,128)} %get-tuple-element.24), channel_id=1, source_target_pairs={{32,0},{64,32},{96,64},{128,96},{160,128},{192,160},{224,192},{33,... | collective-permute-start | bytes 540680 | tf_op jit(solution)/shard_map/ppermute | solution.py:50
  10.7 3.1 %collective-permute-start = (f32[32,2432]{1,0:T(8,128)}, f32[32,2432]{1,0:T(8,128)S(1)}, u32[]{:S(2)}, u32[]{:S(2)}) collective-permute-start(f32[32,2432]{1,0:T(8,128)} %get-tuple-element.23), channel_id=1, source_target_pairs={{0,32},{32,64},{64,96},{96,128},{128,160},{160,192},{192,224},{1,3... | collective-permute-start | bytes 933896 | tf_op jit(solution)/shard_map/ppermute | solution.py:50
  13.8 0.9 constant_dynamic-update-slice_fusion.1
  14.7 5.7 %collective-permute-start.4 = (bf16[32,3200]{1,0:T(8,128)(2,1)S(1)}, bf16[32,3200]{1,0:T(8,128)(2,1)S(1)}, u32[]{:S(2)}, u32[]{:S(2)}) collective-permute-start(bf16[32,3200]{1,0:T(8,128)(2,1)S(1)} %constant_dynamic-update-slice_fusion.refs_0_), channel_id=1, source_target_pairs={{0,7},{1,0},{2,1},{3,2},{4,3},{5,4},{6,5},{7,6},{8,15},{9,8},{10,9... | collective-permute-start | bytes 614408 | tf_op jit(solution)/shard_map/ppermute | solution.py:44
  20.4 2.7 %collective-permute-start.13 = (bf16[32,3200]{1,0:T(8,128)(2,1)S(1)}, bf16[32,3200]{1,0:T(8,128)(2,1)S(1)}, u32[]{:S(2)}, u32[]{:S(2)}) collective-permute-start(bf16[32,3200]{1,0:T(8,128)(2,1)S(1)} %constant_dynamic-update-slice_fusion.2.refs_8_), channel_id=1, source_target_pairs={{0,7},{1,0},{2,1},{3,2},{4,3},{5,4},{6,5},{7,6},{8,15},{9,8},{10,9... | collective-permute-start | bytes 614408 | tf_op jit(solution)/shard_map/ppermute | solution.py:44
  23.2 2.1 %collective-permute-done.4.refs_2_ = bf16[32,3200]{1,0:T(8,128)(2,1)S(1)} collective-permute-done((bf16[32,3200]{1,0:T(8,128)(2,1)S(1)}, bf16[32,3200]{1,0:T(8,128)(2,1)S(1)}, u32[]{:S(2)}, u32[]{:S(2)}) %collective-permute-start.4) | collective-permute-done | bytes 204832 | tf_op jit(solution)/shard_map/ppermute | solution.py:44
  25.3 3.4 %collective-permute-start.6 = (bf16[32,3200]{1,0:T(8,128)(2,1)S(1)}, bf16[32,3200]{1,0:T(8,128)(2,1)S(1)}, u32[]{:S(2)}, u32[]{:S(2)}) collective-permute-start(bf16[32,3200]{1,0:T(8,128)(2,1)S(1)} %collective-permute-done.4.refs_2_), channel_id=1, source_target_pairs={{0,7},{1,0},{2,1},{3,2},{4,3},{5,4},{6,5},{7,6},{8,15},{9,8},{10,9... | collective-permute-start | bytes 614408 | tf_op jit(solution)/shard_map/ppermute | solution.py:44
  28.7 0.8 collective-permute-done.13.refs_10_
  29.5 3.2 %collective-permute-start.15 = (bf16[32,3200]{1,0:T(8,128)(2,1)S(1)}, bf16[32,3200]{1,0:T(8,128)(2,1)S(1)}, u32[]{:S(2)}, u32[]{:S(2)}) collective-permute-start(bf16[32,3200]{1,0:T(8,128)(2,1)S(1)} %collective-permute-done.13.refs_10_), channel_id=1, source_target_pairs={{0,7},{1,0},{2,1},{3,2},{4,3},{5,4},{6,5},{7,6},{8,15},{9,8},{10,9... | collective-permute-start | bytes 614408 | tf_op jit(solution)/shard_map/ppermute | solution.py:44
  33.1 2.9 %shard_map.47 = (f32[32,12544]{1,0:T(8,128)S(1)}, bf16[32,3200]{1,0:T(8,128)(2,1)S(1)}, bf16[32,3200]{1,0:T(8,128)(2,1)S(1)}, bf16[32,3200]{1,0:T(8,128)(2,1)S(1)}, bf16[32,3200]{1,0:T(8,128)(2,1)S(1)}) custom-call(s32[2,8]{1,0:T(2,128)S(1)} %copy-done.2, s32[2,8]{1,0:T(2,128)S(1)} %slice_convert_fusion.1.upper_offsets_ref, ...), custom_call_target="tpu_custom_call" | custom-call | flops 16056320 | bytes 4816896 | tf_op jit(solution)/shard_map/pallas_call | solution.py:31
  36.4 2.4 %collective-permute-start.20 = (bf16[32,3200]{1,0:T(8,128)(2,1)S(1)}, bf16[32,3200]{1,0:T(8,128)(2,1)S(1)}, u32[]{:S(2)}, u32[]{:S(2)}) collective-permute-start(bf16[32,3200]{1,0:T(8,128)(2,1)S(1)} %get-tuple-element.32), channel_id=1, source_target_pairs={{0,24},{8,0},{16,8},{24,16},{1,25},{9,1},{17,9},{25,17},{2,26},{10... | collective-permute-start | bytes 614408 | tf_op jit(solution)/shard_map/ppermute | solution.py:44
  38.8 2.7 %collective-permute-start.17 = (bf16[32,3200]{1,0:T(8,128)(2,1)S(1)}, bf16[32,3200]{1,0:T(8,128)(2,1)S(1)}, u32[]{:S(2)}, u32[]{:S(2)}) collective-permute-start(bf16[32,3200]{1,0:T(8,128)(2,1)S(1)} %collective-permute-done.15.refs_12_), channel_id=1, source_target_pairs={{0,7},{1,0},{2,1},{3,2},{4,3},{5,4},{6,5},{7,6},{8,15},{9,8},{10,9... | collective-permute-start | bytes 614408 | tf_op jit(solution)/shard_map/ppermute | solution.py:44
  41.5 1.4 %collective-permute-start.21 = (bf16[32,3200]{1,0:T(8,128)(2,1)S(1)}, bf16[32,3200]{1,0:T(8,128)(2,1)S(1)}, u32[]{:S(2)}, u32[]{:S(2)}) collective-permute-start(bf16[32,3200]{1,0:T(8,128)(2,1)S(1)} %get-tuple-element.33), channel_id=1, source_target_pairs={{0,16},{8,24},{16,0},{24,8},{1,17},{9,25},{17,1},{25,9},{2,18},{10... | collective-permute-start | bytes 614408 | tf_op jit(solution)/shard_map/ppermute | solution.py:44
  42.9 0.6 collective-permute-done.19.refs_17_
  43.6 2.4 %collective-permute-start.8 = (bf16[32,3200]{1,0:T(8,128)(2,1)S(1)}, bf16[32,3200]{1,0:T(8,128)(2,1)S(1)}, u32[]{:S(2)}, u32[]{:S(2)}) collective-permute-start(bf16[32,3200]{1,0:T(8,128)(2,1)S(1)} %collective-permute-done.6.refs_4_), channel_id=1, source_target_pairs={{0,7},{1,0},{2,1},{3,2},{4,3},{5,4},{6,5},{7,6},{8,15},{9,8},{10,9... | collective-permute-start | bytes 614408 | tf_op jit(solution)/shard_map/ppermute | solution.py:44
  46.1 2.7 %collective-permute-start.18 = (bf16[32,3200]{1,0:T(8,128)(2,1)S(1)}, bf16[32,3200]{1,0:T(8,128)(2,1)S(1)}, u32[]{:S(2)}, u32[]{:S(2)}) collective-permute-start(bf16[32,3200]{1,0:T(8,128)(2,1)S(1)} %collective-permute-done.17.refs_14_), channel_id=1, source_target_pairs={{0,7},{1,0},{2,1},{3,2},{4,3},{5,4},{6,5},{7,6},{8,15},{9,8},{10,9... | collective-permute-start | bytes 614408 | tf_op jit(solution)/shard_map/ppermute | solution.py:44
  49.0 2.8 %collective-permute-done.16.refs_13_ = bf16[32,3200]{1,0:T(8,128)(2,1)S(1)} collective-permute-done((bf16[32,3200]{1,0:T(8,128)(2,1)S(1)}, bf16[32,3200]{1,0:T(8,128)(2,1)S(1)}, u32[]{:S(2)}, u32[]{:S(2)}) %collective-permute-start.16) | collective-permute-done | bytes 204832 | tf_op jit(solution)/shard_map/ppermute | solution.py:44
  51.8 3.9 %collective-permute-done.9.refs_7_ = bf16[32,3200]{1,0:T(8,128)(2,1)S(1)} collective-permute-done((bf16[32,3200]{1,0:T(8,128)(2,1)S(1)}, bf16[32,3200]{1,0:T(8,128)(2,1)S(1)}, u32[]{:S(2)}, u32[]{:S(2)}) %collective-permute-start.9) | collective-permute-done | bytes 204832 | tf_op jit(solution)/shard_map/ppermute | solution.py:44
  55.7 2.6 %shard_map.48 = (bf16[512,3200]{1,0:T(8,128)(2,1)S(1)}, bf16[1792,128]{1,0:T(8,128)(2,1)S(1)}) custom-call(bf16[32,3200]{1,0:T(8,128)(2,1)S(1)} %constant_dynamic-update-slice_fusion.refs_0_, bf16[32,3200]{1,0:T(8,128)(2,1)S(1)} %collective-permute-done.3.refs_1_, bf16[32,3200]{1,0:T(8,128)(2,1)S(1)} %collective-permute-done.4.refs_2_, ...), custom_call_target="tpu_custom_call" | custom-call | flops 2097152000 | bytes 9830400 | tf_op jit(solution)/shard_map/pallas_call | solution.py:31
  58.3 20.7 %all_to_all.10.parts_ref = bf16[32,56,128]{2,1,0:T(8,128)(2,1)S(1)} all-to-all(bf16[32,56,128]{2,1,0:T(8,128)(2,1)S(1)} %bitcast.3), channel_id=1, replica_groups=mesh['y'=4,'core'=2,'x'=4,'z'=8] {'y','x','core'}, dimensions={0} | all-to-all | bytes 917504 | tf_op jit(solution)/shard_map/all_to_all | solution.py:555
  79.1 14.3 %all_to_all.11 = bf16[32,56,128]{2,1,0:T(8,128)(2,1)S(1)} all-to-all(bf16[32,56,128]{2,1,0:T(8,128)(2,1)S(1)} %shard_map.49), channel_id=1, replica_groups=mesh['y'=4,'core'=2,'x'=4,'z'=8] {'y','x','core'}, dimensions={0} | all-to-all | bytes 917504 | tf_op jit(solution)/shard_map/all_to_all | solution.py:555
  93.5 3.7 %shard_map.50 = (bf16[32,3200]{1,0:T(8,128)(2,1)S(1)}, bf16[32,3200]{1,0:T(8,128)(2,1)S(1)}, bf16[32,3200]{1,0:T(8,128)(2,1)S(1)}, bf16[16,3200]{1,0:T(8,128)(2,1)S(1)}, bf16[16,3200]{1,0:T(8,128)(2,1)S(1)}) custom-call(bf16[1792,128]{1,0:T(8,128)(2,1)S(1)} %bitcast.2, bf16[512,3200]{1,0:T(8,128)(2,1)S(1)} %get-tuple-element.35.ordered_ref), custom_call_target="tpu_custom_call" | custom-call | flops 419430400 | bytes 6553600 | tf_op jit(solution)/shard_map/pallas_call | solution.py:31
  97.2 0.7 collective-permute-start.22
  97.9 2.1 %collective-permute-start.23 = (bf16[32,3200]{1,0:T(8,128)(2,1)S(1)}, bf16[32,3200]{1,0:T(8,128)(2,1)S(1)}, u32[]{:S(2)}, u32[]{:S(2)}) collective-permute-start(bf16[32,3200]{1,0:T(8,128)(2,1)S(1)} %get-tuple-element.38), channel_id=1, source_target_pairs={{0,24},{8,0},{16,8},{24,16},{1,25},{9,1},{17,9},{25,17},{2,26},{10... | collective-permute-start | bytes 614408 | tf_op jit(solution)/shard_map/ppermute | solution.py:44
  100.0 3.0 %collective-permute-start.25 = (bf16[16,3200]{1,0:T(8,128)(2,1)S(1)}, bf16[16,3200]{1,0:T(8,128)(2,1)S(1)}, u32[]{:S(2)}, u32[]{:S(2)}) collective-permute-start(bf16[16,3200]{1,0:T(8,128)(2,1)S(1)} %get-tuple-element.40), channel_id=1, source_target_pairs={{0,16},{8,24},{16,0},{24,8},{1,17},{9,25},{17,1},{25,9},{2,18},{10... | collective-permute-start | bytes 307208 | tf_op jit(solution)/shard_map/ppermute | solution.py:44
  102.9 4.6 %collective-permute-done.24.half0 = bf16[16,3200]{1,0:T(8,128)(2,1)S(1)} collective-permute-done((bf16[16,3200]{1,0:T(8,128)(2,1)S(1)}, bf16[16,3200]{1,0:T(8,128)(2,1)S(1)}, u32[]{:S(2)}, u32[]{:S(2)}) %collective-permute-start.24) | collective-permute-done | bytes 102432 | tf_op jit(solution)/shard_map/ppermute | solution.py:44
  107.5 2.2 %collective-permute-done.25.half1 = bf16[16,3200]{1,0:T(8,128)(2,1)S(1)} collective-permute-done((bf16[16,3200]{1,0:T(8,128)(2,1)S(1)}, bf16[16,3200]{1,0:T(8,128)(2,1)S(1)}, u32[]{:S(2)}, u32[]{:S(2)}) %collective-permute-start.25) | collective-permute-done | bytes 102432 | tf_op jit(solution)/shard_map/ppermute | solution.py:44
  109.7 1.2 %shard_map.51 = f32[32,12544]{1,0:T(8,128)} custom-call(f32[32,12544]{1,0:T(8,128)S(1)} %get-tuple-element.25.eigen_ref, bf16[32,3200]{1,0:T(8,128)(2,1)S(1)} %get-tuple-element.36.mine, bf16[32,3200]{1,0:T(8,128)(2,1)S(1)} %collective-permute-done.22.one, bf16[32,3200]{1,0:T(8,128)(2,1)S(1)} %collective-permute-done.23.two, ...), custom_call_target="tpu_custom_call" | custom-call | flops 401408 | bytes 4014080 | tf_op jit(solution)/shard_map/pallas_call | solution.py:31
  (40 shorter events, 1.3 us)
Async XLA Ops:
  0.0 33.0 %copy-start.2 = (s32[2,8]{1,0:T(2,128)S(1)}, s32[2,8]{1,0:T(2,128)}, u32[]{:S(2)}) copy-start(s32[2,8]{1,0:T(2,128)} %offsets_ref.3) | copy-start | bytes 196
  0.0 33.0 %copy-start.1 = (f32[2,8,4,128]{3,2,1,0:T(4,128)S(1)}, f32[2,8,4,128]{3,2,1,0:T(4,128)}, u32[]{:S(2)}) copy-start(f32[2,8,4,128]{3,2,1,0:T(4,128)} %vectors_ref.3) | copy-start | bytes 98308
  0.0 33.1 %copy-start = (f32[32,12544]{1,0:T(8,128)S(1)}, f32[32,12544]{1,0:T(8,128)}, u32[]{:S(2)}) copy-start(f32[32,12544]{1,0:T(8,128)} %own_ref.1) | copy-start | bytes 4816900
  2.2 12.5 %collective-permute-start.2 = (bf16[16,3200]{1,0:T(8,128)(2,1)}, bf16[16,3200]{1,0:T(8,128)(2,1)S(1)}, u32[]{:S(2)}, u32[]{:S(2)}) collective-permute-start(bf16[16,3200]{1,0:T(8,128)(2,1)} %get-tuple-element.27), channel_id=1, source_target_pairs={{0,8},{8,16},{16,24},{24,0},{1,9},{9,17},{17,25},{25,1},{2,10},{10... | collective-permute-start | bytes 307208 | tf_op jit(solution)/shard_map/ppermute | solution.py:44
  4.3 16.1 %collective-permute-start.10 = (bf16[16,3200]{1,0:T(8,128)(2,1)}, bf16[16,3200]{1,0:T(8,128)(2,1)S(1)}, u32[]{:S(2)}, u32[]{:S(2)}) collective-permute-start(bf16[16,3200]{1,0:T(8,128)(2,1)} %get-tuple-element.28), channel_id=1, source_target_pairs={{0,24},{8,0},{16,8},{24,16},{1,25},{9,1},{17,9},{25,17},{2,26},{10... | collective-permute-start | bytes 307208 | tf_op jit(solution)/shard_map/ppermute | solution.py:44
  5.6 14.8 %collective-permute-start.11 = (bf16[16,3200]{1,0:T(8,128)(2,1)}, bf16[16,3200]{1,0:T(8,128)(2,1)S(1)}, u32[]{:S(2)}, u32[]{:S(2)}) collective-permute-start(bf16[16,3200]{1,0:T(8,128)(2,1)} %get-tuple-element.29), channel_id=1, source_target_pairs={{0,16},{8,24},{16,0},{24,8},{1,17},{9,25},{17,1},{25,9},{2,18},{10... | collective-permute-start | bytes 307208 | tf_op jit(solution)/shard_map/ppermute | solution.py:44
  7.3 15.9 %collective-permute-start.1 = (f32[32,1408]{1,0:T(8,128)}, f32[32,1408]{1,0:T(8,128)S(1)}, u32[]{:S(2)}, u32[]{:S(2)}) collective-permute-start(f32[32,1408]{1,0:T(8,128)} %get-tuple-element.24), channel_id=1, source_target_pairs={{32,0},{64,32},{96,64},{128,96},{160,128},{192,160},{224,192},{33,... | collective-permute-start | bytes 540680 | tf_op jit(solution)/shard_map/ppermute | solution.py:50
  10.7 22.3 %collective-permute-start = (f32[32,2432]{1,0:T(8,128)}, f32[32,2432]{1,0:T(8,128)S(1)}, u32[]{:S(2)}, u32[]{:S(2)}) collective-permute-start(f32[32,2432]{1,0:T(8,128)} %get-tuple-element.23), channel_id=1, source_target_pairs={{0,32},{32,64},{64,96},{96,128},{128,160},{160,192},{192,224},{1,3... | collective-permute-start | bytes 933896 | tf_op jit(solution)/shard_map/ppermute | solution.py:50
  14.7 10.5 %collective-permute-start.4 = (bf16[32,3200]{1,0:T(8,128)(2,1)S(1)}, bf16[32,3200]{1,0:T(8,128)(2,1)S(1)}, u32[]{:S(2)}, u32[]{:S(2)}) collective-permute-start(bf16[32,3200]{1,0:T(8,128)(2,1)S(1)} %constant_dynamic-update-slice_fusion.refs_0_), channel_id=1, source_target_pairs={{0,7},{1,0},{2,1},{3,2},{4,3},{5,4},{6,5},{7,6},{8,15},{9,8},{10,9... | collective-permute-start | bytes 614408 | tf_op jit(solution)/shard_map/ppermute | solution.py:44
  20.4 8.3 %collective-permute-start.3 = (bf16[32,3200]{1,0:T(8,128)(2,1)S(1)}, bf16[32,3200]{1,0:T(8,128)(2,1)S(1)}, u32[]{:S(2)}, u32[]{:S(2)}) collective-permute-start(bf16[32,3200]{1,0:T(8,128)(2,1)S(1)} %constant_dynamic-update-slice_fusion.refs_0_), channel_id=1, source_target_pairs={{0,1},{1,2},{2,3},{3,4},{4,5},{5,6},{6,7},{7,0},{8,9},{9,10},{10,1... | collective-permute-start | bytes 614408 | tf_op jit(solution)/shard_map/ppermute | solution.py:44
  20.4 9.0 %collective-permute-start.13 = (bf16[32,3200]{1,0:T(8,128)(2,1)S(1)}, bf16[32,3200]{1,0:T(8,128)(2,1)S(1)}, u32[]{:S(2)}, u32[]{:S(2)}) collective-permute-start(bf16[32,3200]{1,0:T(8,128)(2,1)S(1)} %constant_dynamic-update-slice_fusion.2.refs_8_), channel_id=1, source_target_pairs={{0,7},{1,0},{2,1},{3,2},{4,3},{5,4},{6,5},{7,6},{8,15},{9,8},{10,9... | collective-permute-start | bytes 614408 | tf_op jit(solution)/shard_map/ppermute | solution.py:44
  23.2 9.8 %collective-permute-start.12 = (bf16[32,3200]{1,0:T(8,128)(2,1)S(1)}, bf16[32,3200]{1,0:T(8,128)(2,1)S(1)}, u32[]{:S(2)}, u32[]{:S(2)}) collective-permute-start(bf16[32,3200]{1,0:T(8,128)(2,1)S(1)} %constant_dynamic-update-slice_fusion.2.refs_8_), channel_id=1, source_target_pairs={{0,1},{1,2},{2,3},{3,4},{4,5},{5,6},{6,7},{7,0},{8,9},{9,10},{10,1... | collective-permute-start | bytes 614408 | tf_op jit(solution)/shard_map/ppermute | solution.py:44
  25.3 11.1 %collective-permute-start.6 = (bf16[32,3200]{1,0:T(8,128)(2,1)S(1)}, bf16[32,3200]{1,0:T(8,128)(2,1)S(1)}, u32[]{:S(2)}, u32[]{:S(2)}) collective-permute-start(bf16[32,3200]{1,0:T(8,128)(2,1)S(1)} %collective-permute-done.4.refs_2_), channel_id=1, source_target_pairs={{0,7},{1,0},{2,1},{3,2},{4,3},{5,4},{6,5},{7,6},{8,15},{9,8},{10,9... | collective-permute-start | bytes 614408 | tf_op jit(solution)/shard_map/ppermute | solution.py:44
  28.7 10.1 %collective-permute-start.5 = (bf16[32,3200]{1,0:T(8,128)(2,1)S(1)}, bf16[32,3200]{1,0:T(8,128)(2,1)S(1)}, u32[]{:S(2)}, u32[]{:S(2)}) collective-permute-start(bf16[32,3200]{1,0:T(8,128)(2,1)S(1)} %collective-permute-done.3.refs_1_), channel_id=1, source_target_pairs={{0,1},{1,2},{2,3},{3,4},{4,5},{5,6},{6,7},{7,0},{8,9},{9,10},{10,1... | collective-permute-start | bytes 614408 | tf_op jit(solution)/shard_map/ppermute | solution.py:44
  29.5 9.3 %collective-permute-start.15 = (bf16[32,3200]{1,0:T(8,128)(2,1)S(1)}, bf16[32,3200]{1,0:T(8,128)(2,1)S(1)}, u32[]{:S(2)}, u32[]{:S(2)}) collective-permute-start(bf16[32,3200]{1,0:T(8,128)(2,1)S(1)} %collective-permute-done.13.refs_10_), channel_id=1, source_target_pairs={{0,7},{1,0},{2,1},{3,2},{4,3},{5,4},{6,5},{7,6},{8,15},{9,8},{10,9... | collective-permute-start | bytes 614408 | tf_op jit(solution)/shard_map/ppermute | solution.py:44
  33.0 8.5 %collective-permute-start.14 = (bf16[32,3200]{1,0:T(8,128)(2,1)S(1)}, bf16[32,3200]{1,0:T(8,128)(2,1)S(1)}, u32[]{:S(2)}, u32[]{:S(2)}) collective-permute-start(bf16[32,3200]{1,0:T(8,128)(2,1)S(1)} %collective-permute-done.12.refs_9_), channel_id=1, source_target_pairs={{0,1},{1,2},{2,3},{3,4},{4,5},{5,6},{6,7},{7,0},{8,9},{9,10},{10,1... | collective-permute-start | bytes 614408 | tf_op jit(solution)/shard_map/ppermute | solution.py:44
  36.0 7.6 %collective-permute-start.19 = (bf16[32,3200]{1,0:T(8,128)(2,1)S(1)}, bf16[32,3200]{1,0:T(8,128)(2,1)S(1)}, u32[]{:S(2)}, u32[]{:S(2)}) collective-permute-start(bf16[32,3200]{1,0:T(8,128)(2,1)S(1)} %get-tuple-element.31), channel_id=1, source_target_pairs={{0,8},{8,16},{16,24},{24,0},{1,9},{9,17},{17,25},{25,1},{2,10},{10... | collective-permute-start | bytes 614408 | tf_op jit(solution)/shard_map/ppermute | solution.py:44
  36.4 9.6 %collective-permute-start.20 = (bf16[32,3200]{1,0:T(8,128)(2,1)S(1)}, bf16[32,3200]{1,0:T(8,128)(2,1)S(1)}, u32[]{:S(2)}, u32[]{:S(2)}) collective-permute-start(bf16[32,3200]{1,0:T(8,128)(2,1)S(1)} %get-tuple-element.32), channel_id=1, source_target_pairs={{0,24},{8,0},{16,8},{24,16},{1,25},{9,1},{17,9},{25,17},{2,26},{10... | collective-permute-start | bytes 614408 | tf_op jit(solution)/shard_map/ppermute | solution.py:44
  38.8 7.2 %collective-permute-start.7 = (bf16[32,3200]{1,0:T(8,128)(2,1)S(1)}, bf16[32,3200]{1,0:T(8,128)(2,1)S(1)}, u32[]{:S(2)}, u32[]{:S(2)}) collective-permute-start(bf16[32,3200]{1,0:T(8,128)(2,1)S(1)} %collective-permute-done.5.refs_3_), channel_id=1, source_target_pairs={{0,1},{1,2},{2,3},{3,4},{4,5},{5,6},{6,7},{7,0},{8,9},{9,10},{10,1... | collective-permute-start | bytes 614408 | tf_op jit(solution)/shard_map/ppermute | solution.py:44
  38.8 7.3 %collective-permute-start.17 = (bf16[32,3200]{1,0:T(8,128)(2,1)S(1)}, bf16[32,3200]{1,0:T(8,128)(2,1)S(1)}, u32[]{:S(2)}, u32[]{:S(2)}) collective-permute-start(bf16[32,3200]{1,0:T(8,128)(2,1)S(1)} %collective-permute-done.15.refs_12_), channel_id=1, source_target_pairs={{0,7},{1,0},{2,1},{3,2},{4,3},{5,4},{6,5},{7,6},{8,15},{9,8},{10,9... | collective-permute-start | bytes 614408 | tf_op jit(solution)/shard_map/ppermute | solution.py:44
  41.5 7.2 %collective-permute-start.21 = (bf16[32,3200]{1,0:T(8,128)(2,1)S(1)}, bf16[32,3200]{1,0:T(8,128)(2,1)S(1)}, u32[]{:S(2)}, u32[]{:S(2)}) collective-permute-start(bf16[32,3200]{1,0:T(8,128)(2,1)S(1)} %get-tuple-element.33), channel_id=1, source_target_pairs={{0,16},{8,24},{16,0},{24,8},{1,17},{9,25},{17,1},{25,9},{2,18},{10... | collective-permute-start | bytes 614408 | tf_op jit(solution)/shard_map/ppermute | solution.py:44
  43.6 5.4 %collective-permute-start.8 = (bf16[32,3200]{1,0:T(8,128)(2,1)S(1)}, bf16[32,3200]{1,0:T(8,128)(2,1)S(1)}, u32[]{:S(2)}, u32[]{:S(2)}) collective-permute-start(bf16[32,3200]{1,0:T(8,128)(2,1)S(1)} %collective-permute-done.6.refs_4_), channel_id=1, source_target_pairs={{0,7},{1,0},{2,1},{3,2},{4,3},{5,4},{6,5},{7,6},{8,15},{9,8},{10,9... | collective-permute-start | bytes 614408 | tf_op jit(solution)/shard_map/ppermute | solution.py:44
  46.0 5.8 %collective-permute-start.16 = (bf16[32,3200]{1,0:T(8,128)(2,1)S(1)}, bf16[32,3200]{1,0:T(8,128)(2,1)S(1)}, u32[]{:S(2)}, u32[]{:S(2)}) collective-permute-start(bf16[32,3200]{1,0:T(8,128)(2,1)S(1)} %collective-permute-done.14.refs_11_), channel_id=1, source_target_pairs={{0,1},{1,2},{2,3},{3,4},{4,5},{5,6},{6,7},{7,0},{8,9},{9,10},{10,1... | collective-permute-start | bytes 614408 | tf_op jit(solution)/shard_map/ppermute | solution.py:44
  46.0 9.7 %collective-permute-start.9 = (bf16[32,3200]{1,0:T(8,128)(2,1)S(1)}, bf16[32,3200]{1,0:T(8,128)(2,1)S(1)}, u32[]{:S(2)}, u32[]{:S(2)}) collective-permute-start(bf16[32,3200]{1,0:T(8,128)(2,1)S(1)} %collective-permute-done.7.refs_5_), channel_id=1, source_target_pairs={{0,1},{1,2},{2,3},{3,4},{4,5},{5,6},{6,7},{7,0},{8,9},{9,10},{10,1... | collective-permute-start | bytes 614408 | tf_op jit(solution)/shard_map/ppermute | solution.py:44
  46.1 9.6 %collective-permute-start.18 = (bf16[32,3200]{1,0:T(8,128)(2,1)S(1)}, bf16[32,3200]{1,0:T(8,128)(2,1)S(1)}, u32[]{:S(2)}, u32[]{:S(2)}) collective-permute-start(bf16[32,3200]{1,0:T(8,128)(2,1)S(1)} %collective-permute-done.17.refs_14_), channel_id=1, source_target_pairs={{0,7},{1,0},{2,1},{3,2},{4,3},{5,4},{6,5},{7,6},{8,15},{9,8},{10,9... | collective-permute-start | bytes 614408 | tf_op jit(solution)/shard_map/ppermute | solution.py:44
  97.2 12.5 %collective-permute-start.22 = (bf16[32,3200]{1,0:T(8,128)(2,1)S(1)}, bf16[32,3200]{1,0:T(8,128)(2,1)S(1)}, u32[]{:S(2)}, u32[]{:S(2)}) collective-permute-start(bf16[32,3200]{1,0:T(8,128)(2,1)S(1)} %get-tuple-element.37), channel_id=1, source_target_pairs={{0,8},{8,16},{16,24},{24,0},{1,9},{9,17},{17,25},{25,1},{2,10},{10... | collective-permute-start | bytes 614408 | tf_op jit(solution)/shard_map/ppermute | solution.py:44
  97.9 11.8 %collective-permute-start.23 = (bf16[32,3200]{1,0:T(8,128)(2,1)S(1)}, bf16[32,3200]{1,0:T(8,128)(2,1)S(1)}, u32[]{:S(2)}, u32[]{:S(2)}) collective-permute-start(bf16[32,3200]{1,0:T(8,128)(2,1)S(1)} %get-tuple-element.38), channel_id=1, source_target_pairs={{0,24},{8,0},{16,8},{24,16},{1,25},{9,1},{17,9},{25,17},{2,26},{10... | collective-permute-start | bytes 614408 | tf_op jit(solution)/shard_map/ppermute | solution.py:44
  100.0 7.6 %collective-permute-start.24 = (bf16[16,3200]{1,0:T(8,128)(2,1)S(1)}, bf16[16,3200]{1,0:T(8,128)(2,1)S(1)}, u32[]{:S(2)}, u32[]{:S(2)}) collective-permute-start(bf16[16,3200]{1,0:T(8,128)(2,1)S(1)} %get-tuple-element.39), channel_id=1, source_target_pairs={{0,16},{8,24},{16,0},{24,8},{1,17},{9,25},{17,1},{25,9},{2,18},{10... | collective-permute-start | bytes 307208 | tf_op jit(solution)/shard_map/ppermute | solution.py:44
  100.0 9.8 %collective-permute-start.25 = (bf16[16,3200]{1,0:T(8,128)(2,1)S(1)}, bf16[16,3200]{1,0:T(8,128)(2,1)S(1)}, u32[]{:S(2)}, u32[]{:S(2)}) collective-permute-start(bf16[16,3200]{1,0:T(8,128)(2,1)S(1)} %get-tuple-element.40), channel_id=1, source_target_pairs={{0,16},{8,24},{16,0},{24,8},{1,17},{9,25},{17,1},{25,9},{2,18},{10... | collective-permute-start | bytes 307208 | tf_op jit(solution)/shard_map/ppermute | solution.py:44
